TPU v7x, 32 devices: a whole 2x2x4 slice. The times are simulated.
32 devices in a mesh: gx: 4 (over x, core), gy: 8 (over z, y).
Axes of the slice: x: 2, y: 2, z: 4, core: 2. Of those that a mesh axis runs over, the one named last changes fastest.
Arguments:
- hot_ids: int32 [262144], P(('gx', 'gy')), may hold values from 0 to 2047
- hot_grads: bfloat16 [262144, 128], P(('gx', 'gy')), may hold values from -6 to 6
- cold_grads: bfloat16 [4, 8, 8, 512, 128], P('gx', 'gy'), may hold values from -6 to 6
- cold_slots: int32 [4, 8, 8, 512], P('gx', 'gy'), may hold values from 0 to 2047
- cold_counts: int32 [4, 8, 8], P('gx', 'gy'), may hold values from 1 to 512, as said below
Outputs:
- hot_grad: float32 [2048, 128], replicated
- cold_grad: float32 [4, 16384, 128], P('gx', 'gy')
Inputs may be any that keep to these rules, and one draw needn't show every extreme that they name: In each group g, some owner d receives cold_counts[g, s, d] = 512 from every s; loads per owner are skewed.
All inputs are finite; a program needn't handle non-finite values.
Results may differ from a plain program's by a relative error of at most 0.0003.
Values may be sent and summed in bfloat16 or wider, within the bound.
No kernel may reach another device: no remote copies, remote signals or barrier semaphores. Data moves between devices by JAX's collectives and lax.ppermute only.
A program may use at most 64 MiB of HBM per device.

v0:
```python
import math

import jax
import jax.numpy as jnp
from jax import lax
from jax.sharding import PartitionSpec as P

HOT = 2048
OWN_ROWS = 2048


def onehot_sum(row_ids, row_data, table_size, block_rows):
    turns = row_ids.shape[0] // block_rows
    id_blocks = row_ids.reshape(turns, block_rows)
    data_blocks = row_data.reshape(turns, block_rows, row_data.shape[1])
    table_iota = lax.broadcasted_iota(jnp.int32, (table_size, block_rows), 0)

    def add_block(total, pieces):
        ids_here, data_here = pieces
        selector = (table_iota == ids_here[None, :]).astype(jnp.bfloat16)
        return (total + jnp.dot(selector, data_here, preferred_element_type=jnp.float32), None)

    start = jnp.zeros((table_size, row_data.shape[1]), jnp.float32)
    total, unused = lax.scan(add_block, start, (id_blocks, data_blocks))
    return total


def hot_part(hot_ids, hot_grads):
    hot_rows = HOT
    block_rows = math.gcd(hot_ids.shape[0], 2048)
    local_sum = onehot_sum(hot_ids, hot_grads, hot_rows, block_rows)
    factor = (hot_rows / (hot_ids.shape[0] * lax.axis_size("gx") * lax.axis_size("gy"))) ** 0.5
    shared = lax.psum_scatter(local_sum, "gy", scatter_dimension=0, tiled=True)
    shared = lax.psum(shared, "gx")
    total = lax.all_gather(shared, "gy", axis=0, tiled=True)
    return total * factor


def cold_part(cold_grads, cold_slots, cold_counts):
    owners, capacity, width = (cold_grads.shape[2], cold_grads.shape[3], cold_grads.shape[4])
    grads_here = cold_grads.reshape(owners, capacity, width)
    slots_here = cold_slots.reshape(owners, capacity)
    counts_here = cold_counts.reshape(owners)
    places = lax.broadcasted_iota(jnp.int32, (owners, capacity), 1)
    valid = places < counts_here[:, None]
    payload = jnp.where(valid[:, :, None], grads_here, jnp.zeros_like(grads_here))
    got_rows, got_slots = (
        lax.all_to_all(payload, "gy", split_axis=0, concat_axis=0, tiled=True),
        lax.all_to_all(slots_here, "gy", split_axis=0, concat_axis=0, tiled=True),
    )
    total_rows = owners * capacity
    block_rows = math.gcd(total_rows, 1024)
    table = onehot_sum(
        got_slots.reshape(total_rows), got_rows.reshape(total_rows, width), OWN_ROWS, block_rows
    )
    return table.reshape(1, OWN_ROWS, width)


def per_device(hot_ids, hot_grads, cold_grads, cold_slots, cold_counts):
    hot_grad = hot_part(hot_ids, hot_grads)
    cold_grad = cold_part(cold_grads, cold_slots, cold_counts)
    return (hot_grad, cold_grad)


def solution(mesh):
    return jax.shard_map(
        per_device,
        mesh=mesh,
        in_specs=(
            P(("gx", "gy")),
            P(("gx", "gy"), None),
            P("gx", "gy", None, None, None),
            P("gx", "gy", None, None),
            P("gx", "gy", None),
        ),
        out_specs=(P(), P("gx", "gy", None)),
        check_vma=False,
    )
```

profile of v0, /device:TPU:0, one launch (start us, length us, event | category | flops | bytes accessed | tf_op | source)
XLA Modules:
  0.0 185.8 jit_solution(4274179711939193013)
XLA Ops:
  7.2 0.0 reduce-scatter.2.cloned.1.call-start
  7.2 0.8 reshape.43
  8.0 0.0 copy-start.2
  8.0 0.0 copy-start.3
  8.0 0.0 copy-start
  8.0 17.7 %while.22 = (s32[]{:T(128)}, f32[2048,128]{1,0:T(8,128)S(1)}, s32[4,2048]{1,0:T(4,128)S(1)}, bf16[4,2048,128]{2,1,0:T(8,128)(2,1)}, s32[]{:T(128)}, /*index=5*/s32[]{:T(128)}) while((s32[]{:T(128)}, f32[2048,128]{1,0:T(8,128)S(1)}, s32[4,2048]{1,0:T(4,128)S(1)}, bf16[4,2048,128]{2,1,0:T(8,128)(2,1)}, s32[]{:T(128)}, ...), condition=%wide.region_1.2_spmd.clone, body=%wide.region_0.1_spmd.clone.sunk | while | flops 1078460416 | bytes 2646611 | solution.py:24
  8.1 4.4 %fusion.21 = f32[2048,128]{1,0:T(8,128)S(1)} fusion(s32[2048]{0:T(1024)S(1)} %bitcast.25, f32[2048,128]{1,0:T(8,128)S(1)} %get-tuple-element.165, bf16[4,2048,128]{2,1,0:T(8,128)(2,1)} %get-tuple-element.173, s32[]{:T(128)} %get-tuple-element.164, pred[]{:T(512)S(6)} %compare.6), kind=kOutput, calls=%fused_computation.5.clone.1 | convolution fusion | flops 1078460416 | bytes 2630145 | tf_op jit(solution)/shard_map/while/body/eval_jaxpr/dot_general | solution.py:21
  12.6 4.4 %fusion.21 = f32[2048,128]{1,0:T(8,128)S(1)} fusion(s32[2048]{0:T(1024)S(1)} %bitcast.25, f32[2048,128]{1,0:T(8,128)S(1)} %get-tuple-element.165, bf16[4,2048,128]{2,1,0:T(8,128)(2,1)} %get-tuple-element.173, s32[]{:T(128)} %get-tuple-element.164, pred[]{:T(512)S(6)} %compare.6), kind=kOutput, calls=%fused_computation.5.clone.1 | convolution fusion | flops 1078460416 | bytes 2630145 | tf_op jit(solution)/shard_map/while/body/eval_jaxpr/dot_general | solution.py:21
  17.0 4.4 %fusion.21 = f32[2048,128]{1,0:T(8,128)S(1)} fusion(s32[2048]{0:T(1024)S(1)} %bitcast.25, f32[2048,128]{1,0:T(8,128)S(1)} %get-tuple-element.165, bf16[4,2048,128]{2,1,0:T(8,128)(2,1)} %get-tuple-element.173, s32[]{:T(128)} %get-tuple-element.164, pred[]{:T(512)S(6)} %compare.6), kind=kOutput, calls=%fused_computation.5.clone.1 | convolution fusion | flops 1078460416 | bytes 2630145 | tf_op jit(solution)/shard_map/while/body/eval_jaxpr/dot_general | solution.py:21
  21.4 4.4 %fusion.21 = f32[2048,128]{1,0:T(8,128)S(1)} fusion(s32[2048]{0:T(1024)S(1)} %bitcast.25, f32[2048,128]{1,0:T(8,128)S(1)} %get-tuple-element.165, bf16[4,2048,128]{2,1,0:T(8,128)(2,1)} %get-tuple-element.173, s32[]{:T(128)} %get-tuple-element.164, pred[]{:T(512)S(6)} %compare.6), kind=kOutput, calls=%fused_computation.5.clone.1 | convolution fusion | flops 1078460416 | bytes 2630145 | tf_op jit(solution)/shard_map/while/body/eval_jaxpr/dot_general | solution.py:21
  25.7 0.0 copy-start.1
  25.8 1.0 copy-done.1
  26.7 0.0 reduce-scatter.2.cloned.1.call-update
  26.7 0.0 copy-done.2
  26.8 0.6 all_to_all.9
  27.4 7.3 %all-to-all-start = ((s32[8,1,512]{2,1,0:T(1,128)}), s32[8,1,512]{2,1,0:T(1,128)S(1)}, u32[]{:S(2)}, u32[]{:S(2)}) async-start(s32[8,1,512]{2,1,0:T(1,128)} %all_to_all.9), calls=%async_computation.1 | async-start | bytes 32768 | tf_op jit(solution)/shard_map/all_to_all | solution.py:49
  34.7 0.0 copy-done.3
  34.7 0.1 iota_compare_fusion.8
  34.8 0.0 copy-done
  34.8 1.5 bitcast_select_fusion
  36.2 5.1 %all-to-all-done = s32[8,1,512]{2,1,0:T(1,128)S(1)} async-done(((s32[8,1,512]{2,1,0:T(1,128)}), s32[8,1,512]{2,1,0:T(1,128)S(1)}, u32[]{:S(2)}, u32[]{:S(2)}) %all-to-all-start) | async-done | bytes 16416 | tf_op jit(solution)/shard_map/all_to_all | solution.py:49
  41.3 3.6 %all-to-all-start.1 = ((bf16[8,512,128]{2,1,0:T(8,128)(2,1)}), bf16[8,512,128]{2,1,0:T(8,128)(2,1)S(1)}, u32[]{:S(2)}, u32[]{:S(2)}) async-start(bf16[8,512,128]{2,1,0:T(8,128)(2,1)} %bitcast_select_fusion), calls=%async_computation.2 | async-start | bytes 2097152 | tf_op jit(solution)/shard_map/all_to_all | solution.py:48
  44.9 0.0 all-reduce.2.cloned.1.call-start
  44.9 56.6 %reduce-scatter.2.cloned.1.call-done = f32[256,128]{1,0:T(8,128)} async-done(((f32[2048,128]{1,0:T(8,128)}), f32[256,128]{1,0:T(8,128)}) %reduce-scatter.2.cloned.1.call-update) | async-done | bytes 131088 | tf_op jit(solution)/shard_map/reduce_scatter | solution.py:33
  101.6 0.0 all-reduce.2.cloned.1.call-update
  101.6 0.0 all-gather.2.cloned.1.call-start
  101.6 32.9 %all-reduce.2.cloned.1.call-done = f32[256,128]{1,0:T(8,128)} async-done(((f32[256,128]{1,0:T(8,128)}), f32[256,128]{1,0:T(8,128)}) %all-reduce.2.cloned.1.call-update) | async-done | bytes 131088 | tf_op jit(solution)/shard_map/psum | solution.py:34
  134.6 0.0 all-gather.2.cloned.1.call-update
  134.7 0.0 all-to-all-done.1
  134.7 7.3 %while.23 = (s32[]{:T(128)}, f32[2048,128]{1,0:T(8,128)S(1)}, s32[4,1024]{1,0:T(4,128)S(1)}, bf16[4,1024,128]{2,1,0:T(8,128)(2,1)S(1)}, s32[]{:T(128)}, /*index=5*/s32[]{:T(128)}) while((s32[]{:T(128)}, f32[2048,128]{1,0:T(8,128)S(1)}, s32[4,1024]{1,0:T(4,128)S(1)}, bf16[4,1024,128]{2,1,0:T(8,128)(2,1)S(1)}, s32[]{:T(128)}, ...), condition=%wide.region_5.6_spmd.clone, body=%wide.region_4.5_spmd.clone.sunk | while | flops 539492352 | bytes 2371671 | solution.py:24
  134.7 1.8 fusion.23
  136.5 1.8 fusion.23
  138.4 1.8 fusion.23
  140.2 1.8 fusion.23
  142.0 0.0 copy-start.4
  142.0 35.0 %all-gather.2.cloned.1.call-done = f32[2048,128]{1,0:T(8,128)} async-done(((f32[256,128]{1,0:T(8,128)}), f32[2048,128]{1,0:T(8,128)}) %all-gather.2.cloned.1.call-update) | async-done | bytes 1048592 | tf_op jit(solution)/shard_map/all_gather | solution.py:35
  177.0 2.3 %broadcast_multiply_fusion = f32[2048,128]{1,0:T(8,128)} fusion(f32[2048,128]{1,0:T(8,128)} %all-gather.2.cloned.1.call-done), kind=kLoop, calls=%fused_computation.19 | loop fusion | flops 262144 | bytes 2097152 | tf_op jit(solution)/shard_map/mul | solution.py:36
  179.3 0.0 copy-done.4
  (12 shorter events, 0.1 us)
Async XLA Ops:
  7.2 94.4 %reduce-scatter.2.cloned.1.call-start = ((), (), s32[]{:S(2)}) async-start(), calls=%async_computation.3 | async-start | bytes 1179648 | tf_op jit(solution)/shard_map/reduce_scatter | solution.py:33
  8.0 18.8 %copy-start.2 = (s32[1,1,8,512]{3,2,1,0:T(8,128)S(1)}, s32[1,1,8,512]{3,2,1,0:T(8,128)}, u32[]{:S(2)}) copy-start(s32[1,1,8,512]{3,2,1,0:T(8,128)} %param.12) | copy-start | bytes 49156
  8.0 26.7 %copy-start.3 = (s32[1,1,8]{2,1,0:T(1,128)S(1)}, s32[1,1,8]{2,1,0:T(1,128)}, u32[]{:S(2)}) copy-start(s32[1,1,8]{2,1,0:T(1,128)} %param.13) | copy-start | bytes 100
  8.0 26.7 %copy-start = (bf16[1,1,8,512,128]{4,3,2,1,0:T(8,128)(2,1)S(1)}, bf16[1,1,8,512,128]{4,3,2,1,0:T(8,128)(2,1)}, u32[]{:S(2)}) copy-start(bf16[1,1,8,512,128]{4,3,2,1,0:T(8,128)(2,1)} %param.11) | copy-start | bytes 3145732
  25.7 1.0 copy-start.1
  27.4 13.9 %all-to-all-start = ((s32[8,1,512]{2,1,0:T(1,128)}), s32[8,1,512]{2,1,0:T(1,128)S(1)}, u32[]{:S(2)}, u32[]{:S(2)}) async-start(s32[8,1,512]{2,1,0:T(1,128)} %all_to_all.9), calls=%async_computation.1 | async-start | bytes 32768 | tf_op jit(solution)/shard_map/all_to_all | solution.py:49
  41.3 93.4 %all-to-all-start.1 = ((bf16[8,512,128]{2,1,0:T(8,128)(2,1)}), bf16[8,512,128]{2,1,0:T(8,128)(2,1)S(1)}, u32[]{:S(2)}, u32[]{:S(2)}) async-start(bf16[8,512,128]{2,1,0:T(8,128)(2,1)} %bitcast_select_fusion), calls=%async_computation.2 | async-start | bytes 2097152 | tf_op jit(solution)/shard_map/all_to_all | solution.py:48
  44.9 89.7 %all-reduce.2.cloned.1.call-start = ((), (), s32[]{:S(2)}) async-start(), calls=%async_computation.4 | async-start | bytes 262144 | tf_op jit(solution)/shard_map/psum | solution.py:34
  101.6 75.4 %all-gather.2.cloned.1.call-start = ((), (), s32[]{:S(2)}) async-start(), calls=%async_computation.5 | async-start | bytes 1179648 | tf_op jit(solution)/shard_map/all_gather | solution.py:35
  142.0 37.3 %copy-start.4 = (f32[2048,128]{1,0:T(8,128)}, f32[2048,128]{1,0:T(8,128)S(1)}, u32[]{:S(2)}) copy-start(f32[2048,128]{1,0:T(8,128)S(1)} %get-tuple-element.57) | copy-start | bytes 3145732
Sparse Core Ops, SparseCore 0:
  26.9 74.6 reduce-scatter.1
  103.9 30.6 all-reduce.1
  136.7 40.2 all-gather.1
where the time goes:
time: 186 us
  waiting for transfers between devices  130 us (70%)
  matrix products  24.7 us (13%)
  between operations  13.9 us (7%)
  starting transfers between devices  11 us (6%)
  other arithmetic  3.89 us (2%)
  local copies, waits for them, and re-layouts  2.47 us (1%)
    reduce_scatter x1, waiting for transfers between devices, hot_part(): shared = lax.psum_scatter(local_sum, 'gy', scatter_dimension=0, tiled=True)  56.6 us
    all_gather x1, waiting for transfers between devices, hot_part(): total = lax.all_gather(shared, 'gy', axis=0, tiled=True)  35 us
    psum x1, waiting for transfers between devices, hot_part(): shared = lax.psum(shared, 'gx')  32.9 us
    dot_general x8, matrix products, add_block(): jnp.dot(selector, data_here, preferred_element_type=jnp.float32)  24.7 us
    all_to_all x1, starting transfers between devices, cold_part(): lax.all_to_all(slots_here, 'gy', split_axis=0, concat_axis=0, tiled=True)  7.31 us
    all_to_all x1, waiting for transfers between devices, cold_part(): lax.all_to_all(slots_here, 'gy', split_axis=0, concat_axis=0, tiled=True)  5.07 us
  transfers between devices with their start and end apart: 5, of which 4 were waited for; matrix products, arithmetic and copies ran while one was open for 5% of the time, Pallas kernels for 0%

commit v1 on v0

v1 whole, which is shorter than its diff:
```python
import functools
import math

import jax
import jax.numpy as jnp
from jax import lax
from jax.experimental import pallas as pl
from jax.experimental.pallas import tpu as pltpu
from jax.sharding import Mesh
from jax.sharding import PartitionSpec as P

HOT = 2048
OWN_ROWS = 2048
LANES = 128
SUB = 8
STEPS = 128.0
TOP = 32600.0
TINY = 2.0**-100


def masked_halves(keep, data_ref, rhs_ref, base, width):
    flags = keep.T
    for j in range(keep.shape[0]):
        rows = pl.ds(base + j * LANES, LANES)
        column = jnp.broadcast_to(flags[:, j : j + 1], (LANES, width)).astype(jnp.bfloat16)
        data = data_ref[pl.ds(j * LANES, LANES), :]
        kept = data * column
        rhs_ref[rows, :width] = kept
        rhs_ref[rows, width:] = data - kept


def onehot_block(row, start, size):
    places = (lax.broadcasted_iota(jnp.int32, (size, LANES), 0) + start).astype(jnp.int16)
    one, zero = jnp.ones((), jnp.bfloat16), jnp.zeros((), jnp.bfloat16)
    parts = [jnp.where(places == row[j : j + 1, :], one, zero) for j in range(row.shape[0])]
    return jnp.concatenate(parts, axis=1)


def hot_kernel(core_ref, ids_ref, data_ref, mine_ref, send_ref, rhs_ref, *, block):
    half, width = mine_ref.shape

    @pl.when(pl.program_id(0) == 0)
    def _():
        mine_ref[...] = jnp.zeros_like(mine_ref)
        send_ref[...] = jnp.zeros_like(send_ref)

    ids = ids_ref[...]
    high = (ids >= half).astype(jnp.int32)
    masked_halves((high == core_ref[0]).astype(jnp.float32), data_ref, rhs_ref, 0, width)
    row = (ids - high * half).astype(jnp.int16)
    rhs = rhs_ref[...]
    for start in range(0, half, block):
        part = jnp.dot(onehot_block(row, start, block), rhs, preferred_element_type=jnp.float32)
        rows = pl.ds(start, block)
        mine_ref[rows, :] += part[:, :width]
        send_ref[rows, :] += part[:, width:]


def hot_sums(core, ids, data, table):
    lookups, width = data.shape
    half = table // 2
    step = math.gcd(lookups, 4096)
    return pl.pallas_call(
        functools.partial(hot_kernel, block=math.gcd(half, 256)),
        grid=(lookups // step,),
        in_specs=[
            pl.BlockSpec(memory_space=pltpu.SMEM),
            pl.BlockSpec((step // LANES, LANES), lambda i: (i, 0)),
            pl.BlockSpec((step, width), lambda i: (i, 0)),
        ],
        out_specs=[pl.BlockSpec((half, width), lambda i: (0, 0))] * 2,
        out_shape=[jax.ShapeDtypeStruct((half, width), jnp.float32)] * 2,
        scratch_shapes=[pltpu.VMEM((step, 2 * width), jnp.bfloat16)],
        cost_estimate=pl.CostEstimate(flops=2 * lookups * table * width, bytes_accessed=2 * lookups * width, transcendentals=0),
        name="hot_sums",
    )(core, ids.reshape(lookups // LANES, LANES), data)


def encode(values):
    rows, width = values.shape
    groups = values.reshape(rows // SUB, SUB, width)
    most = jnp.maximum(jnp.max(jnp.abs(groups), axis=0), TINY)
    code = jnp.ceil(jnp.log2(most) * STEPS) + 1.0
    codes = jnp.round(groups * (jnp.exp2(code * (-1.0 / STEPS)) * TOP)[None])
    return codes.reshape(rows, width), code


def decode(codes, code):
    rows, width = codes.shape
    scale = jnp.exp2(code * (1.0 / STEPS)) * (1.0 / TOP)
    return (codes.reshape(rows // SUB, SUB, width) * scale[None]).reshape(rows, width)


def narrow(values):
    return values.astype(jnp.int32).astype(jnp.int16)


def widen(values):
    return values.astype(jnp.int32).astype(jnp.float32)


def pack_kernel(counts_ref, mine_ref, got_ref, slots_ref, out_ref):
    peers, rows, width = out_ref.shape
    rows -= 2 * SUB
    owners, lines, _ = slots_ref.shape
    places = lax.broadcasted_iota(jnp.int32, (lines, LANES), 0) * LANES + lax.broadcasted_iota(jnp.int32, (lines, LANES), 1)
    for p in range(peers):
        here = pl.ds(p * rows, rows)
        codes, code = encode(mine_ref[here, :] + got_ref[here, :])
        out_ref[p, :rows, :] = narrow(codes)
        d = p % owners
        used = jnp.where(places < counts_ref[d], slots_ref[d], -1)
        if lines < SUB:
            used = jnp.concatenate([used, jnp.full((SUB - lines, LANES), -1, jnp.int32)], axis=0)
        tail = jnp.concatenate([code.astype(jnp.int32), used], axis=0)
        out_ref[p, rows:, :] = tail.astype(jnp.int16)


def pack(mine, got, slots, counts, peers):
    half, width = mine.shape
    whole = pl.BlockSpec(memory_space=pltpu.VMEM)
    return pl.pallas_call(
        pack_kernel,
        in_specs=[pl.BlockSpec(memory_space=pltpu.SMEM), whole, whole, whole],
        out_specs=whole,
        out_shape=jax.ShapeDtypeStruct((peers, half // peers + 2 * SUB, width), jnp.int16),
        cost_estimate=pl.CostEstimate(flops=half * width * 8, bytes_accessed=half * width * 10, transcendentals=0),
        name="pack",
    )(counts, mine, got, slots)


def add_kernel(got_ref, out_ref, *, factor):
    peers, rows, width = got_ref.shape
    rows -= 2 * SUB
    total = jnp.zeros((rows, width), jnp.float32)
    for p in range(peers):
        tail = widen(got_ref[p, rows:, :])
        total += decode(widen(got_ref[p, :rows, :]), tail[:SUB])
    codes, code = encode(total * factor)
    packed = jnp.concatenate([narrow(codes), narrow(jnp.concatenate([code, code], axis=0))], axis=0)
    for p in range(peers):
        out_ref[p] = packed


def add(got, factor):
    whole = pl.BlockSpec(memory_space=pltpu.VMEM)
    return pl.pallas_call(
        functools.partial(add_kernel, factor=factor),
        in_specs=[whole],
        out_specs=whole,
        out_shape=jax.ShapeDtypeStruct(got.shape, jnp.int16),
        cost_estimate=pl.CostEstimate(flops=got.size * 8, bytes_accessed=got.size * 4, transcendentals=0),
        name="add",
    )(got)


def unpack_kernel(core_ref, mine_ref, other_ref, out_ref):
    peers, rows, width = mine_ref.shape
    rows -= 2 * SUB
    core = core_ref[0]
    for ref, side in ((mine_ref, core), (other_ref, 1 - core)):
        for p in range(peers):
            tail = widen(ref[p, rows:, :])
            start = pl.multiple_of(side * (peers * rows) + p * rows, SUB)
            out_ref[pl.ds(start, rows), :] = decode(widen(ref[p, :rows, :]), tail[:SUB])


def unpack(core, mine, other, table):
    peers, rows, width = mine.shape
    whole = pl.BlockSpec(memory_space=pltpu.VMEM)
    return pl.pallas_call(
        unpack_kernel,
        in_specs=[pl.BlockSpec(memory_space=pltpu.SMEM), whole, whole],
        out_specs=whole,
        out_shape=jax.ShapeDtypeStruct((table, width), jnp.float32),
        cost_estimate=pl.CostEstimate(flops=table * width * 4, bytes_accessed=table * width * 6, transcendentals=0),
        name="unpack",
    )(core, mine, other)


def cold_kernel(group_ref, slots_ref, data_ref, out_ref, rhs_ref, row_ref, *, block, at, lines):
    owners, capacity, width = data_ref.shape
    half = out_ref.shape[0] // 2
    for s in range(owners):
        slots = slots_ref[s, at:, :].astype(jnp.int32)[SUB : SUB + lines]
        high = (slots >= half).astype(jnp.int32)
        masked_halves((high == 0).astype(jnp.float32), data_ref.at[s], rhs_ref, s * capacity, width)
        row_ref[pl.ds(s * lines, lines), :] = slots - high * half
    row = row_ref[...].astype(jnp.int16)
    rhs = rhs_ref[...]
    for start in range(0, half, block):
        part = jnp.dot(onehot_block(row, start, block), rhs, preferred_element_type=jnp.float32)
        out_ref[pl.ds(start, block), :] = part[:, :width]
        out_ref[pl.ds(half + start, block), :] = part[:, width:]


def cold_sums(group, got, data, table):
    owners, capacity, width = data.shape
    lines = capacity // LANES
    rows = got.shape[1]
    return pl.pallas_call(
        functools.partial(cold_kernel, block=math.gcd(table // 2, 256), at=rows - 2 * SUB, lines=lines),
        grid_spec=pltpu.PrefetchScalarGridSpec(
            num_scalar_prefetch=1,
            grid=(1,),
            in_specs=[
                pl.BlockSpec((owners, rows, LANES), lambda i, group: (group[0], 0, 0)),
                pl.BlockSpec((owners, capacity, width), lambda i, group: (0, 0, 0)),
            ],
            out_specs=pl.BlockSpec((table, width), lambda i, group: (0, 0)),
            scratch_shapes=[
                pltpu.VMEM((owners * capacity, 2 * width), jnp.bfloat16),
                pltpu.VMEM((owners * lines, LANES), jnp.int32),
            ],
        ),
        out_shape=jax.ShapeDtypeStruct((table, width), jnp.float32),
        cost_estimate=pl.CostEstimate(flops=2 * owners * capacity * table * width, bytes_accessed=2 * owners * capacity * width, transcendentals=0),
        name="cold_sums",
    )(group, got, data)


def per_device(hot_ids, hot_grads, cold_grads, cold_slots, cold_counts):
    groups, owners = lax.axis_size("chip"), lax.axis_size("gy")
    peers = groups * owners
    everyone = ("chip", "gy")
    core = lax.axis_index("core").astype(jnp.int32).reshape(1)
    chip = lax.axis_index("chip").astype(jnp.int32).reshape(1)
    swap = [(0, 1), (1, 0)]
    factor = (HOT / (hot_ids.shape[0] * peers * 2)) ** 0.5

    capacity, width = cold_grads.shape[3:]
    blocks = cold_grads.reshape(owners, capacity, width)
    slots = cold_slots.reshape(owners, capacity // LANES, LANES)
    cold_rows = lax.all_to_all(blocks, "gy", split_axis=0, concat_axis=0, tiled=True)

    mine, send = hot_sums(core, hot_ids, hot_grads, HOT)
    got = lax.ppermute(send, "core", swap)
    packed = pack(mine, got, slots, cold_counts.reshape(owners), peers)
    parts = lax.all_to_all(packed, everyone, split_axis=0, concat_axis=0, tiled=True)
    summed = add(parts, factor)
    all_rows = lax.all_to_all(summed, everyone, split_axis=0, concat_axis=0, tiled=True)
    others = lax.ppermute(all_rows, "core", swap)
    hot_grad = unpack(core, all_rows, others, HOT)

    cold_grad = cold_sums(chip, parts, cold_rows, OWN_ROWS)
    return hot_grad, cold_grad.reshape(1, OWN_ROWS, width)


def solution(mesh):
    wide, owners = mesh.devices.shape
    split = Mesh(mesh.devices.reshape(wide // 2, 2, owners), ("chip", "core", "gy"))
    every = ("chip", "core", "gy")
    gx = ("chip", "core")
    return jax.shard_map(
        per_device,
        mesh=split,
        in_specs=(
            P(every),
            P(every, None),
            P(gx, "gy", None, None, None),
            P(gx, "gy", None, None),
            P(gx, "gy", None),
        ),
        out_specs=(P(), P(gx, "gy", None)),
        check_vma=False,
    )
```

time: 186 us -> 87.1 us (0.47)
  waiting for transfers between devices: 130 us -> 25.8 us
  blocking collectives: 0 us -> 34.1 us
  matrix products: 24.7 us -> 0 us
  Pallas kernels: 0 us -> 18.9 us
  between operations: 13.9 us -> 0.68 us
  starting transfers between devices: 11 us -> 4.12 us
  other arithmetic: 3.89 us -> 0 us
    reduce_scatter x1 -> x0, waiting for transfers between devices: 56.6 us -> none  [hot_part(): shared = lax.psum_scatter(local_sum, 'gy', scatter_dimension=0, tiled=True)]
    all_gather x1 -> x0, waiting for transfers between devices: 35 us -> none  [hot_part(): total = lax.all_gather(shared, 'gy', axis=0, tiled=True)]
    all_to_all x0 -> x2, blocking collectives: none -> 34.1 us  [the longest x1 19.9 us: per_device(): lax.all_to_all(packed, everyone, split_axis=0, concat_axis=0, tiled=True)]
    psum x1 -> x0, waiting for transfers between devices: 32.9 us -> none  [hot_part(): shared = lax.psum(shared, 'gx')]
    dot_general x8 -> x0, matrix products: 24.7 us -> none  [add_block(): jnp.dot(selector, data_here, preferred_element_type=jnp.float32)]
    all_to_all x2 -> x1, waiting for transfers between devices: 5.07 us -> 24.6 us  [per_device(): lax.all_to_all(blocks, 'gy', split_axis=0, concat_axis=0, tiled=True)]
    pallas_call x0 -> x5, Pallas kernels: none -> 18.9 us  [the longest x1 7.5 us: hot_sums(): pl.pallas_call(functools.partial(hot_kernel, block=math.gcd(half, 256)),...]
    all_to_all x2 -> x1, starting transfers between devices: 10.9 us -> 3.56 us  [per_device(): lax.all_to_all(blocks, 'gy', split_axis=0, concat_axis=0, tiled=True)]
  transfers between devices with their start and end apart: 5 -> 3, of which waited for: 4 -> 2; matrix products, arithmetic and copies ran while one was open for 5% -> 1% of each run, Pallas kernels for 0% -> 6%
where the time goes in v1:
time: 87.1 us; the launch traced here: 86.6 us
  blocking collectives  34.1 us (39%)
  waiting for transfers between devices  25.8 us (30%)
  Pallas kernels  18.9 us (22%)
  starting transfers between devices  4.12 us (5%)
  local copies, waits for them, and re-layouts  3.09 us (4%)
    all_to_all x1, waiting for transfers between devices, per_device(): lax.all_to_all(blocks, 'gy', split_axis=0, concat_axis=0, tiled=True)  24.6 us
    all_to_all x1, blocking collectives, per_device(): lax.all_to_all(packed, everyone, split_axis=0, concat_axis=0, tiled=True)  19.9 us
    all_to_all x1, blocking collectives, per_device(): lax.all_to_all(summed, everyone, split_axis=0, concat_axis=0, tiled=True)  14.1 us
    pallas_call x1, Pallas kernels, hot_sums(): pl.pallas_call(functools.partial(hot_kernel, block=math.gcd(half, 256)),...  7.5 us
    pallas_call x1, Pallas kernels, cold_sums(): pl.pallas_call(functools.partial(cold_kernel, block=math.gcd(table // 2,...  5.35 us
    all_to_all x1, starting transfers between devices, per_device(): lax.all_to_all(blocks, 'gy', split_axis=0, concat_axis=0, tiled=True)  3.56 us
    unnamed x10, local copies, waits for them, and re-layouts  2.49 us
    pallas_call x1, Pallas kernels, unpack(): pl.pallas_call(unpack_kernel, in_specs=[pl.BlockSpec(memory_space=pltpu.S...  2.17 us
  transfers between devices with their start and end apart: 3, of which 2 were waited for; matrix products, arithmetic and copies ran while one was open for 1% of the time, Pallas kernels for 6%

profile of v1, /device:TPU:0, one launch (start us, length us, event | category | flops | bytes accessed | tf_op | source)
XLA Modules:
  0.0 86.6 jit_solution(1668473759975337562)
XLA Ops:
  0.6 0.0 copy-start.4
  0.6 7.5 %hot_sums.1 = (f32[1024,128]{1,0:T(8,128)}, f32[1024,128]{1,0:T(8,128)}) custom-call(s32[1]{0:T(128)} %bitcast.core_ref, s32[64,128]{1,0:T(8,128)} %bitcast.9, bf16[8192,128]{1,0:T(8,128)(2,1)} %data_ref.1), custom_call_target="tpu_custom_call" | custom-call | flops 4294967296 | bytes 2097152 | tf_op jit(solution)/shard_map/hot_sums/pallas_call | solution.py:63
  8.1 0.5 collective-permute-start
  8.6 0.0 copy-done.4
  8.6 0.6 reshape.28.slots_ref
  9.2 1.1 %collective-permute-done.got_ref = f32[1024,128]{1,0:T(8,128)S(1)} collective-permute-done((f32[1024,128]{1,0:T(8,128)}, f32[1024,128]{1,0:T(8,128)S(1)}, u32[]{:S(2)}, u32[]{:S(2)}) %collective-permute-start) | collective-permute-done | bytes 524320 | tf_op jit(solution)/shard_map/ppermute | solution.py:237
  10.4 0.0 copy-start.2
  10.4 0.8 copy-done.2
  11.2 2.1 %pack.1 = s16[16,80,128]{2,1,0:T(8,128)(2,1)} custom-call(s32[8]{0:T(128)} %bitcast.8, f32[1024,128]{1,0:T(8,128)} %get-tuple-element.4.mine_ref, f32[1024,128]{1,0:T(8,128)} %copy-done.2, s32[8,4,128]{2,1,0:T(4,128)} %reshape.28.slots_ref), custom_call_target="tpu_custom_call" | custom-call | flops 1048576 | bytes 1310720 | tf_op jit(solution)/shard_map/pack/pallas_call | solution.py:122
  13.2 19.9 %all_to_all.15.got_ref.slots_ref = s16[16,80,128]{2,1,0:T(8,128)(2,1)} all-to-all(s16[16,80,128]{2,1,0:T(8,128)(2,1)} %pack.1), channel_id=1, replica_groups=mesh['chip'=2,'core'=2,'gy'=8] {'chip','gy'}, dimensions={0} | all-to-all | bytes 655360 | tf_op jit(solution)/shard_map/all_to_all | solution.py:239
  33.2 1.8 %add.1 = s16[16,80,128]{2,1,0:T(8,128)(2,1)} custom-call(s16[16,80,128]{2,1,0:T(8,128)(2,1)} %all_to_all.15.got_ref.slots_ref), custom_call_target="tpu_custom_call" | custom-call | flops 1310720 | bytes 655360 | tf_op jit(solution)/shard_map/add/pallas_call | solution.py:147
  35.0 14.1 %all_to_all.16.mine_ref = s16[16,80,128]{2,1,0:T(8,128)(2,1)S(1)} all-to-all(s16[16,80,128]{2,1,0:T(8,128)(2,1)} %add.1), channel_id=1, replica_groups=mesh['chip'=2,'core'=2,'gy'=8] {'chip','gy'}, dimensions={0} | all-to-all | bytes 655360 | tf_op jit(solution)/shard_map/all_to_all | solution.py:241
  49.1 0.0 copy-start
  49.1 3.6 %all-to-all-start.2 = ((bf16[8,512,128]{2,1,0:T(8,128)(2,1)}), bf16[8,512,128]{2,1,0:T(8,128)(2,1)S(1)}, u32[]{:S(2)}, u32[]{:S(2)}) async-start(bf16[8,512,128]{2,1,0:T(8,128)(2,1)} %bitcast.4), calls=%async_computation.2 | async-start | bytes 2097152 | tf_op jit(solution)/shard_map/all_to_all | solution.py:234
  52.7 0.1 collective-permute-start.1
  52.8 24.6 %all-to-all-done.2.data_ref = bf16[8,512,128]{2,1,0:T(8,128)(2,1)S(1)} async-done(((bf16[8,512,128]{2,1,0:T(8,128)(2,1)}), bf16[8,512,128]{2,1,0:T(8,128)(2,1)S(1)}, u32[]{:S(2)}, u32[]{:S(2)}) %all-to-all-start.2) | async-done | bytes 1048608 | tf_op jit(solution)/shard_map/all_to_all | solution.py:234
  77.4 0.0 copy-start.1
  77.4 1.0 %copy-done.1 = bf16[8,512,128]{2,1,0:T(8,128)(2,1)} copy-done((bf16[8,512,128]{2,1,0:T(8,128)(2,1)}, bf16[8,512,128]{2,1,0:T(8,128)(2,1)S(1)}, u32[]{:S(2)}) %copy-start.1) | copy-done | bytes 1048600
  78.4 5.4 %cold_sums.1 = f32[2048,128]{1,0:T(8,128)} custom-call(s32[1]{0:T(128)} %bitcast.3.group_ref, s16[16,80,128]{2,1,0:T(8,128)(2,1)} %all_to_all.15.got_ref.slots_ref, bf16[8,512,128]{2,1,0:T(8,128)(2,1)} %copy-done.1), custom_call_target="tpu_custom_call" | custom-call | flops 2147483648 | bytes 1048576 | tf_op jit(solution)/shard_map/cold_sums/pallas_call | solution.py:201
  83.7 0.0 copy-done
  83.7 0.0 collective-permute-done.1.other_ref
  83.7 0.0 copy-start.3
  83.7 0.7 copy-done.3
  84.5 2.2 %unpack.1 = f32[2048,128]{1,0:T(8,128)} custom-call(s32[1]{0:T(128)} %bitcast.core_ref, s16[16,80,128]{2,1,0:T(8,128)(2,1)} %copy-done, s16[16,80,128]{2,1,0:T(8,128)(2,1)} %copy-done.3), custom_call_target="tpu_custom_call" | custom-call | flops 1048576 | bytes 1572864 | tf_op jit(solution)/shard_map/unpack/pallas_call | solution.py:171
Async XLA Ops:
  0.6 8.0 %copy-start.4 = (s32[1,1,8,512]{3,2,1,0:T(8,128)S(1)}, s32[1,1,8,512]{3,2,1,0:T(8,128)}, u32[]{:S(2)}) copy-start(s32[1,1,8,512]{3,2,1,0:T(8,128)} %param.8) | copy-start | bytes 49156
  8.1 2.2 %collective-permute-start = (f32[1024,128]{1,0:T(8,128)}, f32[1024,128]{1,0:T(8,128)S(1)}, u32[]{:S(2)}, u32[]{:S(2)}) collective-permute-start(f32[1024,128]{1,0:T(8,128)} %get-tuple-element.5), channel_id=1, source_target_pairs={{0,8},{8,0},{1,9},{9,1},{2,10},{10,2},{3,11},{11,3},{4,12},{12,4},... | collective-permute-start | bytes 1572872 | tf_op jit(solution)/shard_map/ppermute | solution.py:237
  10.4 0.8 copy-start.2
  49.1 34.6 %copy-start = (s16[16,80,128]{2,1,0:T(8,128)(2,1)}, s16[16,80,128]{2,1,0:T(8,128)(2,1)S(1)}, u32[]{:S(2)}) copy-start(s16[16,80,128]{2,1,0:T(8,128)(2,1)S(1)} %all_to_all.16.mine_ref) | copy-start | bytes 983044
  49.1 28.3 %all-to-all-start.2 = ((bf16[8,512,128]{2,1,0:T(8,128)(2,1)}), bf16[8,512,128]{2,1,0:T(8,128)(2,1)S(1)}, u32[]{:S(2)}, u32[]{:S(2)}) async-start(bf16[8,512,128]{2,1,0:T(8,128)(2,1)} %bitcast.4), calls=%async_computation.2 | async-start | bytes 2097152 | tf_op jit(solution)/shard_map/all_to_all | solution.py:234
  52.7 31.0 %collective-permute-start.1 = (s16[16,80,128]{2,1,0:T(8,128)(2,1)S(1)}, s16[16,80,128]{2,1,0:T(8,128)(2,1)S(1)}, u32[]{:S(2)}, u32[]{:S(2)}) collective-permute-start(s16[16,80,128]{2,1,0:T(8,128)(2,1)S(1)} %all_to_all.16.mine_ref), channel_id=1, source_target_pairs={{0,8},{8,0},{1,9},{9,1},{2,10},{10,2},{3,11},{11,3},{4,12},{12,4},... | collective-permute-start | bytes 983048 | tf_op jit(solution)/shard_map/ppermute | solution.py:242
  77.4 1.0 %copy-start.1 = (bf16[8,512,128]{2,1,0:T(8,128)(2,1)}, bf16[8,512,128]{2,1,0:T(8,128)(2,1)S(1)}, u32[]{:S(2)}) copy-start(bf16[8,512,128]{2,1,0:T(8,128)(2,1)S(1)} %all-to-all-done.2.data_ref) | copy-start | bytes 3145732
  83.7 0.7 copy-start.3

commit v2 on v1

--- a/solution.py
+++ b/solution.py
@@ -9,6 +9,7 @@
 from jax.sharding import Mesh
 from jax.sharding import PartitionSpec as P
 
+
 HOT = 2048
 OWN_ROWS = 2048
 LANES = 128
@@ -16,6 +17,7 @@
 STEPS = 128.0
 TOP = 32600.0
 TINY = 2.0**-100
+ROOM = pltpu.CompilerParams(vmem_limit_bytes=20 * 2**20)
 
 
 def masked_halves(keep, data_ref, rhs_ref, base, width):
@@ -72,6 +74,7 @@
         out_shape=[jax.ShapeDtypeStruct((half, width), jnp.float32)] * 2,
         scratch_shapes=[pltpu.VMEM((step, 2 * width), jnp.bfloat16)],
         cost_estimate=pl.CostEstimate(flops=2 * lookups * table * width, bytes_accessed=2 * lookups * width, transcendentals=0),
+        compiler_params=ROOM,
         name="hot_sums",
     )(core, ids.reshape(lookups // LANES, LANES), data)
 
@@ -100,7 +103,7 @@
 
 
 def pack_kernel(counts_ref, mine_ref, got_ref, slots_ref, out_ref):
-    peers, rows, width = out_ref.shape
+    peers, rows, _ = out_ref.shape
     rows -= 2 * SUB
     owners, lines, _ = slots_ref.shape
     places = lax.broadcasted_iota(jnp.int32, (lines, LANES), 0) * LANES + lax.broadcasted_iota(jnp.int32, (lines, LANES), 1)
@@ -125,6 +128,7 @@
         out_specs=whole,
         out_shape=jax.ShapeDtypeStruct((peers, half // peers + 2 * SUB, width), jnp.int16),
         cost_estimate=pl.CostEstimate(flops=half * width * 8, bytes_accessed=half * width * 10, transcendentals=0),
+        compiler_params=ROOM,
         name="pack",
     )(counts, mine, got, slots)
 
@@ -150,12 +154,13 @@
         out_specs=whole,
         out_shape=jax.ShapeDtypeStruct(got.shape, jnp.int16),
         cost_estimate=pl.CostEstimate(flops=got.size * 8, bytes_accessed=got.size * 4, transcendentals=0),
+        compiler_params=ROOM,
         name="add",
     )(got)
 
 
 def unpack_kernel(core_ref, mine_ref, other_ref, out_ref):
-    peers, rows, width = mine_ref.shape
+    peers, rows, _ = mine_ref.shape
     rows -= 2 * SUB
     core = core_ref[0]
     for ref, side in ((mine_ref, core), (other_ref, 1 - core)):
@@ -166,7 +171,7 @@
 
 
 def unpack(core, mine, other, table):
-    peers, rows, width = mine.shape
+    _, _, width = mine.shape
     whole = pl.BlockSpec(memory_space=pltpu.VMEM)
     return pl.pallas_call(
         unpack_kernel,
@@ -174,18 +179,28 @@
         out_specs=whole,
         out_shape=jax.ShapeDtypeStruct((table, width), jnp.float32),
         cost_estimate=pl.CostEstimate(flops=table * width * 4, bytes_accessed=table * width * 6, transcendentals=0),
+        compiler_params=ROOM,
         name="unpack",
     )(core, mine, other)
 
 
-def cold_kernel(group_ref, slots_ref, data_ref, out_ref, rhs_ref, row_ref, *, block, at, lines):
-    owners, capacity, width = data_ref.shape
+def partner(me, step, count):
+    if count & (count - 1):
+        return (me - step) % count, (me + step) % count
+    return me ^ step, me ^ step
+
+
+def cold_kernel(place_ref, slots_ref, own_ref, *refs, block, at, lines):
+    moved, (out_ref, rhs_ref, row_ref) = refs[:-3], refs[-3:]
+    _, capacity, width = own_ref.shape
+    owners = len(moved) + 1
     half = out_ref.shape[0] // 2
-    for s in range(owners):
-        slots = slots_ref[s, at:, :].astype(jnp.int32)[SUB : SUB + lines]
+    for step, ref in enumerate((own_ref.at[0], *moved)):
+        source, _ = partner(place_ref[1], step, owners)
+        slots = slots_ref[source, at:, :].astype(jnp.int32)[SUB : SUB + lines]
         high = (slots >= half).astype(jnp.int32)
-        masked_halves((high == 0).astype(jnp.float32), data_ref.at[s], rhs_ref, s * capacity, width)
-        row_ref[pl.ds(s * lines, lines), :] = slots - high * half
+        masked_halves((high == 0).astype(jnp.float32), ref, rhs_ref, step * capacity, width)
+        row_ref[pl.ds(step * lines, lines), :] = slots - high * half
     row = row_ref[...].astype(jnp.int16)
     rhs = rhs_ref[...]
     for start in range(0, half, block):
@@ -194,8 +209,8 @@
         out_ref[pl.ds(half + start, block), :] = part[:, width:]
 
 
-def cold_sums(group, got, data, table):
-    owners, capacity, width = data.shape
+def cold_sums(place, got, own, moved, table):
+    owners, capacity, width = own.shape
     lines = capacity // LANES
     rows = got.shape[1]
     return pl.pallas_call(
@@ -204,10 +219,11 @@
             num_scalar_prefetch=1,
             grid=(1,),
             in_specs=[
-                pl.BlockSpec((owners, rows, LANES), lambda i, group: (group[0], 0, 0)),
-                pl.BlockSpec((owners, capacity, width), lambda i, group: (0, 0, 0)),
-            ],
-            out_specs=pl.BlockSpec((table, width), lambda i, group: (0, 0)),
+                pl.BlockSpec((owners, rows, LANES), lambda i, place: (place[0], 0, 0)),
+                pl.BlockSpec((1, capacity, width), lambda i, place: (place[1], 0, 0)),
+            ]
+            + [pl.BlockSpec((capacity, width), lambda i, place: (0, 0))] * len(moved),
+            out_specs=pl.BlockSpec((table, width), lambda i, place: (0, 0)),
             scratch_shapes=[
                 pltpu.VMEM((owners * capacity, 2 * width), jnp.bfloat16),
                 pltpu.VMEM((owners * lines, LANES), jnp.int32),
@@ -215,8 +231,9 @@
         ),
         out_shape=jax.ShapeDtypeStruct((table, width), jnp.float32),
         cost_estimate=pl.CostEstimate(flops=2 * owners * capacity * table * width, bytes_accessed=2 * owners * capacity * width, transcendentals=0),
+        compiler_params=ROOM,
         name="cold_sums",
-    )(group, got, data)
+    )(place, got, own, *moved)
 
 
 def per_device(hot_ids, hot_grads, cold_grads, cold_slots, cold_counts):
@@ -224,25 +241,28 @@
     peers = groups * owners
     everyone = ("chip", "gy")
     core = lax.axis_index("core").astype(jnp.int32).reshape(1)
-    chip = lax.axis_index("chip").astype(jnp.int32).reshape(1)
+    chip, owner = lax.axis_index("chip"), lax.axis_index("gy")
+    place = jnp.stack([chip, owner]).astype(jnp.int32)
     swap = [(0, 1), (1, 0)]
     factor = (HOT / (hot_ids.shape[0] * peers * 2)) ** 0.5
 
     capacity, width = cold_grads.shape[3:]
     blocks = cold_grads.reshape(owners, capacity, width)
     slots = cold_slots.reshape(owners, capacity // LANES, LANES)
-    cold_rows = lax.all_to_all(blocks, "gy", split_axis=0, concat_axis=0, tiled=True)
-
+    moved = []
+    for step in range(1, owners):
+        pairs = [(i, partner(i, step, owners)[1]) for i in range(owners)]
+        block = lax.dynamic_index_in_dim(blocks, partner(owner, step, owners)[1], 0, keepdims=False)
+        moved.append(lax.ppermute(block, "gy", pairs))
     mine, send = hot_sums(core, hot_ids, hot_grads, HOT)
     got = lax.ppermute(send, "core", swap)
     packed = pack(mine, got, slots, cold_counts.reshape(owners), peers)
     parts = lax.all_to_all(packed, everyone, split_axis=0, concat_axis=0, tiled=True)
     summed = add(parts, factor)
     all_rows = lax.all_to_all(summed, everyone, split_axis=0, concat_axis=0, tiled=True)
+    cold_grad = cold_sums(place, parts, blocks, moved, OWN_ROWS)
     others = lax.ppermute(all_rows, "core", swap)
     hot_grad = unpack(core, all_rows, others, HOT)
-
-    cold_grad = cold_sums(chip, parts, cold_rows, OWN_ROWS)
     return hot_grad, cold_grad.reshape(1, OWN_ROWS, width)
 
 

time: 87.1 us -> 73.6 us (0.85)
  blocking collectives: 34.1 us -> 19.6 us
  starting transfers between devices: 4.12 us -> 15.9 us
  Pallas kernels: 18.9 us -> 12.5 us
  waiting for transfers between devices: 25.8 us -> 22 us
    all_to_all x1, waiting for transfers between devices: 24.6 us -> 0.01 us  [per_device(): lax.all_to_all(summed, everyone, split_axis=0, concat_axis=0, tiled=True)]
    ppermute x0 -> x7, waiting for transfers between devices: none -> 20.5 us  [per_device(): moved.append(lax.ppermute(block, 'gy', pairs))]
    all_to_all x1 -> x0, blocking collectives: 14.1 us -> none  [per_device(): lax.all_to_all(summed, everyone, split_axis=0, concat_axis=0, tiled=True)]
    ppermute x0 -> x7, starting transfers between devices: none -> 11.7 us  [per_device(): moved.append(lax.ppermute(block, 'gy', pairs))]
    pallas_call x1, Pallas kernels: 7.5 us -> 5.3 us  [hot_sums(): pl.pallas_call(functools.partial(hot_kernel, block=math.gcd(half, 256)),...]
    pallas_call x1, Pallas kernels: 2.05 us -> 0.67 us  [pack(): pl.pallas_call(pack_kernel, in_specs=[pl.BlockSpec(memory_space=pltpu.SME...]
    pallas_call x1, Pallas kernels: 2.17 us -> 1.1 us  [unpack(): pl.pallas_call(unpack_kernel, in_specs=[pl.BlockSpec(memory_space=pltpu.S...]
    pallas_call x1, Pallas kernels: 1.83 us -> 0.86 us  [add(): pl.pallas_call(functools.partial(add_kernel, factor=factor), in_specs=[wh...]
  transfers between devices with their start and end apart: 3 -> 10, of which waited for: 2 -> 5; matrix products, arithmetic and copies ran while one was open for 1% -> 0% of each run, Pallas kernels for 6% -> 6%
where the time goes in v2:
time: 73.6 us; the launch traced here: 73.3 us
  waiting for transfers between devices  22 us (30%)
  blocking collectives  19.6 us (27%)
  starting transfers between devices  15.9 us (22%)
  Pallas kernels  12.5 us (17%)
  local copies, waits for them, and re-layouts  2.44 us (3%)
  between operations  0.75 us (1%)
    ppermute x7, waiting for transfers between devices, per_device(): moved.append(lax.ppermute(block, 'gy', pairs))  20.5 us
    all_to_all x1, blocking collectives, per_device(): lax.all_to_all(packed, everyone, split_axis=0, concat_axis=0, tiled=True)  19.6 us
    ppermute x7, starting transfers between devices, per_device(): moved.append(lax.ppermute(block, 'gy', pairs))  11.7 us
    pallas_call x1, Pallas kernels, hot_sums(): pl.pallas_call(functools.partial(hot_kernel, block=math.gcd(half, 256)),...  5.3 us
    pallas_call x1, Pallas kernels, cold_sums(): pl.pallas_call(functools.partial(cold_kernel, block=math.gcd(table // 2,...  4.57 us
    all_to_all x1, starting transfers between devices, per_device(): lax.all_to_all(summed, everyone, split_axis=0, concat_axis=0, tiled=True)  3.54 us
    unnamed x10, local copies, waits for them, and re-layouts  2.36 us
    ppermute x1, waiting for transfers between devices, per_device(): got = lax.ppermute(send, 'core', swap)  1.52 us
  transfers between devices with their start and end apart: 10, of which 5 were waited for; matrix products, arithmetic and copies ran while one was open for 0% of the time, Pallas kernels for 6%

profile of v2, /device:TPU:0, one launch (start us, length us, event | category | flops | bytes accessed | tf_op | source)
XLA Modules:
  0.0 73.3 jit_solution(13151919957647226377)
XLA Ops:
  0.6 0.0 copy-start.2
  0.6 1.6 %copy-done.2 = bf16[8192,128]{1,0:T(8,128)(2,1)S(1)} copy-done((bf16[8192,128]{1,0:T(8,128)(2,1)S(1)}, bf16[8192,128]{1,0:T(8,128)(2,1)}, u32[]{:S(2)}) %copy-start.2) | copy-done | bytes 2097176
  2.2 0.0 copy-start.3
  2.2 0.8 %copy-done.3 = s32[8192]{0:T(1024)S(1)} copy-done((s32[8192]{0:T(1024)S(1)}, s32[8192]{0:T(1024)}, u32[]{:S(2)}) %copy-start.3) | copy-done | bytes 32792
  3.0 0.0 copy-start.4
  3.0 0.0 copy-start.1
  3.0 5.3 %hot_sums.1 = (f32[1024,128]{1,0:T(8,128)S(1)}, f32[1024,128]{1,0:T(8,128)S(1)}) custom-call(s32[1]{0:T(128)} %bitcast.core_ref, s32[64,128]{1,0:T(8,128)S(1)} %bitcast.25, bf16[8192,128]{1,0:T(8,128)(2,1)S(1)} %copy-done.2), custom_call_target="tpu_custom_call" | custom-call | flops 4294967296 | bytes 2097152 | tf_op jit(solution)/shard_map/hot_sums/pallas_call | solution.py:65
  8.3 0.0 copy-start
  8.3 0.6 collective-permute-start
  8.9 0.0 copy-done.4
  8.9 1.5 %collective-permute-done.got_ref = f32[1024,128]{1,0:T(8,128)S(1)} collective-permute-done((f32[1024,128]{1,0:T(8,128)S(1)}, f32[1024,128]{1,0:T(8,128)S(1)}, u32[]{:S(2)}, u32[]{:S(2)}) %collective-permute-start) | collective-permute-done | bytes 524320 | tf_op jit(solution)/shard_map/ppermute | solution.py:258
  10.4 0.0 copy-done.1
  10.4 0.7 pack.1
  11.1 19.6 %all_to_all.10.got_ref.slots_ref = s16[16,80,128]{2,1,0:T(8,128)(2,1)S(1)} all-to-all(s16[16,80,128]{2,1,0:T(8,128)(2,1)S(1)} %pack.1), channel_id=1, replica_groups=mesh['chip'=2,'core'=2,'gy'=8] {'chip','gy'}, dimensions={0} | all-to-all | bytes 655360 | tf_op jit(solution)/shard_map/all_to_all | solution.py:260
  30.7 0.9 %add.32 = s16[16,80,128]{2,1,0:T(8,128)(2,1)} custom-call(s16[16,80,128]{2,1,0:T(8,128)(2,1)S(1)} %all_to_all.10.got_ref.slots_ref), custom_call_target="tpu_custom_call" | custom-call | flops 1310720 | bytes 655360 | tf_op jit(solution)/shard_map/add/pallas_call | solution.py:151
  31.6 3.5 %all-to-all-start.1 = ((s16[16,80,128]{2,1,0:T(8,128)(2,1)}), s16[16,80,128]{2,1,0:T(8,128)(2,1)S(1)}, u32[]{:S(2)}, u32[]{:S(2)}) async-start(s16[16,80,128]{2,1,0:T(8,128)(2,1)} %add.32), calls=%async_computation.1 | async-start | bytes 655360 | tf_op jit(solution)/shard_map/all_to_all | solution.py:262
  35.2 0.0 copy-done
  35.2 0.1 dynamic-slice_bitcast_fusion
  35.3 4.6 %collective-permute-start.8 = (bf16[512,128]{1,0:T(8,128)(2,1)S(1)}, bf16[512,128]{1,0:T(8,128)(2,1)S(1)}, u32[]{:S(2)}, u32[]{:S(2)}) collective-permute-start(bf16[512,128]{1,0:T(8,128)(2,1)S(1)} %get-tuple-element.6), channel_id=1, source_target_pairs={{0,7},{1,6},{2,5},{3,4},{4,3},{5,2},{6,1},{7,0},{8,15},{9,14},{10,... | collective-permute-start | bytes 393224 | tf_op jit(solution)/shard_map/ppermute | solution.py:256
  39.8 0.0 collective-permute-start.6
  39.8 2.9 %collective-permute-start.5 = (bf16[512,128]{1,0:T(8,128)(2,1)S(1)}, bf16[512,128]{1,0:T(8,128)(2,1)S(1)}, u32[]{:S(2)}, u32[]{:S(2)}) collective-permute-start(bf16[512,128]{1,0:T(8,128)(2,1)S(1)} %get-tuple-element.8), channel_id=1, source_target_pairs={{0,4},{1,5},{2,6},{3,7},{4,0},{5,1},{6,2},{7,3},{8,12},{9,13},{10,... | collective-permute-start | bytes 393224 | tf_op jit(solution)/shard_map/ppermute | solution.py:256
  42.8 0.6 collective-permute-start.4
  43.3 2.4 %collective-permute-start.3 = (bf16[512,128]{1,0:T(8,128)(2,1)S(1)}, bf16[512,128]{1,0:T(8,128)(2,1)S(1)}, u32[]{:S(2)}, u32[]{:S(2)}) collective-permute-start(bf16[512,128]{1,0:T(8,128)(2,1)S(1)} %get-tuple-element.10), channel_id=1, source_target_pairs={{0,2},{1,3},{2,0},{3,1},{4,6},{5,7},{6,4},{7,5},{8,10},{9,11},{10,... | collective-permute-start | bytes 393224 | tf_op jit(solution)/shard_map/ppermute | solution.py:256
  45.7 3.8 %collective-permute-done.8.refs_6_ = bf16[512,128]{1,0:T(8,128)(2,1)S(1)} collective-permute-done((bf16[512,128]{1,0:T(8,128)(2,1)S(1)}, bf16[512,128]{1,0:T(8,128)(2,1)S(1)}, u32[]{:S(2)}, u32[]{:S(2)}) %collective-permute-start.8) | collective-permute-done | bytes 131104 | tf_op jit(solution)/shard_map/ppermute | solution.py:256
  49.5 0.6 collective-permute-start.2
  50.1 10.8 %collective-permute-done.6.refs_4_ = bf16[512,128]{1,0:T(8,128)(2,1)S(1)} collective-permute-done((bf16[512,128]{1,0:T(8,128)(2,1)S(1)}, bf16[512,128]{1,0:T(8,128)(2,1)S(1)}, u32[]{:S(2)}, u32[]{:S(2)}) %collective-permute-start.6) | collective-permute-done | bytes 131104 | tf_op jit(solution)/shard_map/ppermute | solution.py:256
  60.9 0.8 %collective-permute-start.7 = (bf16[512,128]{1,0:T(8,128)(2,1)S(1)}, bf16[512,128]{1,0:T(8,128)(2,1)S(1)}, u32[]{:S(2)}, u32[]{:S(2)}) collective-permute-start(bf16[512,128]{1,0:T(8,128)(2,1)S(1)} %get-tuple-element.12), channel_id=1, source_target_pairs={{0,6},{1,7},{2,4},{3,5},{4,2},{5,3},{6,0},{7,1},{8,14},{9,15},{10,... | collective-permute-start | bytes 393224 | tf_op jit(solution)/shard_map/ppermute | solution.py:256
  61.6 1.1 %collective-permute-done.5.refs_3_ = bf16[512,128]{1,0:T(8,128)(2,1)S(1)} collective-permute-done((bf16[512,128]{1,0:T(8,128)(2,1)S(1)}, bf16[512,128]{1,0:T(8,128)(2,1)S(1)}, u32[]{:S(2)}, u32[]{:S(2)}) %collective-permute-start.5) | collective-permute-done | bytes 131104 | tf_op jit(solution)/shard_map/ppermute | solution.py:256
  62.8 0.0 all-to-all-done.1.mine_ref
  62.8 0.0 collective-permute-start.1
  62.8 0.1 pad_add_fusion.place_ref
  62.9 0.0 collective-permute-done.4.refs_2_
  62.9 0.0 collective-permute-done.3.refs_1_
  62.9 0.0 collective-permute-done.2.refs_0_
  62.9 4.7 %collective-permute-done.7.refs_5_ = bf16[512,128]{1,0:T(8,128)(2,1)S(1)} collective-permute-done((bf16[512,128]{1,0:T(8,128)(2,1)S(1)}, bf16[512,128]{1,0:T(8,128)(2,1)S(1)}, u32[]{:S(2)}, u32[]{:S(2)}) %collective-permute-start.7) | collective-permute-done | bytes 131104 | tf_op jit(solution)/shard_map/ppermute | solution.py:256
  67.6 4.6 %cold_sums.1 = f32[2048,128]{1,0:T(8,128)} custom-call(s32[2]{0:T(128)S(1)} %pad_add_fusion.place_ref, s16[16,80,128]{2,1,0:T(8,128)(2,1)S(1)} %all_to_all.10.got_ref.slots_ref, bf16[8,512,128]{2,1,0:T(8,128)(2,1)S(1)} %bitcast.23, bf16[512,128]{1,0:T(8,128)(2,1)S(1)} %collective-permute-done.2.refs_0_, bf16[512,128]{1,0:T(8,128)(2,1)S(1)} %collective-permute-done.3.refs_1_, ...), custom_call_target="tpu_custom_call" | custom-call | flops 2147483648 | bytes 1048576 | tf_op jit(solution)/shard_map/cold_sums/pallas_call | solution.py:216
  72.2 0.0 collective-permute-done.1.other_ref
  72.2 1.1 %unpack.1 = f32[2048,128]{1,0:T(8,128)} custom-call(s32[1]{0:T(128)} %bitcast.core_ref, s16[16,80,128]{2,1,0:T(8,128)(2,1)S(1)} %all-to-all-done.1.mine_ref, s16[16,80,128]{2,1,0:T(8,128)(2,1)S(1)} %collective-permute-done.1.other_ref), custom_call_target="tpu_custom_call" | custom-call | flops 1048576 | bytes 1572864 | tf_op jit(solution)/shard_map/unpack/pallas_call | solution.py:176
  (1 shorter events, 0.0 us)
Async XLA Ops:
  0.6 1.6 %copy-start.2 = (bf16[8192,128]{1,0:T(8,128)(2,1)S(1)}, bf16[8192,128]{1,0:T(8,128)(2,1)}, u32[]{:S(2)}) copy-start(bf16[8192,128]{1,0:T(8,128)(2,1)} %data_ref.1) | copy-start | bytes 6291460
  2.2 0.8 %copy-start.3 = (s32[8192]{0:T(1024)S(1)}, s32[8192]{0:T(1024)}, u32[]{:S(2)}) copy-start(s32[8192]{0:T(1024)} %param.5) | copy-start | bytes 98308
  3.0 5.9 %copy-start.4 = (s32[1,1,8,512]{3,2,1,0:T(8,128)S(1)}, s32[1,1,8,512]{3,2,1,0:T(8,128)}, u32[]{:S(2)}) copy-start(s32[1,1,8,512]{3,2,1,0:T(8,128)} %param.8) | copy-start | bytes 49156
  3.0 7.4 %copy-start.1 = (s32[1,1,8]{2,1,0:T(1,128)S(1)}, s32[1,1,8]{2,1,0:T(1,128)}, u32[]{:S(2)}) copy-start(s32[1,1,8]{2,1,0:T(1,128)} %param.9) | copy-start | bytes 100
  8.3 26.9 %copy-start = (bf16[1,1,8,512,128]{4,3,2,1,0:T(8,128)(2,1)S(1)}, bf16[1,1,8,512,128]{4,3,2,1,0:T(8,128)(2,1)}, u32[]{:S(2)}) copy-start(bf16[1,1,8,512,128]{4,3,2,1,0:T(8,128)(2,1)} %param.7) | copy-start | bytes 3145732
  8.3 2.1 %collective-permute-start = (f32[1024,128]{1,0:T(8,128)S(1)}, f32[1024,128]{1,0:T(8,128)S(1)}, u32[]{:S(2)}, u32[]{:S(2)}) collective-permute-start(f32[1024,128]{1,0:T(8,128)S(1)} %get-tuple-element.5), channel_id=1, source_target_pairs={{0,8},{8,0},{1,9},{9,1},{2,10},{10,2},{3,11},{11,3},{4,12},{12,4},... | collective-permute-start | bytes 1572872 | tf_op jit(solution)/shard_map/ppermute | solution.py:258
  31.6 31.2 %all-to-all-start.1 = ((s16[16,80,128]{2,1,0:T(8,128)(2,1)}), s16[16,80,128]{2,1,0:T(8,128)(2,1)S(1)}, u32[]{:S(2)}, u32[]{:S(2)}) async-start(s16[16,80,128]{2,1,0:T(8,128)(2,1)} %add.32), calls=%async_computation.1 | async-start | bytes 655360 | tf_op jit(solution)/shard_map/all_to_all | solution.py:262
  35.3 14.2 %collective-permute-start.8 = (bf16[512,128]{1,0:T(8,128)(2,1)S(1)}, bf16[512,128]{1,0:T(8,128)(2,1)S(1)}, u32[]{:S(2)}, u32[]{:S(2)}) collective-permute-start(bf16[512,128]{1,0:T(8,128)(2,1)S(1)} %get-tuple-element.6), channel_id=1, source_target_pairs={{0,7},{1,6},{2,5},{3,4},{4,3},{5,2},{6,1},{7,0},{8,15},{9,14},{10,... | collective-permute-start | bytes 393224 | tf_op jit(solution)/shard_map/ppermute | solution.py:256
  39.8 21.0 %collective-permute-start.6 = (bf16[512,128]{1,0:T(8,128)(2,1)S(1)}, bf16[512,128]{1,0:T(8,128)(2,1)S(1)}, u32[]{:S(2)}, u32[]{:S(2)}) collective-permute-start(bf16[512,128]{1,0:T(8,128)(2,1)S(1)} %get-tuple-element.7), channel_id=1, source_target_pairs={{0,5},{1,4},{2,7},{3,6},{4,1},{5,0},{6,3},{7,2},{8,13},{9,12},{10,... | collective-permute-start | bytes 393224 | tf_op jit(solution)/shard_map/ppermute | solution.py:256
  39.8 22.9 %collective-permute-start.5 = (bf16[512,128]{1,0:T(8,128)(2,1)S(1)}, bf16[512,128]{1,0:T(8,128)(2,1)S(1)}, u32[]{:S(2)}, u32[]{:S(2)}) collective-permute-start(bf16[512,128]{1,0:T(8,128)(2,1)S(1)} %get-tuple-element.8), channel_id=1, source_target_pairs={{0,4},{1,5},{2,6},{3,7},{4,0},{5,1},{6,2},{7,3},{8,12},{9,13},{10,... | collective-permute-start | bytes 393224 | tf_op jit(solution)/shard_map/ppermute | solution.py:256
  42.8 20.1 %collective-permute-start.4 = (bf16[512,128]{1,0:T(8,128)(2,1)S(1)}, bf16[512,128]{1,0:T(8,128)(2,1)S(1)}, u32[]{:S(2)}, u32[]{:S(2)}) collective-permute-start(bf16[512,128]{1,0:T(8,128)(2,1)S(1)} %get-tuple-element.9), channel_id=1, source_target_pairs={{0,3},{1,2},{2,1},{3,0},{4,7},{5,6},{6,5},{7,4},{8,11},{9,10},{10,... | collective-permute-start | bytes 393224 | tf_op jit(solution)/shard_map/ppermute | solution.py:256
  43.3 19.6 %collective-permute-start.3 = (bf16[512,128]{1,0:T(8,128)(2,1)S(1)}, bf16[512,128]{1,0:T(8,128)(2,1)S(1)}, u32[]{:S(2)}, u32[]{:S(2)}) collective-permute-start(bf16[512,128]{1,0:T(8,128)(2,1)S(1)} %get-tuple-element.10), channel_id=1, source_target_pairs={{0,2},{1,3},{2,0},{3,1},{4,6},{5,7},{6,4},{7,5},{8,10},{9,11},{10,... | collective-permute-start | bytes 393224 | tf_op jit(solution)/shard_map/ppermute | solution.py:256
  49.5 13.4 %collective-permute-start.2 = (bf16[512,128]{1,0:T(8,128)(2,1)S(1)}, bf16[512,128]{1,0:T(8,128)(2,1)S(1)}, u32[]{:S(2)}, u32[]{:S(2)}) collective-permute-start(bf16[512,128]{1,0:T(8,128)(2,1)S(1)} %get-tuple-element.11), channel_id=1, source_target_pairs={{0,1},{1,0},{2,3},{3,2},{4,5},{5,4},{6,7},{7,6},{8,9},{9,8},{10,11... | collective-permute-start | bytes 393224 | tf_op jit(solution)/shard_map/ppermute | solution.py:256
  60.9 6.8 %collective-permute-start.7 = (bf16[512,128]{1,0:T(8,128)(2,1)S(1)}, bf16[512,128]{1,0:T(8,128)(2,1)S(1)}, u32[]{:S(2)}, u32[]{:S(2)}) collective-permute-start(bf16[512,128]{1,0:T(8,128)(2,1)S(1)} %get-tuple-element.12), channel_id=1, source_target_pairs={{0,6},{1,7},{2,4},{3,5},{4,2},{5,3},{6,0},{7,1},{8,14},{9,15},{10,... | collective-permute-start | bytes 393224 | tf_op jit(solution)/shard_map/ppermute | solution.py:256
  62.8 9.4 %collective-permute-start.1 = (s16[16,80,128]{2,1,0:T(8,128)(2,1)S(1)}, s16[16,80,128]{2,1,0:T(8,128)(2,1)S(1)}, u32[]{:S(2)}, u32[]{:S(2)}) collective-permute-start(s16[16,80,128]{2,1,0:T(8,128)(2,1)S(1)} %all-to-all-done.1.mine_ref), channel_id=1, source_target_pairs={{0,8},{8,0},{1,9},{9,1},{2,10},{10,2},{3,11},{11,3},{4,12},{12,4},... | collective-permute-start | bytes 983048 | tf_op jit(solution)/shard_map/ppermute | solution.py:264

commit v3 on v2

v3 whole, which is shorter than its diff:
```python
import functools
import math

import jax
import jax.numpy as jnp
from jax import lax
from jax.experimental import pallas as pl
from jax.experimental.pallas import tpu as pltpu
from jax.sharding import Mesh
from jax.sharding import PartitionSpec as P


HOT = 2048
OWN_ROWS = 2048
LANES = 128
SUB = 8
SCALES = SUB // 2
STEPS = 128.0
TOP = 32600.0
TINY = 2.0**-100
ROOM = pltpu.CompilerParams(vmem_limit_bytes=20 * 2**20)


def in_hbm(array):
    return pltpu.with_memory_space_constraint(array, pltpu.HBM)


def masked_halves(keep, data_ref, rhs_ref, base, width):
    flags = keep.T
    for j in range(keep.shape[0]):
        rows = pl.ds(base + j * LANES, LANES)
        column = jnp.broadcast_to(flags[:, j : j + 1], (LANES, width)).astype(jnp.bfloat16)
        data = data_ref[pl.ds(j * LANES, LANES), :]
        kept = data * column
        rhs_ref[rows, :width] = kept
        rhs_ref[rows, width:] = data - kept


def onehot_block(row, start, size):
    places = (lax.broadcasted_iota(jnp.int32, (size, LANES), 0) + start).astype(jnp.int16)
    one, zero = jnp.ones((), jnp.bfloat16), jnp.zeros((), jnp.bfloat16)
    parts = [jnp.where(places == row[j : j + 1, :], one, zero) for j in range(row.shape[0])]
    return jnp.concatenate(parts, axis=1)


def hot_kernel(ids_ref, data_ref, mine_ref, send_ref, rhs_ref, *, block, step):
    half, width = mine_ref.shape
    core = lax.axis_index("core")
    lines = step // LANES
    for first in range(0, data_ref.shape[0], step):
        ids = ids_ref[pl.ds(first // LANES, lines), :]
        high = (ids >= half).astype(jnp.int32)
        masked_halves((high == core).astype(jnp.float32), data_ref.at[pl.ds(first, step)], rhs_ref, 0, width)
        row = (ids - high * half).astype(jnp.int16)
        rhs = rhs_ref[...]
        for start in range(0, half, block):
            part = jnp.dot(onehot_block(row, start, block), rhs, preferred_element_type=jnp.float32)
            rows = pl.ds(start, block)
            if first == 0:
                mine_ref[rows, :] = part[:, :width]
                send_ref[rows, :] = part[:, width:]
            else:
                mine_ref[rows, :] += part[:, :width]
                send_ref[rows, :] += part[:, width:]


def hot_sums(ids, data, table):
    lookups, width = data.shape
    half = table // 2
    step = math.gcd(lookups, 4096)
    whole = pl.BlockSpec(memory_space=pltpu.VMEM)
    return pl.pallas_call(
        functools.partial(hot_kernel, block=math.gcd(half, 256), step=step),
        in_specs=[whole, whole],
        out_specs=[whole, whole],
        out_shape=[jax.ShapeDtypeStruct((half, width), jnp.float32)] * 2,
        scratch_shapes=[pltpu.VMEM((step, 2 * width), jnp.bfloat16)],
        cost_estimate=pl.CostEstimate(flops=2 * lookups * table * width, bytes_accessed=2 * lookups * width, transcendentals=0),
        compiler_params=ROOM,
        name="hot_sums",
    )(ids.reshape(lookups // LANES, LANES), data)


def pick_kernel(blocks_hbm, *refs, steps):
    outs, sems = refs[:-1], refs[-1]
    owner, owners = lax.axis_index("gy"), blocks_hbm.shape[0]
    copies = [
        pltpu.make_async_copy(blocks_hbm.at[partner(owner, step, owners)[1]], out, sems.at[n])
        for n, (step, out) in enumerate(zip(steps, outs))
    ]
    for copy in copies:
        copy.start()
    for copy in copies:
        copy.wait()


def pick(blocks, steps):
    count = len(steps)
    return pl.pallas_call(
        functools.partial(pick_kernel, steps=steps),
        in_specs=[pl.BlockSpec(memory_space=pltpu.HBM)],
        out_specs=[pl.BlockSpec(memory_space=pltpu.VMEM)] * count,
        out_shape=[jax.ShapeDtypeStruct(blocks.shape[1:], blocks.dtype)] * count,
        scratch_shapes=[pltpu.SemaphoreType.DMA((count,))],
        cost_estimate=pl.CostEstimate(flops=5 * 10**9, bytes_accessed=count * blocks[0].size * 2, transcendentals=0),
        compiler_params=ROOM,
        name="pick",
    )(in_hbm(blocks))


def encode(values):
    rows, width = values.shape
    groups = values.reshape(rows // SUB, SUB, width)
    most = jnp.max(jnp.abs(groups), axis=0)
    most = jnp.maximum(jnp.maximum(most[:SCALES], most[SCALES:]), TINY)
    code = jnp.ceil(jnp.log2(most) * STEPS) + 1.0
    scale = jnp.exp2(code * (-1.0 / STEPS)) * TOP
    codes = jnp.round(groups * jnp.concatenate([scale, scale], axis=0)[None])
    return codes.reshape(rows, width), code


def decode(codes, code):
    rows, width = codes.shape
    scale = jnp.exp2(code * (1.0 / STEPS)) * (1.0 / TOP)
    scale = jnp.concatenate([scale, scale], axis=0)
    return (codes.reshape(rows // SUB, SUB, width) * scale[None]).reshape(rows, width)


def narrow(values):
    return values.astype(jnp.int32).astype(jnp.int16)


def widen(values):
    return values.astype(jnp.int32).astype(jnp.float32)


def tail_rows(lines):
    return -(-(SCALES + lines) // SUB) * SUB


def pack_kernel(mine_ref, got_ref, slots_ref, out_ref):
    owners, lines, _ = slots_ref.shape
    tail = tail_rows(lines)
    peers, rows, _ = out_ref.shape
    rows -= tail
    spare = tail - SCALES - lines
    for p in range(peers):
        here = pl.ds(p * rows, rows)
        codes, code = encode(mine_ref[here, :] + got_ref[here, :])
        out_ref[p, :rows, :] = narrow(codes)
        pieces = [code.astype(jnp.int32), slots_ref[p % owners]]
        if spare:
            pieces.append(jnp.zeros((spare, LANES), jnp.int32))
        out_ref[p, rows:, :] = jnp.concatenate(pieces, axis=0).astype(jnp.int16)


def pack(mine, got, slots, peers):
    half, width = mine.shape
    whole = pl.BlockSpec(memory_space=pltpu.VMEM)
    return pl.pallas_call(
        pack_kernel,
        in_specs=[whole, whole, whole],
        out_specs=whole,
        out_shape=jax.ShapeDtypeStruct((peers, half // peers + tail_rows(slots.shape[1]), width), jnp.int16),
        cost_estimate=pl.CostEstimate(flops=half * width * 8, bytes_accessed=half * width * 10, transcendentals=0),
        compiler_params=ROOM,
        name="pack",
    )(mine, got, slots)


def add_kernel(got_ref, out_ref, *, factor, tail):
    peers, rows, width = got_ref.shape
    rows -= tail
    total = jnp.zeros((rows, width), jnp.float32)
    for p in range(peers):
        ends = widen(got_ref[p, rows:, :])
        total += decode(widen(got_ref[p, :rows, :]), ends[:SCALES])
    codes, code = encode(total * factor)
    body, ends = narrow(codes), narrow(jnp.concatenate([code, code], axis=0))
    for p in range(peers):
        out_ref[p, :rows, :] = body
        out_ref[p, rows:, :] = ends


def add(got, factor, tail):
    peers, rows, width = got.shape
    whole = pl.BlockSpec(memory_space=pltpu.VMEM)
    return pl.pallas_call(
        functools.partial(add_kernel, factor=factor, tail=tail),
        in_specs=[whole],
        out_specs=whole,
        out_shape=jax.ShapeDtypeStruct((peers, rows - tail + SUB, width), jnp.int16),
        cost_estimate=pl.CostEstimate(flops=got.size * 8, bytes_accessed=got.size * 4, transcendentals=0),
        compiler_params=ROOM,
        name="add",
    )(got)


def unpack_kernel(mine_ref, other_ref, out_ref):
    peers, rows, _ = mine_ref.shape
    rows -= SUB
    core = lax.axis_index("core")
    for ref, side in ((mine_ref, core), (other_ref, 1 - core)):
        for p in range(peers):
            ends = widen(ref[p, rows:, :])
            start = pl.multiple_of(side * (peers * rows) + p * rows, SUB)
            out_ref[pl.ds(start, rows), :] = decode(widen(ref[p, :rows, :]), ends[:SCALES])


def unpack(mine, other, table):
    width = mine.shape[2]
    whole = pl.BlockSpec(memory_space=pltpu.VMEM)
    return pl.pallas_call(
        unpack_kernel,
        in_specs=[whole, whole],
        out_specs=whole,
        out_shape=jax.ShapeDtypeStruct((table, width), jnp.float32),
        cost_estimate=pl.CostEstimate(flops=table * width * 4, bytes_accessed=table * width * 6, transcendentals=0),
        compiler_params=ROOM,
        name="unpack",
    )(mine, other)


def partner(me, step, count):
    if count & (count - 1):
        return (me - step) % count, (me + step) % count
    return me ^ step, me ^ step


def cold_steps(owners):
    far, near = list(range(owners // 2, owners)), list(range(1, owners // 2))
    early = len(far) * 3 // 4
    return far[:early], far[early:] + near


def cold_kernel(got_ref, own_ref, *refs, block, at, lines):
    moved, (out_ref, rhs_ref, row_ref) = refs[:-3], refs[-3:]
    owners, capacity, width = own_ref.shape
    half = out_ref.shape[0] // 2
    chip, owner = lax.axis_index("chip"), lax.axis_index("gy")
    for step, ref in enumerate((own_ref.at[owner], *moved)):
        source, _ = partner(owner, step, owners)
        slots = got_ref[chip * owners + source, at:, :].astype(jnp.int32)[SCALES : SCALES + lines]
        high = (slots >= half).astype(jnp.int32)
        masked_halves((high == 0).astype(jnp.float32), ref, rhs_ref, step * capacity, width)
        row_ref[pl.ds(step * lines, lines), :] = slots - high * half
    row = row_ref[...].astype(jnp.int16)
    rhs = rhs_ref[...]
    for start in range(0, half, block):
        part = jnp.dot(onehot_block(row, start, block), rhs, preferred_element_type=jnp.float32)
        out_ref[pl.ds(start, block), :] = part[:, :width]
        out_ref[pl.ds(half + start, block), :] = part[:, width:]


def cold_sums(got, own, moved, table):
    owners, capacity, width = own.shape
    lines = capacity // LANES
    whole = pl.BlockSpec(memory_space=pltpu.VMEM)
    return pl.pallas_call(
        functools.partial(cold_kernel, block=math.gcd(table // 2, 256), at=got.shape[1] - tail_rows(lines), lines=lines),
        in_specs=[whole] * (2 + len(moved)),
        out_specs=whole,
        out_shape=jax.ShapeDtypeStruct((table, width), jnp.float32),
        scratch_shapes=[
            pltpu.VMEM((owners * capacity, 2 * width), jnp.bfloat16),
            pltpu.VMEM((owners * lines, LANES), jnp.int32),
        ],
        cost_estimate=pl.CostEstimate(flops=2 * owners * capacity * table * width, bytes_accessed=2 * owners * capacity * width, transcendentals=0),
        compiler_params=ROOM,
        name="cold_sums",
    )(got, own, *moved)


def per_device(hot_ids, hot_grads, cold_grads, cold_slots, cold_counts):
    groups, owners = lax.axis_size("chip"), lax.axis_size("gy")
    peers = groups * owners
    everyone = ("chip", "gy")
    swap = [(0, 1), (1, 0)]
    factor = (HOT / (hot_ids.shape[0] * peers * 2)) ** 0.5

    capacity, width = cold_grads.shape[3:]
    lines = capacity // LANES
    blocks = cold_grads.reshape(owners, capacity, width)
    moved = {}

    def move(steps):
        picked = pick(blocks, steps)
        for n, block in zip(steps, picked):
            moved[n] = lax.ppermute(block, "gy", [(i, partner(i, n, owners)[1]) for i in range(owners)])

    early, late = cold_steps(owners)
    move(early)
    mine, send = hot_sums(hot_ids, hot_grads, HOT)
    got = lax.ppermute(send, "core", swap)
    places = lax.broadcasted_iota(jnp.int32, (owners, capacity), 1)
    used = jnp.where(places < cold_counts.reshape(owners, 1), cold_slots.reshape(owners, capacity), -1)
    packed = pack(mine, got, used.reshape(owners, lines, LANES), peers)
    parts = lax.all_to_all(packed, everyone, split_axis=0, concat_axis=0, tiled=True)
    move(late)
    summed = add(parts, factor, tail_rows(lines))
    all_rows = lax.all_to_all(summed, everyone, split_axis=0, concat_axis=0, tiled=True)
    cold_grad = cold_sums(parts, blocks, [moved[n] for n in range(1, owners)], OWN_ROWS)
    others = lax.ppermute(all_rows, "core", swap)
    hot_grad = unpack(all_rows, others, HOT)
    return hot_grad, cold_grad.reshape(1, OWN_ROWS, width)


def solution(mesh):
    wide, owners = mesh.devices.shape
    split = Mesh(mesh.devices.reshape(wide // 2, 2, owners), ("chip", "core", "gy"))
    every = ("chip", "core", "gy")
    gx = ("chip", "core")
    return jax.shard_map(
        per_device,
        mesh=split,
        in_specs=(
            P(every),
            P(every, None),
            P(gx, "gy", None, None, None),
            P(gx, "gy", None, None),
            P(gx, "gy", None),
        ),
        out_specs=(P(), P(gx, "gy", None)),
        check_vma=False,
    )
```

time: 73.6 us -> 71.6 us (0.973)
  starting transfers between devices: 15.9 us -> 12.8 us
  waiting for transfers between devices: 22 us -> 23.1 us
    ppermute x7, starting transfers between devices: 11.7 us -> 8.66 us  [move(): lax.ppermute(block, 'gy', [(i, partner(i, n, owners)[1]) for i in range(o...]
    pallas_call x4 -> x6, Pallas kernels: 7.93 us -> 9.16 us  [the longest x1 4.86 us: hot_sums(): pl.pallas_call(functools.partial(hot_kernel, block=math.gcd(half, 256), s...]
    ppermute x7, waiting for transfers between devices: 20.5 us -> 21.6 us  [move(): lax.ppermute(block, 'gy', [(i, partner(i, n, owners)[1]) for i in range(o...]
  transfers between devices with their start and end apart: 10 -> 10, of which waited for: 5 -> 5; matrix products, arithmetic and copies ran while one was open for 0% -> 0% of each run, Pallas kernels for 6% -> 9%
where the time goes in v3:
time: 71.6 us; the launch traced here: 71.2 us
  waiting for transfers between devices  23.1 us (32%)
  blocking collectives  19 us (27%)
  Pallas kernels  13.2 us (18%)
  starting transfers between devices  12.8 us (18%)
  local copies, waits for them, and re-layouts  2.36 us (3%)
  between operations  0.72 us (1%)
    ppermute x7, waiting for transfers between devices, move(): lax.ppermute(block, 'gy', [(i, partner(i, n, owners)[1]) for i in range(o...  21.6 us
    all_to_all x1, blocking collectives, per_device(): lax.all_to_all(packed, everyone, split_axis=0, concat_axis=0, tiled=True)  19 us
    ppermute x7, starting transfers between devices, move(): lax.ppermute(block, 'gy', [(i, partner(i, n, owners)[1]) for i in range(o...  8.66 us
    pallas_call x1, Pallas kernels, hot_sums(): pl.pallas_call(functools.partial(hot_kernel, block=math.gcd(half, 256), s...  4.86 us
    pallas_call x1, Pallas kernels, cold_sums(): pl.pallas_call(functools.partial(cold_kernel, block=math.gcd(table // 2,...  4.03 us
    all_to_all x1, starting transfers between devices, per_device(): lax.all_to_all(summed, everyone, split_axis=0, concat_axis=0, tiled=True)  3.54 us
    unnamed x10, local copies, waits for them, and re-layouts  2.35 us
    pallas_call x2, Pallas kernels, pick(): pl.pallas_call(functools.partial(pick_kernel, steps=steps), in_specs=[pl....  2.19 us
  transfers between devices with their start and end apart: 10, of which 5 were waited for; matrix products, arithmetic and copies ran while one was open for 0% of the time, Pallas kernels for 9%

profile of v3, /device:TPU:0, one launch (start us, length us, event | category | flops | bytes accessed | tf_op | source)
XLA Modules:
  0.0 71.2 jit_solution(454000835798480092)
XLA Ops:
  0.6 0.0 copy-start
  0.6 1.6 %copy-done = bf16[8192,128]{1,0:T(8,128)(2,1)S(1)} copy-done((bf16[8192,128]{1,0:T(8,128)(2,1)S(1)}, bf16[8192,128]{1,0:T(8,128)(2,1)}, u32[]{:S(2)}) %copy-start) | copy-done | bytes 2097176
  2.2 0.0 copy-start.2
  2.2 0.8 %copy-done.2 = s32[8192]{0:T(1024)S(1)} copy-done((s32[8192]{0:T(1024)S(1)}, s32[8192]{0:T(1024)}, u32[]{:S(2)}) %copy-start.2) | copy-done | bytes 32792
  3.0 0.0 copy-start.3
  3.0 0.0 copy-start.4
  3.0 4.9 %hot_sums.1 = (f32[1024,128]{1,0:T(8,128)S(1)}, f32[1024,128]{1,0:T(8,128)S(1)}) custom-call(s32[64,128]{1,0:T(8,128)S(1)} %bitcast.9, bf16[8192,128]{1,0:T(8,128)(2,1)S(1)} %copy-done), custom_call_target="tpu_custom_call" | custom-call | flops 4294967296 | bytes 2097152 | tf_op jit(solution)/shard_map/hot_sums/pallas_call | solution.py:72
  7.9 0.6 collective-permute-start
  8.4 0.0 copy-done.3
  8.4 0.0 copy-done.4
  8.5 0.1 compare_select_fusion.slots_ref
  8.5 1.4 %collective-permute-done.got_ref = f32[1024,128]{1,0:T(8,128)S(1)} collective-permute-done((f32[1024,128]{1,0:T(8,128)S(1)}, f32[1024,128]{1,0:T(8,128)S(1)}, u32[]{:S(2)}, u32[]{:S(2)}) %collective-permute-start) | collective-permute-done | bytes 524320 | tf_op jit(solution)/shard_map/ppermute | solution.py:294
  10.0 0.1 pack.1
  10.1 19.0 %all_to_all.10.got_ref = s16[16,72,128]{2,1,0:T(8,128)(2,1)S(1)} all-to-all(s16[16,72,128]{2,1,0:T(8,128)(2,1)S(1)} %pack.1), channel_id=1, replica_groups=mesh['chip'=2,'core'=2,'gy'=8] {'chip','gy'}, dimensions={0} | all-to-all | bytes 589824 | tf_op jit(solution)/shard_map/all_to_all | solution.py:298
  29.1 0.9 %add.5 = s16[16,72,128]{2,1,0:T(8,128)(2,1)} custom-call(s16[16,72,128]{2,1,0:T(8,128)(2,1)S(1)} %all_to_all.10.got_ref), custom_call_target="tpu_custom_call" | custom-call | flops 1179648 | bytes 589824 | tf_op jit(solution)/shard_map/add/pallas_call | solution.py:188
  30.0 3.5 %all-to-all-start.1 = ((s16[16,72,128]{2,1,0:T(8,128)(2,1)}), s16[16,72,128]{2,1,0:T(8,128)(2,1)S(1)}, u32[]{:S(2)}, u32[]{:S(2)}) async-start(s16[16,72,128]{2,1,0:T(8,128)(2,1)} %add.5), calls=%async_computation.1 | async-start | bytes 589824 | tf_op jit(solution)/shard_map/all_to_all | solution.py:301
  33.5 1.1 %pick.3 = (bf16[512,128]{1,0:T(8,128)(2,1)S(1)}, bf16[512,128]{1,0:T(8,128)(2,1)S(1)}, bf16[512,128]{1,0:T(8,128)(2,1)S(1)}) custom-call(bf16[8,512,128]{2,1,0:T(8,128)(2,1)} %bitcast.6), custom_call_target="tpu_custom_call" | custom-call | flops 5000000000 | bytes 393216 | tf_op jit(solution)/shard_map/pick/pallas_call | solution.py:99
  34.6 2.8 %collective-permute-start.5 = (bf16[512,128]{1,0:T(8,128)(2,1)S(1)}, bf16[512,128]{1,0:T(8,128)(2,1)S(1)}, u32[]{:S(2)}, u32[]{:S(2)}) collective-permute-start(bf16[512,128]{1,0:T(8,128)(2,1)S(1)} %get-tuple-element.16), channel_id=1, source_target_pairs={{0,4},{1,5},{2,6},{3,7},{4,0},{5,1},{6,2},{7,3},{8,12},{9,13},{10,... | collective-permute-start | bytes 393224 | tf_op jit(solution)/shard_map/ppermute | solution.py:289
  37.4 1.4 %collective-permute-start.6 = (bf16[512,128]{1,0:T(8,128)(2,1)S(1)}, bf16[512,128]{1,0:T(8,128)(2,1)S(1)}, u32[]{:S(2)}, u32[]{:S(2)}) collective-permute-start(bf16[512,128]{1,0:T(8,128)(2,1)S(1)} %get-tuple-element.17), channel_id=1, source_target_pairs={{0,5},{1,4},{2,7},{3,6},{4,1},{5,0},{6,3},{7,2},{8,13},{9,12},{10,... | collective-permute-start | bytes 393224 | tf_op jit(solution)/shard_map/ppermute | solution.py:289
  38.8 0.0 copy-start.1
  38.8 3.3 %collective-permute-start.7 = (bf16[512,128]{1,0:T(8,128)(2,1)S(1)}, bf16[512,128]{1,0:T(8,128)(2,1)S(1)}, u32[]{:S(2)}, u32[]{:S(2)}) collective-permute-start(bf16[512,128]{1,0:T(8,128)(2,1)S(1)} %get-tuple-element.18), channel_id=1, source_target_pairs={{0,6},{1,7},{2,4},{3,5},{4,2},{5,3},{6,0},{7,1},{8,14},{9,15},{10,... | collective-permute-start | bytes 393224 | tf_op jit(solution)/shard_map/ppermute | solution.py:289
  42.1 1.1 %pick.2 = (bf16[512,128]{1,0:T(8,128)(2,1)S(1)}, bf16[512,128]{1,0:T(8,128)(2,1)S(1)}, bf16[512,128]{1,0:T(8,128)(2,1)S(1)}, bf16[512,128]{1,0:T(8,128)(2,1)S(1)}) custom-call(bf16[8,512,128]{2,1,0:T(8,128)(2,1)} %bitcast.7), custom_call_target="tpu_custom_call" | custom-call | flops 5000000000 | bytes 524288 | tf_op jit(solution)/shard_map/pick/pallas_call | solution.py:99
  43.2 0.6 collective-permute-start.2
  43.9 0.0 collective-permute-start.3
  43.9 10.8 %collective-permute-done.5.refs_3_ = bf16[512,128]{1,0:T(8,128)(2,1)S(1)} collective-permute-done((bf16[512,128]{1,0:T(8,128)(2,1)S(1)}, bf16[512,128]{1,0:T(8,128)(2,1)S(1)}, u32[]{:S(2)}, u32[]{:S(2)}) %collective-permute-start.5) | collective-permute-done | bytes 131104 | tf_op jit(solution)/shard_map/ppermute | solution.py:289
  54.7 0.0 collective-permute-start.4
  54.7 3.7 %collective-permute-done.6.refs_4_ = bf16[512,128]{1,0:T(8,128)(2,1)S(1)} collective-permute-done((bf16[512,128]{1,0:T(8,128)(2,1)S(1)}, bf16[512,128]{1,0:T(8,128)(2,1)S(1)}, u32[]{:S(2)}, u32[]{:S(2)}) %collective-permute-start.6) | collective-permute-done | bytes 131104 | tf_op jit(solution)/shard_map/ppermute | solution.py:289
  58.4 0.5 collective-permute-start.8
  58.9 0.0 collective-permute-done.7.refs_5_
  58.9 0.0 all-to-all-done.1.mine_ref
  58.9 0.0 collective-permute-start.1
  58.9 0.0 collective-permute-done.2.refs_0_
  58.9 0.0 collective-permute-done.3.refs_1_
  58.9 1.6 %collective-permute-done.4.refs_2_ = bf16[512,128]{1,0:T(8,128)(2,1)S(1)} collective-permute-done((bf16[512,128]{1,0:T(8,128)(2,1)S(1)}, bf16[512,128]{1,0:T(8,128)(2,1)S(1)}, u32[]{:S(2)}, u32[]{:S(2)}) %collective-permute-start.4) | collective-permute-done | bytes 131104 | tf_op jit(solution)/shard_map/ppermute | solution.py:289
  60.5 5.5 %collective-permute-done.8.refs_6_ = bf16[512,128]{1,0:T(8,128)(2,1)S(1)} collective-permute-done((bf16[512,128]{1,0:T(8,128)(2,1)S(1)}, bf16[512,128]{1,0:T(8,128)(2,1)S(1)}, u32[]{:S(2)}, u32[]{:S(2)}) %collective-permute-start.8) | collective-permute-done | bytes 131104 | tf_op jit(solution)/shard_map/ppermute | solution.py:289
  66.0 0.0 copy-done.1
  66.0 4.0 %cold_sums.1 = f32[2048,128]{1,0:T(8,128)} custom-call(s16[16,72,128]{2,1,0:T(8,128)(2,1)S(1)} %all_to_all.10.got_ref, bf16[8,512,128]{2,1,0:T(8,128)(2,1)S(1)} %bitcast.8, bf16[512,128]{1,0:T(8,128)(2,1)S(1)} %collective-permute-done.2.refs_0_, bf16[512,128]{1,0:T(8,128)(2,1)S(1)} %collective-permute-done.3.refs_1_, ...), custom_call_target="tpu_custom_call" | custom-call | flops 2147483648 | bytes 1048576 | tf_op jit(solution)/shard_map/cold_sums/pallas_call | solution.py:259
  70.1 0.0 collective-permute-done.1.other_ref
  70.1 1.1 %unpack.1 = f32[2048,128]{1,0:T(8,128)} custom-call(s16[16,72,128]{2,1,0:T(8,128)(2,1)S(1)} %all-to-all-done.1.mine_ref, s16[16,72,128]{2,1,0:T(8,128)(2,1)S(1)} %collective-permute-done.1.other_ref), custom_call_target="tpu_custom_call" | custom-call | flops 1048576 | bytes 1572864 | tf_op jit(solution)/shard_map/unpack/pallas_call | solution.py:213
  (2 shorter events, 0.0 us)
Async XLA Ops:
  0.6 1.6 %copy-start = (bf16[8192,128]{1,0:T(8,128)(2,1)S(1)}, bf16[8192,128]{1,0:T(8,128)(2,1)}, u32[]{:S(2)}) copy-start(bf16[8192,128]{1,0:T(8,128)(2,1)} %data_ref.1) | copy-start | bytes 6291460
  2.2 0.8 %copy-start.2 = (s32[8192]{0:T(1024)S(1)}, s32[8192]{0:T(1024)}, u32[]{:S(2)}) copy-start(s32[8192]{0:T(1024)} %param.5) | copy-start | bytes 98308
  3.0 5.4 %copy-start.3 = (s32[1,1,8,512]{3,2,1,0:T(8,128)S(1)}, s32[1,1,8,512]{3,2,1,0:T(8,128)}, u32[]{:S(2)}) copy-start(s32[1,1,8,512]{3,2,1,0:T(8,128)} %param.8) | copy-start | bytes 49156
  3.0 5.5 %copy-start.4 = (s32[1,1,8]{2,1,0:T(1,128)S(1)}, s32[1,1,8]{2,1,0:T(1,128)}, u32[]{:S(2)}) copy-start(s32[1,1,8]{2,1,0:T(1,128)} %param.9) | copy-start | bytes 100
  7.9 2.1 %collective-permute-start = (f32[1024,128]{1,0:T(8,128)S(1)}, f32[1024,128]{1,0:T(8,128)S(1)}, u32[]{:S(2)}, u32[]{:S(2)}) collective-permute-start(f32[1024,128]{1,0:T(8,128)S(1)} %get-tuple-element.12), channel_id=1, source_target_pairs={{0,8},{8,0},{1,9},{9,1},{2,10},{10,2},{3,11},{11,3},{4,12},{12,4},... | collective-permute-start | bytes 1572872 | tf_op jit(solution)/shard_map/ppermute | solution.py:294
  30.0 28.9 %all-to-all-start.1 = ((s16[16,72,128]{2,1,0:T(8,128)(2,1)}), s16[16,72,128]{2,1,0:T(8,128)(2,1)S(1)}, u32[]{:S(2)}, u32[]{:S(2)}) async-start(s16[16,72,128]{2,1,0:T(8,128)(2,1)} %add.5), calls=%async_computation.1 | async-start | bytes 589824 | tf_op jit(solution)/shard_map/all_to_all | solution.py:301
  34.6 20.1 %collective-permute-start.5 = (bf16[512,128]{1,0:T(8,128)(2,1)S(1)}, bf16[512,128]{1,0:T(8,128)(2,1)S(1)}, u32[]{:S(2)}, u32[]{:S(2)}) collective-permute-start(bf16[512,128]{1,0:T(8,128)(2,1)S(1)} %get-tuple-element.16), channel_id=1, source_target_pairs={{0,4},{1,5},{2,6},{3,7},{4,0},{5,1},{6,2},{7,3},{8,12},{9,13},{10,... | collective-permute-start | bytes 393224 | tf_op jit(solution)/shard_map/ppermute | solution.py:289
  37.4 21.0 %collective-permute-start.6 = (bf16[512,128]{1,0:T(8,128)(2,1)S(1)}, bf16[512,128]{1,0:T(8,128)(2,1)S(1)}, u32[]{:S(2)}, u32[]{:S(2)}) collective-permute-start(bf16[512,128]{1,0:T(8,128)(2,1)S(1)} %get-tuple-element.17), channel_id=1, source_target_pairs={{0,5},{1,4},{2,7},{3,6},{4,1},{5,0},{6,3},{7,2},{8,13},{9,12},{10,... | collective-permute-start | bytes 393224 | tf_op jit(solution)/shard_map/ppermute | solution.py:289
  38.8 27.2 %copy-start.1 = (bf16[1,1,8,512,128]{4,3,2,1,0:T(8,128)(2,1)S(1)}, bf16[1,1,8,512,128]{4,3,2,1,0:T(8,128)(2,1)}, u32[]{:S(2)}) copy-start(bf16[1,1,8,512,128]{4,3,2,1,0:T(8,128)(2,1)} %param.7) | copy-start | bytes 3145732
  38.8 20.1 %collective-permute-start.7 = (bf16[512,128]{1,0:T(8,128)(2,1)S(1)}, bf16[512,128]{1,0:T(8,128)(2,1)S(1)}, u32[]{:S(2)}, u32[]{:S(2)}) collective-permute-start(bf16[512,128]{1,0:T(8,128)(2,1)S(1)} %get-tuple-element.18), channel_id=1, source_target_pairs={{0,6},{1,7},{2,4},{3,5},{4,2},{5,3},{6,0},{7,1},{8,14},{9,15},{10,... | collective-permute-start | bytes 393224 | tf_op jit(solution)/shard_map/ppermute | solution.py:289
  43.2 15.7 %collective-permute-start.2 = (bf16[512,128]{1,0:T(8,128)(2,1)S(1)}, bf16[512,128]{1,0:T(8,128)(2,1)S(1)}, u32[]{:S(2)}, u32[]{:S(2)}) collective-permute-start(bf16[512,128]{1,0:T(8,128)(2,1)S(1)} %get-tuple-element.13), channel_id=1, source_target_pairs={{0,1},{1,0},{2,3},{3,2},{4,5},{5,4},{6,7},{7,6},{8,9},{9,8},{10,11... | collective-permute-start | bytes 393224 | tf_op jit(solution)/shard_map/ppermute | solution.py:289
  43.9 15.0 %collective-permute-start.3 = (bf16[512,128]{1,0:T(8,128)(2,1)S(1)}, bf16[512,128]{1,0:T(8,128)(2,1)S(1)}, u32[]{:S(2)}, u32[]{:S(2)}) collective-permute-start(bf16[512,128]{1,0:T(8,128)(2,1)S(1)} %get-tuple-element.14), channel_id=1, source_target_pairs={{0,2},{1,3},{2,0},{3,1},{4,6},{5,7},{6,4},{7,5},{8,10},{9,11},{10,... | collective-permute-start | bytes 393224 | tf_op jit(solution)/shard_map/ppermute | solution.py:289
  54.7 5.9 %collective-permute-start.4 = (bf16[512,128]{1,0:T(8,128)(2,1)S(1)}, bf16[512,128]{1,0:T(8,128)(2,1)S(1)}, u32[]{:S(2)}, u32[]{:S(2)}) collective-permute-start(bf16[512,128]{1,0:T(8,128)(2,1)S(1)} %get-tuple-element.15), channel_id=1, source_target_pairs={{0,3},{1,2},{2,1},{3,0},{4,7},{5,6},{6,5},{7,4},{8,11},{9,10},{10,... | collective-permute-start | bytes 393224 | tf_op jit(solution)/shard_map/ppermute | solution.py:289
  58.4 7.7 %collective-permute-start.8 = (bf16[512,128]{1,0:T(8,128)(2,1)S(1)}, bf16[512,128]{1,0:T(8,128)(2,1)S(1)}, u32[]{:S(2)}, u32[]{:S(2)}) collective-permute-start(bf16[512,128]{1,0:T(8,128)(2,1)S(1)} %get-tuple-element.19), channel_id=1, source_target_pairs={{0,7},{1,6},{2,5},{3,4},{4,3},{5,2},{6,1},{7,0},{8,15},{9,14},{10,... | collective-permute-start | bytes 393224 | tf_op jit(solution)/shard_map/ppermute | solution.py:289
  58.9 11.2 %collective-permute-start.1 = (s16[16,72,128]{2,1,0:T(8,128)(2,1)S(1)}, s16[16,72,128]{2,1,0:T(8,128)(2,1)S(1)}, u32[]{:S(2)}, u32[]{:S(2)}) collective-permute-start(s16[16,72,128]{2,1,0:T(8,128)(2,1)S(1)} %all-to-all-done.1.mine_ref), channel_id=1, source_target_pairs={{0,8},{8,0},{1,9},{9,1},{2,10},{10,2},{3,11},{11,3},{4,12},{12,4},... | collective-permute-start | bytes 884744 | tf_op jit(solution)/shard_map/ppermute | solution.py:303

commit v4 on v3

--- a/solution.py
+++ b/solution.py
@@ -138,34 +138,71 @@
     return -(-(SCALES + lines) // SUB) * SUB
 
 
-def pack_kernel(mine_ref, got_ref, slots_ref, out_ref):
+def pack_kernel(mine_ref, got_ref, own_ref, *out_refs):
+    owners, rows, _ = out_refs[0].shape
+    rows -= SUB
+    groups = len(out_refs) + 1
+    chip = lax.axis_index("chip")
+    for step, out_ref in enumerate(out_refs, 1):
+        base = partner(chip, step, groups)[1] * (owners * rows)
+        for p in range(owners):
+            here = pl.ds(pl.multiple_of(base + p * rows, SUB), rows)
+            codes, code = encode(mine_ref[here, :] + got_ref[here, :])
+            out_ref[p, :rows, :] = narrow(codes)
+            out_ref[p, rows:, :] = narrow(jnp.concatenate([code, code], axis=0))
+    here = pl.ds(pl.multiple_of(chip * (owners * rows), SUB), owners * rows)
+    own_ref[...] = mine_ref[here, :] + got_ref[here, :]
+
+
+def pack(mine, got, groups, owners):
+    half, width = mine.shape
+    rows = half // (groups * owners)
+    whole = pl.BlockSpec(memory_space=pltpu.VMEM)
+    own, *coded = pl.pallas_call(
+        pack_kernel,
+        in_specs=[whole, whole],
+        out_specs=[whole] * groups,
+        out_shape=[jax.ShapeDtypeStruct((owners * rows, width), jnp.float32)]
+        + [jax.ShapeDtypeStruct((owners, rows + SUB, width), jnp.int16)] * (groups - 1),
+        cost_estimate=pl.CostEstimate(flops=half * width * 8, bytes_accessed=half * width * 10, transcendentals=0),
+        compiler_params=ROOM,
+        name="pack",
+    )(mine, got)
+    return own, coded
+
+
+def join_kernel(own_ref, slots_ref, *refs):
+    got_refs, out_ref = refs[:-1], refs[-1]
     owners, lines, _ = slots_ref.shape
     tail = tail_rows(lines)
-    peers, rows, _ = out_ref.shape
-    rows -= tail
+    rows = out_ref.shape[1] - tail
     spare = tail - SCALES - lines
-    for p in range(peers):
-        here = pl.ds(p * rows, rows)
-        codes, code = encode(mine_ref[here, :] + got_ref[here, :])
+    for p in range(owners):
+        total = own_ref[p * rows : (p + 1) * rows, :]
+        for ref in got_refs:
+            ends = widen(ref[p, rows:, :])
+            total += decode(widen(ref[p, :rows, :]), ends[:SCALES])
+        codes, code = encode(total)
         out_ref[p, :rows, :] = narrow(codes)
-        pieces = [code.astype(jnp.int32), slots_ref[p % owners]]
+        pieces = [code.astype(jnp.int32), slots_ref[p]]
         if spare:
             pieces.append(jnp.zeros((spare, LANES), jnp.int32))
         out_ref[p, rows:, :] = jnp.concatenate(pieces, axis=0).astype(jnp.int16)
 
 
-def pack(mine, got, slots, peers):
-    half, width = mine.shape
-    whole = pl.BlockSpec(memory_space=pltpu.VMEM)
-    return pl.pallas_call(
-        pack_kernel,
-        in_specs=[whole, whole, whole],
+def join(own, slots, got):
+    owners, lines, _ = slots.shape
+    total, width = own.shape
+    whole = pl.BlockSpec(memory_space=pltpu.VMEM)
+    return pl.pallas_call(
+        join_kernel,
+        in_specs=[whole] * (2 + len(got)),
         out_specs=whole,
-        out_shape=jax.ShapeDtypeStruct((peers, half // peers + tail_rows(slots.shape[1]), width), jnp.int16),
-        cost_estimate=pl.CostEstimate(flops=half * width * 8, bytes_accessed=half * width * 10, transcendentals=0),
-        compiler_params=ROOM,
-        name="pack",
-    )(mine, got, slots)
+        out_shape=jax.ShapeDtypeStruct((owners, total // owners + tail_rows(lines), width), jnp.int16),
+        cost_estimate=pl.CostEstimate(flops=total * width * 8, bytes_accessed=total * width * 10, transcendentals=0),
+        compiler_params=ROOM,
+        name="join",
+    )(own, slots, *got)
 
 
 def add_kernel(got_ref, out_ref, *, factor, tail):
@@ -177,19 +214,19 @@
         total += decode(widen(got_ref[p, :rows, :]), ends[:SCALES])
     codes, code = encode(total * factor)
     body, ends = narrow(codes), narrow(jnp.concatenate([code, code], axis=0))
-    for p in range(peers):
+    for p in range(out_ref.shape[0]):
         out_ref[p, :rows, :] = body
         out_ref[p, rows:, :] = ends
 
 
-def add(got, factor, tail):
-    peers, rows, width = got.shape
+def add(got, factor, tail, copies):
+    _, rows, width = got.shape
     whole = pl.BlockSpec(memory_space=pltpu.VMEM)
     return pl.pallas_call(
         functools.partial(add_kernel, factor=factor, tail=tail),
         in_specs=[whole],
         out_specs=whole,
-        out_shape=jax.ShapeDtypeStruct((peers, rows - tail + SUB, width), jnp.int16),
+        out_shape=jax.ShapeDtypeStruct((copies, rows - tail + SUB, width), jnp.int16),
         cost_estimate=pl.CostEstimate(flops=got.size * 8, bytes_accessed=got.size * 4, transcendentals=0),
         compiler_params=ROOM,
         name="add",
@@ -229,18 +266,18 @@
 
 def cold_steps(owners):
     far, near = list(range(owners // 2, owners)), list(range(1, owners // 2))
-    early = len(far) * 3 // 4
-    return far[:early], far[early:] + near
+    a, b, c, n = len(far) // 4, len(far) // 2, len(far) * 3 // 4, len(near) * 2 // 3
+    return far[:a], far[a:b], far[b:c] + near[:n], far[c:] + near[n:]
 
 
 def cold_kernel(got_ref, own_ref, *refs, block, at, lines):
     moved, (out_ref, rhs_ref, row_ref) = refs[:-3], refs[-3:]
     owners, capacity, width = own_ref.shape
     half = out_ref.shape[0] // 2
-    chip, owner = lax.axis_index("chip"), lax.axis_index("gy")
+    owner = lax.axis_index("gy")
     for step, ref in enumerate((own_ref.at[owner], *moved)):
         source, _ = partner(owner, step, owners)
-        slots = got_ref[chip * owners + source, at:, :].astype(jnp.int32)[SCALES : SCALES + lines]
+        slots = got_ref[source, at:, :].astype(jnp.int32)[SCALES : SCALES + lines]
         high = (slots >= half).astype(jnp.int32)
         masked_halves((high == 0).astype(jnp.float32), ref, rhs_ref, step * capacity, width)
         row_ref[pl.ds(step * lines, lines), :] = slots - high * half
@@ -283,21 +320,32 @@
     blocks = cold_grads.reshape(owners, capacity, width)
     moved = {}
 
-    def move(steps):
-        picked = pick(blocks, steps)
-        for n, block in zip(steps, picked):
-            moved[n] = lax.ppermute(block, "gy", [(i, partner(i, n, owners)[1]) for i in range(owners)])
-
-    early, late = cold_steps(owners)
-    move(early)
+    def take(steps):
+        if not steps:
+            return {}
+        return dict(zip(steps, pick(blocks, steps)))
+
+    def move(picked, steps):
+        for n in steps:
+            moved[n] = lax.ppermute(picked[n], "gy", [(i, partner(i, n, owners)[1]) for i in range(owners)])
+
+    early, middle, third, late = cold_steps(owners)
+    picked = take(early + middle)
+    move(picked, early)
     mine, send = hot_sums(hot_ids, hot_grads, HOT)
     got = lax.ppermute(send, "core", swap)
+    move(picked, middle)
     places = lax.broadcasted_iota(jnp.int32, (owners, capacity), 1)
     used = jnp.where(places < cold_counts.reshape(owners, 1), cold_slots.reshape(owners, capacity), -1)
-    packed = pack(mine, got, used.reshape(owners, lines, LANES), peers)
-    parts = lax.all_to_all(packed, everyone, split_axis=0, concat_axis=0, tiled=True)
-    move(late)
-    summed = add(parts, factor, tail_rows(lines))
+    own, coded = pack(mine, got, groups, owners)
+    crossed = []
+    for n, block in enumerate(coded, 1):
+        crossed.append(lax.ppermute(block, "chip", [(i, partner(i, n, groups)[1]) for i in range(groups)]))
+    move(take(third), third)
+    joined = join(own, used.reshape(owners, lines, LANES), crossed)
+    parts = lax.all_to_all(joined, "gy", split_axis=0, concat_axis=0, tiled=True)
+    move(take(late), late)
+    summed = add(parts, factor, tail_rows(lines), peers)
     all_rows = lax.all_to_all(summed, everyone, split_axis=0, concat_axis=0, tiled=True)
     cold_grad = cold_sums(parts, blocks, [moved[n] for n in range(1, owners)], OWN_ROWS)
     others = lax.ppermute(all_rows, "core", swap)

time: 71.6 us -> 63.6 us (0.89)
  blocking collectives: 19 us -> 0 us
  starting transfers between devices: 12.8 us -> 26.4 us
  waiting for transfers between devices: 23.1 us -> 18.8 us
  Pallas kernels: 13.2 us -> 14.7 us
    all_to_all x1 -> x0, blocking collectives: 19 us -> none  [per_device(): lax.all_to_all(packed, everyone, split_axis=0, concat_axis=0, tiled=True)]
    ppermute x7 -> x8, waiting for transfers between devices: 21.6 us -> 9.97 us  [the longest x7 5.89 us: move(): lax.ppermute(picked[n], 'gy', [(i, partner(i, n, owners)[1]) for i in ran...]
    all_to_all x0 -> x1, waiting for transfers between devices: none -> 7.36 us  [per_device(): lax.all_to_all(joined, 'gy', split_axis=0, concat_axis=0, tiled=True)]
    ppermute x7 -> x8, starting transfers between devices: 8.66 us -> 15.7 us  [the longest x7 12.8 us: move(): lax.ppermute(picked[n], 'gy', [(i, partner(i, n, owners)[1]) for i in ran...]
    all_to_all x0 -> x1, starting transfers between devices: none -> 6.08 us  [per_device(): lax.all_to_all(joined, 'gy', split_axis=0, concat_axis=0, tiled=True)]
    pallas_call x2 -> x3, Pallas kernels: 2.19 us -> 3.03 us  [pick(): pl.pallas_call(functools.partial(pick_kernel, steps=steps), in_specs=[pl....]
    pallas_call x1 -> x2, Pallas kernels: 0.14 us -> 0.88 us  [the longest x1 0.77 us: join(): pl.pallas_call(join_kernel, in_specs=[whole] * (2 + len(got)), out_specs=...]
  transfers between devices with their start and end apart: 10 -> 12, of which waited for: 5 -> 6; matrix products, arithmetic and copies ran while one was open for 0% -> 0% of each run, Pallas kernels for 9% -> 12%
where the time goes in v4:
time: 63.6 us; the launch traced here: 63.2 us
  starting transfers between devices  26.4 us (42%)
  waiting for transfers between devices  18.8 us (30%)
  Pallas kernels  14.7 us (23%)
  local copies, waits for them, and re-layouts  2.36 us (4%)
  between operations  0.71 us (1%)
    ppermute x7, starting transfers between devices, move(): lax.ppermute(picked[n], 'gy', [(i, partner(i, n, owners)[1]) for i in ran...  12.8 us
    all_to_all x1, waiting for transfers between devices, per_device(): lax.all_to_all(joined, 'gy', split_axis=0, concat_axis=0, tiled=True)  7.36 us
    all_to_all x1, starting transfers between devices, per_device(): lax.all_to_all(joined, 'gy', split_axis=0, concat_axis=0, tiled=True)  6.08 us
    ppermute x7, waiting for transfers between devices, move(): lax.ppermute(picked[n], 'gy', [(i, partner(i, n, owners)[1]) for i in ran...  5.89 us
    pallas_call x1, Pallas kernels, hot_sums(): pl.pallas_call(functools.partial(hot_kernel, block=math.gcd(half, 256), s...  4.86 us
    all_to_all x1, starting transfers between devices, per_device(): lax.all_to_all(summed, everyone, split_axis=0, concat_axis=0, tiled=True)  4.14 us
    ppermute x1, waiting for transfers between devices, per_device(): lax.ppermute(block, 'chip', [(i, partner(i, n, groups)[1]) for i in range...  4.07 us
    pallas_call x1, Pallas kernels, cold_sums(): pl.pallas_call(functools.partial(cold_kernel, block=math.gcd(table // 2,...  4.03 us
  transfers between devices with their start and end apart: 12, of which 6 were waited for; matrix products, arithmetic and copies ran while one was open for 0% of the time, Pallas kernels for 12%

profile of v4, /device:TPU:0, one launch (start us, length us, event | category | flops | bytes accessed | tf_op | source)
XLA Modules:
  0.0 63.2 jit_solution(5364487569525840961)
XLA Ops:
  0.6 0.0 copy-start
  0.6 1.6 %copy-done = bf16[8192,128]{1,0:T(8,128)(2,1)S(1)} copy-done((bf16[8192,128]{1,0:T(8,128)(2,1)S(1)}, bf16[8192,128]{1,0:T(8,128)(2,1)}, u32[]{:S(2)}) %copy-start) | copy-done | bytes 2097176
  2.2 0.0 copy-start.2
  2.2 0.8 %copy-done.2 = s32[8192]{0:T(1024)S(1)} copy-done((s32[8192]{0:T(1024)S(1)}, s32[8192]{0:T(1024)}, u32[]{:S(2)}) %copy-start.2) | copy-done | bytes 32792
  3.0 0.0 copy-start.3
  3.0 0.0 copy-start.4
  3.0 4.9 %hot_sums.1 = (f32[1024,128]{1,0:T(8,128)S(1)}, f32[1024,128]{1,0:T(8,128)S(1)}) custom-call(s32[64,128]{1,0:T(8,128)S(1)} %bitcast.10, bf16[8192,128]{1,0:T(8,128)(2,1)S(1)} %copy-done), custom_call_target="tpu_custom_call" | custom-call | flops 4294967296 | bytes 2097152 | tf_op jit(solution)/shard_map/hot_sums/pallas_call | solution.py:72
  7.9 0.6 collective-permute-start
  8.4 0.0 copy-done.3
  8.4 1.5 %collective-permute-done.got_ref = f32[1024,128]{1,0:T(8,128)S(1)} collective-permute-done((f32[1024,128]{1,0:T(8,128)S(1)}, f32[1024,128]{1,0:T(8,128)S(1)}, u32[]{:S(2)}, u32[]{:S(2)}) %collective-permute-start) | collective-permute-done | bytes 524320 | tf_op jit(solution)/shard_map/ppermute | solution.py:336
  10.0 0.1 pack.1
  10.1 2.9 %collective-permute-start.1 = (s16[8,72,128]{2,1,0:T(8,128)(2,1)S(1)}, s16[8,72,128]{2,1,0:T(8,128)(2,1)S(1)}, u32[]{:S(2)}, u32[]{:S(2)}) collective-permute-start(s16[8,72,128]{2,1,0:T(8,128)(2,1)S(1)} %get-tuple-element.16), channel_id=1, source_target_pairs={{0,16},{16,0},{1,17},{17,1},{2,18},{18,2},{3,19},{19,3},{4,20},{20... | collective-permute-start | bytes 442376 | tf_op jit(solution)/shard_map/ppermute | solution.py:343
  13.0 0.0 copy-done.4
  13.0 0.1 compare_select_fusion.slots_ref
  13.0 4.1 %collective-permute-done.1.refs_0_ = s16[8,72,128]{2,1,0:T(8,128)(2,1)S(1)} collective-permute-done((s16[8,72,128]{2,1,0:T(8,128)(2,1)S(1)}, s16[8,72,128]{2,1,0:T(8,128)(2,1)S(1)}, u32[]{:S(2)}, u32[]{:S(2)}) %collective-permute-start.1) | collective-permute-done | bytes 147488 | tf_op jit(solution)/shard_map/ppermute | solution.py:343
  17.1 0.8 %join.1 = s16[8,72,128]{2,1,0:T(8,128)(2,1)} custom-call(f32[512,128]{1,0:T(8,128)S(1)} %get-tuple-element.15.own_ref, s32[8,4,128]{2,1,0:T(4,128)S(1)} %compare_select_fusion.slots_ref, s16[8,72,128]{2,1,0:T(8,128)(2,1)S(1)} %collective-permute-done.1.refs_0_), custom_call_target="tpu_custom_call" | custom-call | flops 524288 | bytes 655360 | tf_op jit(solution)/shard_map/join/pallas_call | solution.py:197
  17.9 6.1 %all-to-all-start = ((s16[8,72,128]{2,1,0:T(8,128)(2,1)}), s16[8,72,128]{2,1,0:T(8,128)(2,1)S(1)}, u32[]{:S(2)}, u32[]{:S(2)}) async-start(s16[8,72,128]{2,1,0:T(8,128)(2,1)} %join.1), calls=%async_computation | async-start | bytes 294912 | tf_op jit(solution)/shard_map/all_to_all | solution.py:346
  24.0 1.0 %pick.5 = (bf16[512,128]{1,0:T(8,128)(2,1)S(1)}, bf16[512,128]{1,0:T(8,128)(2,1)S(1)}) custom-call(bf16[8,512,128]{2,1,0:T(8,128)(2,1)} %bitcast.6), custom_call_target="tpu_custom_call" | custom-call | flops 5000000000 | bytes 262144 | tf_op jit(solution)/shard_map/pick/pallas_call | solution.py:99
  25.0 3.0 %collective-permute-start.6 = (bf16[512,128]{1,0:T(8,128)(2,1)S(1)}, bf16[512,128]{1,0:T(8,128)(2,1)S(1)}, u32[]{:S(2)}, u32[]{:S(2)}) collective-permute-start(bf16[512,128]{1,0:T(8,128)(2,1)S(1)} %get-tuple-element.20), channel_id=1, source_target_pairs={{0,4},{1,5},{2,6},{3,7},{4,0},{5,1},{6,2},{7,3},{8,12},{9,13},{10,... | collective-permute-start | bytes 393224 | tf_op jit(solution)/shard_map/ppermute | solution.py:330
  28.0 1.5 %collective-permute-start.7 = (bf16[512,128]{1,0:T(8,128)(2,1)S(1)}, bf16[512,128]{1,0:T(8,128)(2,1)S(1)}, u32[]{:S(2)}, u32[]{:S(2)}) collective-permute-start(bf16[512,128]{1,0:T(8,128)(2,1)S(1)} %get-tuple-element.21), channel_id=1, source_target_pairs={{0,5},{1,4},{2,7},{3,6},{4,1},{5,0},{6,3},{7,2},{8,13},{9,12},{10,... | collective-permute-start | bytes 393224 | tf_op jit(solution)/shard_map/ppermute | solution.py:330
  29.4 7.4 %all-to-all-done.got_ref = s16[8,72,128]{2,1,0:T(8,128)(2,1)S(1)} async-done(((s16[8,72,128]{2,1,0:T(8,128)(2,1)}), s16[8,72,128]{2,1,0:T(8,128)(2,1)S(1)}, u32[]{:S(2)}, u32[]{:S(2)}) %all-to-all-start) | async-done | bytes 147488 | tf_op jit(solution)/shard_map/all_to_all | solution.py:346
  36.8 0.8 %add.5 = s16[16,72,128]{2,1,0:T(8,128)(2,1)} custom-call(s16[8,72,128]{2,1,0:T(8,128)(2,1)S(1)} %all-to-all-done.got_ref), custom_call_target="tpu_custom_call" | custom-call | flops 589824 | bytes 294912 | tf_op jit(solution)/shard_map/add/pallas_call | solution.py:225
  37.6 4.1 %all-to-all-start.1 = ((s16[16,72,128]{2,1,0:T(8,128)(2,1)}), s16[16,72,128]{2,1,0:T(8,128)(2,1)S(1)}, u32[]{:S(2)}, u32[]{:S(2)}) async-start(s16[16,72,128]{2,1,0:T(8,128)(2,1)} %add.5), calls=%async_computation.1 | async-start | bytes 589824 | tf_op jit(solution)/shard_map/all_to_all | solution.py:349
  41.8 1.0 %pick.4 = (bf16[512,128]{1,0:T(8,128)(2,1)S(1)}, bf16[512,128]{1,0:T(8,128)(2,1)S(1)}) custom-call(bf16[8,512,128]{2,1,0:T(8,128)(2,1)} %bitcast.7), custom_call_target="tpu_custom_call" | custom-call | flops 5000000000 | bytes 262144 | tf_op jit(solution)/shard_map/pick/pallas_call | solution.py:99
  42.8 2.9 %collective-permute-start.5 = (bf16[512,128]{1,0:T(8,128)(2,1)S(1)}, bf16[512,128]{1,0:T(8,128)(2,1)S(1)}, u32[]{:S(2)}, u32[]{:S(2)}) collective-permute-start(bf16[512,128]{1,0:T(8,128)(2,1)S(1)} %get-tuple-element.19), channel_id=1, source_target_pairs={{0,3},{1,2},{2,1},{3,0},{4,7},{5,6},{6,5},{7,4},{8,11},{9,10},{10,... | collective-permute-start | bytes 393224 | tf_op jit(solution)/shard_map/ppermute | solution.py:330
  45.6 0.0 copy-start.1
  45.6 2.4 %collective-permute-start.9 = (bf16[512,128]{1,0:T(8,128)(2,1)S(1)}, bf16[512,128]{1,0:T(8,128)(2,1)S(1)}, u32[]{:S(2)}, u32[]{:S(2)}) collective-permute-start(bf16[512,128]{1,0:T(8,128)(2,1)S(1)} %get-tuple-element.23), channel_id=1, source_target_pairs={{0,7},{1,6},{2,5},{3,4},{4,3},{5,2},{6,1},{7,0},{8,15},{9,14},{10,... | collective-permute-start | bytes 393224 | tf_op jit(solution)/shard_map/ppermute | solution.py:330
  48.0 1.1 %pick.3 = (bf16[512,128]{1,0:T(8,128)(2,1)S(1)}, bf16[512,128]{1,0:T(8,128)(2,1)S(1)}, bf16[512,128]{1,0:T(8,128)(2,1)S(1)}) custom-call(bf16[8,512,128]{2,1,0:T(8,128)(2,1)} %bitcast.8), custom_call_target="tpu_custom_call" | custom-call | flops 5000000000 | bytes 393216 | tf_op jit(solution)/shard_map/pick/pallas_call | solution.py:99
  49.1 1.5 %collective-permute-start.3 = (bf16[512,128]{1,0:T(8,128)(2,1)S(1)}, bf16[512,128]{1,0:T(8,128)(2,1)S(1)}, u32[]{:S(2)}, u32[]{:S(2)}) collective-permute-start(bf16[512,128]{1,0:T(8,128)(2,1)S(1)} %get-tuple-element.17), channel_id=1, source_target_pairs={{0,1},{1,0},{2,3},{3,2},{4,5},{5,4},{6,7},{7,6},{8,9},{9,8},{10,11... | collective-permute-start | bytes 393224 | tf_op jit(solution)/shard_map/ppermute | solution.py:330
  50.6 0.0 collective-permute-done.6.refs_3_
  50.6 0.6 collective-permute-start.4
  51.2 0.0 collective-permute-done.7.refs_4_
  51.2 1.0 %collective-permute-start.8 = (bf16[512,128]{1,0:T(8,128)(2,1)S(1)}, bf16[512,128]{1,0:T(8,128)(2,1)S(1)}, u32[]{:S(2)}, u32[]{:S(2)}) collective-permute-start(bf16[512,128]{1,0:T(8,128)(2,1)S(1)} %get-tuple-element.22), channel_id=1, source_target_pairs={{0,6},{1,7},{2,4},{3,5},{4,2},{5,3},{6,0},{7,1},{8,14},{9,15},{10,... | collective-permute-start | bytes 393224 | tf_op jit(solution)/shard_map/ppermute | solution.py:330
  52.1 3.3 %collective-permute-done.5.refs_2_ = bf16[512,128]{1,0:T(8,128)(2,1)S(1)} collective-permute-done((bf16[512,128]{1,0:T(8,128)(2,1)S(1)}, bf16[512,128]{1,0:T(8,128)(2,1)S(1)}, u32[]{:S(2)}, u32[]{:S(2)}) %collective-permute-start.5) | collective-permute-done | bytes 131104 | tf_op jit(solution)/shard_map/ppermute | solution.py:330
  55.5 0.0 all-to-all-done.1.mine_ref
  55.5 0.0 collective-permute-start.2
  55.5 0.0 collective-permute-done.9.refs_6_
  55.5 0.9 %collective-permute-done.3.refs_0_ = bf16[512,128]{1,0:T(8,128)(2,1)S(1)} collective-permute-done((bf16[512,128]{1,0:T(8,128)(2,1)S(1)}, bf16[512,128]{1,0:T(8,128)(2,1)S(1)}, u32[]{:S(2)}, u32[]{:S(2)}) %collective-permute-start.3) | collective-permute-done | bytes 131104 | tf_op jit(solution)/shard_map/ppermute | solution.py:330
  56.4 0.0 collective-permute-done.4.refs_1_
  56.4 1.7 %collective-permute-done.8.refs_5_ = bf16[512,128]{1,0:T(8,128)(2,1)S(1)} collective-permute-done((bf16[512,128]{1,0:T(8,128)(2,1)S(1)}, bf16[512,128]{1,0:T(8,128)(2,1)S(1)}, u32[]{:S(2)}, u32[]{:S(2)}) %collective-permute-start.8) | collective-permute-done | bytes 131104 | tf_op jit(solution)/shard_map/ppermute | solution.py:330
  58.0 0.0 copy-done.1
  58.0 4.0 %cold_sums.1 = f32[2048,128]{1,0:T(8,128)} custom-call(s16[8,72,128]{2,1,0:T(8,128)(2,1)S(1)} %all-to-all-done.got_ref, bf16[8,512,128]{2,1,0:T(8,128)(2,1)S(1)} %bitcast.9, bf16[512,128]{1,0:T(8,128)(2,1)S(1)} %collective-permute-done.3.refs_0_, bf16[512,128]{1,0:T(8,128)(2,1)S(1)} %collective-permute-done.4.refs_1_, ...), custom_call_target="tpu_custom_call" | custom-call | flops 2147483648 | bytes 1048576 | tf_op jit(solution)/shard_map/cold_sums/pallas_call | solution.py:296
  62.1 0.0 collective-permute-done.2.other_ref
  62.1 1.1 %unpack.1 = f32[2048,128]{1,0:T(8,128)} custom-call(s16[16,72,128]{2,1,0:T(8,128)(2,1)S(1)} %all-to-all-done.1.mine_ref, s16[16,72,128]{2,1,0:T(8,128)(2,1)S(1)} %collective-permute-done.2.other_ref), custom_call_target="tpu_custom_call" | custom-call | flops 1048576 | bytes 1572864 | tf_op jit(solution)/shard_map/unpack/pallas_call | solution.py:250
  (2 shorter events, 0.0 us)
Async XLA Ops:
  0.6 1.6 %copy-start = (bf16[8192,128]{1,0:T(8,128)(2,1)S(1)}, bf16[8192,128]{1,0:T(8,128)(2,1)}, u32[]{:S(2)}) copy-start(bf16[8192,128]{1,0:T(8,128)(2,1)} %data_ref.1) | copy-start | bytes 6291460
  2.2 0.8 %copy-start.2 = (s32[8192]{0:T(1024)S(1)}, s32[8192]{0:T(1024)}, u32[]{:S(2)}) copy-start(s32[8192]{0:T(1024)} %param.5) | copy-start | bytes 98308
  3.0 5.4 %copy-start.3 = (s32[1,1,8,512]{3,2,1,0:T(8,128)S(1)}, s32[1,1,8,512]{3,2,1,0:T(8,128)}, u32[]{:S(2)}) copy-start(s32[1,1,8,512]{3,2,1,0:T(8,128)} %param.8) | copy-start | bytes 49156
  3.0 10.0 %copy-start.4 = (s32[1,1,8]{2,1,0:T(1,128)S(1)}, s32[1,1,8]{2,1,0:T(1,128)}, u32[]{:S(2)}) copy-start(s32[1,1,8]{2,1,0:T(1,128)} %param.9) | copy-start | bytes 100
  7.9 2.1 %collective-permute-start = (f32[1024,128]{1,0:T(8,128)S(1)}, f32[1024,128]{1,0:T(8,128)S(1)}, u32[]{:S(2)}, u32[]{:S(2)}) collective-permute-start(f32[1024,128]{1,0:T(8,128)S(1)} %get-tuple-element.14), channel_id=1, source_target_pairs={{0,8},{8,0},{1,9},{9,1},{2,10},{10,2},{3,11},{11,3},{4,12},{12,4},... | collective-permute-start | bytes 1572872 | tf_op jit(solution)/shard_map/ppermute | solution.py:336
  10.1 7.1 %collective-permute-start.1 = (s16[8,72,128]{2,1,0:T(8,128)(2,1)S(1)}, s16[8,72,128]{2,1,0:T(8,128)(2,1)S(1)}, u32[]{:S(2)}, u32[]{:S(2)}) collective-permute-start(s16[8,72,128]{2,1,0:T(8,128)(2,1)S(1)} %get-tuple-element.16), channel_id=1, source_target_pairs={{0,16},{16,0},{1,17},{17,1},{2,18},{18,2},{3,19},{19,3},{4,20},{20... | collective-permute-start | bytes 442376 | tf_op jit(solution)/shard_map/ppermute | solution.py:343
  17.9 18.9 %all-to-all-start = ((s16[8,72,128]{2,1,0:T(8,128)(2,1)}), s16[8,72,128]{2,1,0:T(8,128)(2,1)S(1)}, u32[]{:S(2)}, u32[]{:S(2)}) async-start(s16[8,72,128]{2,1,0:T(8,128)(2,1)} %join.1), calls=%async_computation | async-start | bytes 294912 | tf_op jit(solution)/shard_map/all_to_all | solution.py:346
  25.0 25.6 %collective-permute-start.6 = (bf16[512,128]{1,0:T(8,128)(2,1)S(1)}, bf16[512,128]{1,0:T(8,128)(2,1)S(1)}, u32[]{:S(2)}, u32[]{:S(2)}) collective-permute-start(bf16[512,128]{1,0:T(8,128)(2,1)S(1)} %get-tuple-element.20), channel_id=1, source_target_pairs={{0,4},{1,5},{2,6},{3,7},{4,0},{5,1},{6,2},{7,3},{8,12},{9,13},{10,... | collective-permute-start | bytes 393224 | tf_op jit(solution)/shard_map/ppermute | solution.py:330
  28.0 23.2 %collective-permute-start.7 = (bf16[512,128]{1,0:T(8,128)(2,1)S(1)}, bf16[512,128]{1,0:T(8,128)(2,1)S(1)}, u32[]{:S(2)}, u32[]{:S(2)}) collective-permute-start(bf16[512,128]{1,0:T(8,128)(2,1)S(1)} %get-tuple-element.21), channel_id=1, source_target_pairs={{0,5},{1,4},{2,7},{3,6},{4,1},{5,0},{6,3},{7,2},{8,13},{9,12},{10,... | collective-permute-start | bytes 393224 | tf_op jit(solution)/shard_map/ppermute | solution.py:330
  37.6 17.9 %all-to-all-start.1 = ((s16[16,72,128]{2,1,0:T(8,128)(2,1)}), s16[16,72,128]{2,1,0:T(8,128)(2,1)S(1)}, u32[]{:S(2)}, u32[]{:S(2)}) async-start(s16[16,72,128]{2,1,0:T(8,128)(2,1)} %add.5), calls=%async_computation.1 | async-start | bytes 589824 | tf_op jit(solution)/shard_map/all_to_all | solution.py:349
  42.8 12.7 %collective-permute-start.5 = (bf16[512,128]{1,0:T(8,128)(2,1)S(1)}, bf16[512,128]{1,0:T(8,128)(2,1)S(1)}, u32[]{:S(2)}, u32[]{:S(2)}) collective-permute-start(bf16[512,128]{1,0:T(8,128)(2,1)S(1)} %get-tuple-element.19), channel_id=1, source_target_pairs={{0,3},{1,2},{2,1},{3,0},{4,7},{5,6},{6,5},{7,4},{8,11},{9,10},{10,... | collective-permute-start | bytes 393224 | tf_op jit(solution)/shard_map/ppermute | solution.py:330
  45.6 12.4 %copy-start.1 = (bf16[1,1,8,512,128]{4,3,2,1,0:T(8,128)(2,1)S(1)}, bf16[1,1,8,512,128]{4,3,2,1,0:T(8,128)(2,1)}, u32[]{:S(2)}) copy-start(bf16[1,1,8,512,128]{4,3,2,1,0:T(8,128)(2,1)} %param.7) | copy-start | bytes 3145732
  45.6 9.8 %collective-permute-start.9 = (bf16[512,128]{1,0:T(8,128)(2,1)S(1)}, bf16[512,128]{1,0:T(8,128)(2,1)S(1)}, u32[]{:S(2)}, u32[]{:S(2)}) collective-permute-start(bf16[512,128]{1,0:T(8,128)(2,1)S(1)} %get-tuple-element.23), channel_id=1, source_target_pairs={{0,7},{1,6},{2,5},{3,4},{4,3},{5,2},{6,1},{7,0},{8,15},{9,14},{10,... | collective-permute-start | bytes 393224 | tf_op jit(solution)/shard_map/ppermute | solution.py:330
  49.1 7.3 %collective-permute-start.3 = (bf16[512,128]{1,0:T(8,128)(2,1)S(1)}, bf16[512,128]{1,0:T(8,128)(2,1)S(1)}, u32[]{:S(2)}, u32[]{:S(2)}) collective-permute-start(bf16[512,128]{1,0:T(8,128)(2,1)S(1)} %get-tuple-element.17), channel_id=1, source_target_pairs={{0,1},{1,0},{2,3},{3,2},{4,5},{5,4},{6,7},{7,6},{8,9},{9,8},{10,11... | collective-permute-start | bytes 393224 | tf_op jit(solution)/shard_map/ppermute | solution.py:330
  50.6 5.8 %collective-permute-start.4 = (bf16[512,128]{1,0:T(8,128)(2,1)S(1)}, bf16[512,128]{1,0:T(8,128)(2,1)S(1)}, u32[]{:S(2)}, u32[]{:S(2)}) collective-permute-start(bf16[512,128]{1,0:T(8,128)(2,1)S(1)} %get-tuple-element.18), channel_id=1, source_target_pairs={{0,2},{1,3},{2,0},{3,1},{4,6},{5,7},{6,4},{7,5},{8,10},{9,11},{10,... | collective-permute-start | bytes 393224 | tf_op jit(solution)/shard_map/ppermute | solution.py:330
  51.2 6.9 %collective-permute-start.8 = (bf16[512,128]{1,0:T(8,128)(2,1)S(1)}, bf16[512,128]{1,0:T(8,128)(2,1)S(1)}, u32[]{:S(2)}, u32[]{:S(2)}) collective-permute-start(bf16[512,128]{1,0:T(8,128)(2,1)S(1)} %get-tuple-element.22), channel_id=1, source_target_pairs={{0,6},{1,7},{2,4},{3,5},{4,2},{5,3},{6,0},{7,1},{8,14},{9,15},{10,... | collective-permute-start | bytes 393224 | tf_op jit(solution)/shard_map/ppermute | solution.py:330
  55.5 6.6 %collective-permute-start.2 = (s16[16,72,128]{2,1,0:T(8,128)(2,1)S(1)}, s16[16,72,128]{2,1,0:T(8,128)(2,1)S(1)}, u32[]{:S(2)}, u32[]{:S(2)}) collective-permute-start(s16[16,72,128]{2,1,0:T(8,128)(2,1)S(1)} %all-to-all-done.1.mine_ref), channel_id=1, source_target_pairs={{0,8},{8,0},{1,9},{9,1},{2,10},{10,2},{3,11},{11,3},{4,12},{12,4},... | collective-permute-start | bytes 884744 | tf_op jit(solution)/shard_map/ppermute | solution.py:351

commit v5 on v4

--- a/solution.py
+++ b/solution.py
@@ -25,12 +25,12 @@
     return pltpu.with_memory_space_constraint(array, pltpu.HBM)
 
 
-def masked_halves(keep, data_ref, rhs_ref, base, width):
+def masked_halves(keep, data_refs, rhs_ref, base, width):
     flags = keep.T
     for j in range(keep.shape[0]):
         rows = pl.ds(base + j * LANES, LANES)
         column = jnp.broadcast_to(flags[:, j : j + 1], (LANES, width)).astype(jnp.bfloat16)
-        data = data_ref[pl.ds(j * LANES, LANES), :]
+        data = sum(ref[pl.ds(j * LANES, LANES), :] for ref in data_refs)
         kept = data * column
         rhs_ref[rows, :width] = kept
         rhs_ref[rows, width:] = data - kept
@@ -50,7 +50,7 @@
     for first in range(0, data_ref.shape[0], step):
         ids = ids_ref[pl.ds(first // LANES, lines), :]
         high = (ids >= half).astype(jnp.int32)
-        masked_halves((high == core).astype(jnp.float32), data_ref.at[pl.ds(first, step)], rhs_ref, 0, width)
+        masked_halves((high == core).astype(jnp.float32), [data_ref.at[pl.ds(first, step)]], rhs_ref, 0, width)
         row = (ids - high * half).astype(jnp.int16)
         rhs = rhs_ref[...]
         for start in range(0, half, block):
@@ -264,22 +264,23 @@
     return me ^ step, me ^ step
 
 
-def cold_steps(owners):
+def cold_lots(owners):
     far, near = list(range(owners // 2, owners)), list(range(1, owners // 2))
-    a, b, c, n = len(far) // 4, len(far) // 2, len(far) * 3 // 4, len(near) * 2 // 3
-    return far[:a], far[a:b], far[b:c] + near[:n], far[c:] + near[n:]
-
-
-def cold_kernel(got_ref, own_ref, *refs, block, at, lines):
+    a, b, c = len(far) // 4, len(far) // 2, len(far) * 3 // 4
+    return far[:a], far[a:b], far[b:c], near + far[c:]
+
+
+def cold_kernel(got_ref, own_ref, *refs, block, at, lines, steps):
     moved, (out_ref, rhs_ref, row_ref) = refs[:-3], refs[-3:]
     owners, capacity, width = own_ref.shape
     half = out_ref.shape[0] // 2
     owner = lax.axis_index("gy")
-    for step, ref in enumerate((own_ref.at[owner], *moved)):
+    for step in range(owners):
+        blocks = [ref for ref, n in zip(moved, steps) if n == step] or [own_ref.at[owner]]
         source, _ = partner(owner, step, owners)
         slots = got_ref[source, at:, :].astype(jnp.int32)[SCALES : SCALES + lines]
         high = (slots >= half).astype(jnp.int32)
-        masked_halves((high == 0).astype(jnp.float32), ref, rhs_ref, step * capacity, width)
+        masked_halves((high == 0).astype(jnp.float32), blocks, rhs_ref, step * capacity, width)
         row_ref[pl.ds(step * lines, lines), :] = slots - high * half
     row = row_ref[...].astype(jnp.int16)
     rhs = rhs_ref[...]
@@ -289,12 +290,14 @@
         out_ref[pl.ds(half + start, block), :] = part[:, width:]
 
 
-def cold_sums(got, own, moved, table):
+def cold_sums(got, own, moved, steps, table):
     owners, capacity, width = own.shape
     lines = capacity // LANES
     whole = pl.BlockSpec(memory_space=pltpu.VMEM)
     return pl.pallas_call(
-        functools.partial(cold_kernel, block=math.gcd(table // 2, 256), at=got.shape[1] - tail_rows(lines), lines=lines),
+        functools.partial(
+            cold_kernel, block=math.gcd(table // 2, 256), at=got.shape[1] - tail_rows(lines), lines=lines, steps=steps
+        ),
         in_specs=[whole] * (2 + len(moved)),
         out_specs=whole,
         out_shape=jax.ShapeDtypeStruct((table, width), jnp.float32),
@@ -318,36 +321,38 @@
     capacity, width = cold_grads.shape[3:]
     lines = capacity // LANES
     blocks = cold_grads.reshape(owners, capacity, width)
-    moved = {}
-
-    def take(steps):
-        if not steps:
-            return {}
-        return dict(zip(steps, pick(blocks, steps)))
-
-    def move(picked, steps):
-        for n in steps:
-            moved[n] = lax.ppermute(picked[n], "gy", [(i, partner(i, n, owners)[1]) for i in range(owners)])
-
-    early, middle, third, late = cold_steps(owners)
-    picked = take(early + middle)
-    move(picked, early)
+    picked, moved = {}, []
+
+    def take(*lots):
+        steps = sorted({n for lot in lots for n in lot} - set(picked))
+        if steps:
+            picked.update(zip(steps, pick(blocks, steps)))
+
+    def move(lot):
+        for n in lot:
+            pairs = [(i, partner(i, n, owners)[1]) for i in range(owners)]
+            moved.append((n, lax.ppermute(picked[n], "gy", pairs)))
+
+    early, middle, third, late = cold_lots(owners)
+    take(early, middle)
+    move(early)
     mine, send = hot_sums(hot_ids, hot_grads, HOT)
     got = lax.ppermute(send, "core", swap)
-    move(picked, middle)
+    move(middle)
     places = lax.broadcasted_iota(jnp.int32, (owners, capacity), 1)
     used = jnp.where(places < cold_counts.reshape(owners, 1), cold_slots.reshape(owners, capacity), -1)
     own, coded = pack(mine, got, groups, owners)
     crossed = []
     for n, block in enumerate(coded, 1):
         crossed.append(lax.ppermute(block, "chip", [(i, partner(i, n, groups)[1]) for i in range(groups)]))
-    move(take(third), third)
+    take(third, late)
+    move(third)
     joined = join(own, used.reshape(owners, lines, LANES), crossed)
     parts = lax.all_to_all(joined, "gy", split_axis=0, concat_axis=0, tiled=True)
-    move(take(late), late)
+    move(late)
     summed = add(parts, factor, tail_rows(lines), peers)
     all_rows = lax.all_to_all(summed, everyone, split_axis=0, concat_axis=0, tiled=True)
-    cold_grad = cold_sums(parts, blocks, [moved[n] for n in range(1, owners)], OWN_ROWS)
+    cold_grad = cold_sums(parts, blocks, [block for _, block in moved], [n for n, _ in moved], OWN_ROWS)
     others = lax.ppermute(all_rows, "core", swap)
     hot_grad = unpack(all_rows, others, HOT)
     return hot_grad, cold_grad.reshape(1, OWN_ROWS, width)

time: 63.6 us -> 63.9 us (level)
    all_to_all x1, waiting for transfers between devices: 0.01 us -> 2.07 us  [per_device(): lax.all_to_all(summed, everyone, split_axis=0, concat_axis=0, tiled=True)]
    ppermute x7, waiting for transfers between devices: 5.89 us -> 4.29 us  [move(): moved.append((n, lax.ppermute(picked[n], 'gy', pairs)))]
    pallas_call x3 -> x2, Pallas kernels: 3.03 us -> 2.28 us  [pick(): pl.pallas_call(functools.partial(pick_kernel, steps=steps), in_specs=[pl....]
  transfers between devices with their start and end apart: 12 -> 12, of which waited for: 6 -> 6; matrix products, arithmetic and copies ran while one was open for 0% -> 0% of each run, Pallas kernels for 12% -> 11%
where the time goes in v5:
time: 63.9 us; the launch traced here: 63.4 us
  starting transfers between devices  26.9 us (42%)
  waiting for transfers between devices  19.3 us (30%)
  Pallas kernels  14.1 us (22%)
  local copies, waits for them, and re-layouts  2.37 us (4%)
  between operations  0.71 us (1%)
    ppermute x7, starting transfers between devices, move(): moved.append((n, lax.ppermute(picked[n], 'gy', pairs)))  13.2 us
    all_to_all x1, waiting for transfers between devices, per_device(): lax.all_to_all(joined, 'gy', split_axis=0, concat_axis=0, tiled=True)  7.37 us
    all_to_all x1, starting transfers between devices, per_device(): lax.all_to_all(joined, 'gy', split_axis=0, concat_axis=0, tiled=True)  6.08 us
    pallas_call x1, Pallas kernels, hot_sums(): pl.pallas_call(functools.partial(hot_kernel, block=math.gcd(half, 256), s...  4.98 us
    ppermute x7, waiting for transfers between devices, move(): moved.append((n, lax.ppermute(picked[n], 'gy', pairs)))  4.29 us
    all_to_all x1, starting transfers between devices, per_device(): lax.all_to_all(summed, everyone, split_axis=0, concat_axis=0, tiled=True)  4.13 us
    ppermute x1, waiting for transfers between devices, per_device(): lax.ppermute(block, 'chip', [(i, partner(i, n, groups)[1]) for i in range...  4.07 us
    pallas_call x1, Pallas kernels, cold_sums(): pl.pallas_call(functools.partial(cold_kernel, block=math.gcd(table // 2,...  4.03 us
  transfers between devices with their start and end apart: 12, of which 6 were waited for; matrix products, arithmetic and copies ran while one was open for 0% of the time, Pallas kernels for 11%

profile of v5, /device:TPU:0, one launch (start us, length us, event | category | flops | bytes accessed | tf_op | source)
XLA Modules:
  0.0 63.4 jit_solution(2034253444909704189)
XLA Ops:
  0.6 0.0 copy-start
  0.6 1.6 %copy-done = bf16[8192,128]{1,0:T(8,128)(2,1)S(1)} copy-done((bf16[8192,128]{1,0:T(8,128)(2,1)S(1)}, bf16[8192,128]{1,0:T(8,128)(2,1)}, u32[]{:S(2)}) %copy-start) | copy-done | bytes 2097176
  2.2 0.0 copy-start.2
  2.2 0.8 %copy-done.2 = s32[8192]{0:T(1024)S(1)} copy-done((s32[8192]{0:T(1024)S(1)}, s32[8192]{0:T(1024)}, u32[]{:S(2)}) %copy-start.2) | copy-done | bytes 32792
  3.0 0.0 copy-start.3
  3.0 0.0 copy-start.4
  3.0 5.0 %hot_sums.1 = (f32[1024,128]{1,0:T(8,128)S(1)}, f32[1024,128]{1,0:T(8,128)S(1)}) custom-call(s32[64,128]{1,0:T(8,128)S(1)} %bitcast.9, bf16[8192,128]{1,0:T(8,128)(2,1)S(1)} %copy-done), custom_call_target="tpu_custom_call" | custom-call | flops 4294967296 | bytes 2097152 | tf_op jit(solution)/shard_map/hot_sums/pallas_call | solution.py:72
  8.0 0.6 collective-permute-start
  8.5 0.0 copy-done.3
  8.6 1.5 %collective-permute-done.got_ref = f32[1024,128]{1,0:T(8,128)S(1)} collective-permute-done((f32[1024,128]{1,0:T(8,128)S(1)}, f32[1024,128]{1,0:T(8,128)S(1)}, u32[]{:S(2)}, u32[]{:S(2)}) %collective-permute-start) | collective-permute-done | bytes 524320 | tf_op jit(solution)/shard_map/ppermute | solution.py:340
  10.1 0.1 pack.1
  10.2 2.9 %collective-permute-start.1 = (s16[8,72,128]{2,1,0:T(8,128)(2,1)S(1)}, s16[8,72,128]{2,1,0:T(8,128)(2,1)S(1)}, u32[]{:S(2)}, u32[]{:S(2)}) collective-permute-start(s16[8,72,128]{2,1,0:T(8,128)(2,1)S(1)} %get-tuple-element.16), channel_id=1, source_target_pairs={{0,16},{16,0},{1,17},{17,1},{2,18},{18,2},{3,19},{19,3},{4,20},{20... | collective-permute-start | bytes 442376 | tf_op jit(solution)/shard_map/ppermute | solution.py:347
  13.1 0.0 copy-done.4
  13.1 0.1 compare_select_fusion.slots_ref
  13.2 4.1 %collective-permute-done.1.refs_0_ = s16[8,72,128]{2,1,0:T(8,128)(2,1)S(1)} collective-permute-done((s16[8,72,128]{2,1,0:T(8,128)(2,1)S(1)}, s16[8,72,128]{2,1,0:T(8,128)(2,1)S(1)}, u32[]{:S(2)}, u32[]{:S(2)}) %collective-permute-start.1) | collective-permute-done | bytes 147488 | tf_op jit(solution)/shard_map/ppermute | solution.py:347
  17.2 0.8 %join.1 = s16[8,72,128]{2,1,0:T(8,128)(2,1)} custom-call(f32[512,128]{1,0:T(8,128)S(1)} %get-tuple-element.15.own_ref, s32[8,4,128]{2,1,0:T(4,128)S(1)} %compare_select_fusion.slots_ref, s16[8,72,128]{2,1,0:T(8,128)(2,1)S(1)} %collective-permute-done.1.refs_0_), custom_call_target="tpu_custom_call" | custom-call | flops 524288 | bytes 655360 | tf_op jit(solution)/shard_map/join/pallas_call | solution.py:197
  18.0 6.1 %all-to-all-start = ((s16[8,72,128]{2,1,0:T(8,128)(2,1)}), s16[8,72,128]{2,1,0:T(8,128)(2,1)S(1)}, u32[]{:S(2)}, u32[]{:S(2)}) async-start(s16[8,72,128]{2,1,0:T(8,128)(2,1)} %join.1), calls=%async_computation | async-start | bytes 294912 | tf_op jit(solution)/shard_map/all_to_all | solution.py:351
  24.1 1.0 %pick.2 = (bf16[512,128]{1,0:T(8,128)(2,1)S(1)}, bf16[512,128]{1,0:T(8,128)(2,1)S(1)}) custom-call(bf16[8,512,128]{2,1,0:T(8,128)(2,1)} %bitcast.6), custom_call_target="tpu_custom_call" | custom-call | flops 5000000000 | bytes 262144 | tf_op jit(solution)/shard_map/pick/pallas_call | solution.py:99
  25.1 3.0 %collective-permute-start.3 = (bf16[512,128]{1,0:T(8,128)(2,1)S(1)}, bf16[512,128]{1,0:T(8,128)(2,1)S(1)}, u32[]{:S(2)}, u32[]{:S(2)}) collective-permute-start(bf16[512,128]{1,0:T(8,128)(2,1)S(1)} %get-tuple-element.17), channel_id=1, source_target_pairs={{0,4},{1,5},{2,6},{3,7},{4,0},{5,1},{6,2},{7,3},{8,12},{9,13},{10,... | collective-permute-start | bytes 393224 | tf_op jit(solution)/shard_map/ppermute | solution.py:334
  28.1 1.5 %collective-permute-start.4 = (bf16[512,128]{1,0:T(8,128)(2,1)S(1)}, bf16[512,128]{1,0:T(8,128)(2,1)S(1)}, u32[]{:S(2)}, u32[]{:S(2)}) collective-permute-start(bf16[512,128]{1,0:T(8,128)(2,1)S(1)} %get-tuple-element.18), channel_id=1, source_target_pairs={{0,5},{1,4},{2,7},{3,6},{4,1},{5,0},{6,3},{7,2},{8,13},{9,12},{10,... | collective-permute-start | bytes 393224 | tf_op jit(solution)/shard_map/ppermute | solution.py:334
  29.5 7.4 %all-to-all-done.got_ref = s16[8,72,128]{2,1,0:T(8,128)(2,1)S(1)} async-done(((s16[8,72,128]{2,1,0:T(8,128)(2,1)}), s16[8,72,128]{2,1,0:T(8,128)(2,1)S(1)}, u32[]{:S(2)}, u32[]{:S(2)}) %all-to-all-start) | async-done | bytes 147488 | tf_op jit(solution)/shard_map/all_to_all | solution.py:351
  36.9 0.8 %add.5 = s16[16,72,128]{2,1,0:T(8,128)(2,1)} custom-call(s16[8,72,128]{2,1,0:T(8,128)(2,1)S(1)} %all-to-all-done.got_ref), custom_call_target="tpu_custom_call" | custom-call | flops 589824 | bytes 294912 | tf_op jit(solution)/shard_map/add/pallas_call | solution.py:225
  37.7 4.1 %all-to-all-start.1 = ((s16[16,72,128]{2,1,0:T(8,128)(2,1)}), s16[16,72,128]{2,1,0:T(8,128)(2,1)S(1)}, u32[]{:S(2)}, u32[]{:S(2)}) async-start(s16[16,72,128]{2,1,0:T(8,128)(2,1)} %add.5), calls=%async_computation.1 | async-start | bytes 589824 | tf_op jit(solution)/shard_map/all_to_all | solution.py:354
  41.9 0.0 copy-start.1
  41.9 1.3 %pick.3 = (bf16[512,128]{1,0:T(8,128)(2,1)S(1)}, bf16[512,128]{1,0:T(8,128)(2,1)S(1)}, bf16[512,128]{1,0:T(8,128)(2,1)S(1)}, bf16[512,128]{1,0:T(8,128)(2,1)S(1)}, bf16[512,128]{1,0:T(8,128)(2,1)S(1)}) custom-call(bf16[8,512,128]{2,1,0:T(8,128)(2,1)} %bitcast.7), custom_call_target="tpu_custom_call" | custom-call | flops 5000000000 | bytes 655360 | tf_op jit(solution)/shard_map/pick/pallas_call | solution.py:99
  43.2 3.8 %collective-permute-start.5 = (bf16[512,128]{1,0:T(8,128)(2,1)S(1)}, bf16[512,128]{1,0:T(8,128)(2,1)S(1)}, u32[]{:S(2)}, u32[]{:S(2)}) collective-permute-start(bf16[512,128]{1,0:T(8,128)(2,1)S(1)} %get-tuple-element.19), channel_id=1, source_target_pairs={{0,6},{1,7},{2,4},{3,5},{4,2},{5,3},{6,0},{7,1},{8,14},{9,15},{10,... | collective-permute-start | bytes 393224 | tf_op jit(solution)/shard_map/ppermute | solution.py:334
  47.0 1.5 %collective-permute-start.6 = (bf16[512,128]{1,0:T(8,128)(2,1)S(1)}, bf16[512,128]{1,0:T(8,128)(2,1)S(1)}, u32[]{:S(2)}, u32[]{:S(2)}) collective-permute-start(bf16[512,128]{1,0:T(8,128)(2,1)S(1)} %get-tuple-element.20), channel_id=1, source_target_pairs={{0,1},{1,0},{2,3},{3,2},{4,5},{5,4},{6,7},{7,6},{8,9},{9,8},{10,11... | collective-permute-start | bytes 393224 | tf_op jit(solution)/shard_map/ppermute | solution.py:334
  48.4 0.0 collective-permute-start.7
  48.4 0.0 collective-permute-done.3.refs_0_
  48.4 2.0 %collective-permute-start.8 = (bf16[512,128]{1,0:T(8,128)(2,1)S(1)}, bf16[512,128]{1,0:T(8,128)(2,1)S(1)}, u32[]{:S(2)}, u32[]{:S(2)}) collective-permute-start(bf16[512,128]{1,0:T(8,128)(2,1)S(1)} %get-tuple-element.22), channel_id=1, source_target_pairs={{0,3},{1,2},{2,1},{3,0},{4,7},{5,6},{6,5},{7,4},{8,11},{9,10},{10,... | collective-permute-start | bytes 393224 | tf_op jit(solution)/shard_map/ppermute | solution.py:334
  50.5 0.0 collective-permute-done.4.refs_1_
  50.5 1.5 %collective-permute-start.9 = (bf16[512,128]{1,0:T(8,128)(2,1)S(1)}, bf16[512,128]{1,0:T(8,128)(2,1)S(1)}, u32[]{:S(2)}, u32[]{:S(2)}) collective-permute-start(bf16[512,128]{1,0:T(8,128)(2,1)S(1)} %get-tuple-element.23), channel_id=1, source_target_pairs={{0,7},{1,6},{2,5},{3,4},{4,3},{5,2},{6,1},{7,0},{8,15},{9,14},{10,... | collective-permute-start | bytes 393224 | tf_op jit(solution)/shard_map/ppermute | solution.py:334
  51.9 0.6 collective-permute-done.5.refs_2_
  52.5 2.1 %all-to-all-done.1.mine_ref = s16[16,72,128]{2,1,0:T(8,128)(2,1)S(1)} async-done(((s16[16,72,128]{2,1,0:T(8,128)(2,1)}), s16[16,72,128]{2,1,0:T(8,128)(2,1)S(1)}, u32[]{:S(2)}, u32[]{:S(2)}) %all-to-all-start.1) | async-done | bytes 294944 | tf_op jit(solution)/shard_map/all_to_all | solution.py:354
  54.6 0.0 collective-permute-start.2
  54.6 0.0 collective-permute-done.6.refs_3_
  54.6 0.0 collective-permute-done.7.refs_4_
  54.6 3.7 %collective-permute-done.8.refs_5_ = bf16[512,128]{1,0:T(8,128)(2,1)S(1)} collective-permute-done((bf16[512,128]{1,0:T(8,128)(2,1)S(1)}, bf16[512,128]{1,0:T(8,128)(2,1)S(1)}, u32[]{:S(2)}, u32[]{:S(2)}) %collective-permute-start.8) | collective-permute-done | bytes 131104 | tf_op jit(solution)/shard_map/ppermute | solution.py:334
  58.3 0.0 collective-permute-done.9.refs_6_
  58.3 0.0 copy-done.1
  58.3 4.0 %cold_sums.1 = f32[2048,128]{1,0:T(8,128)} custom-call(s16[8,72,128]{2,1,0:T(8,128)(2,1)S(1)} %all-to-all-done.got_ref, bf16[8,512,128]{2,1,0:T(8,128)(2,1)S(1)} %bitcast.8, bf16[512,128]{1,0:T(8,128)(2,1)S(1)} %collective-permute-done.3.refs_0_, bf16[512,128]{1,0:T(8,128)(2,1)S(1)} %collective-permute-done.4.refs_1_, ...), custom_call_target="tpu_custom_call" | custom-call | flops 2147483648 | bytes 1048576 | tf_op jit(solution)/shard_map/cold_sums/pallas_call | solution.py:297
  62.3 0.0 collective-permute-done.2.other_ref
  62.3 1.1 %unpack.1 = f32[2048,128]{1,0:T(8,128)} custom-call(s16[16,72,128]{2,1,0:T(8,128)(2,1)S(1)} %all-to-all-done.1.mine_ref, s16[16,72,128]{2,1,0:T(8,128)(2,1)S(1)} %collective-permute-done.2.other_ref), custom_call_target="tpu_custom_call" | custom-call | flops 1048576 | bytes 1572864 | tf_op jit(solution)/shard_map/unpack/pallas_call | solution.py:250
  (2 shorter events, 0.0 us)
Async XLA Ops:
  0.6 1.6 %copy-start = (bf16[8192,128]{1,0:T(8,128)(2,1)S(1)}, bf16[8192,128]{1,0:T(8,128)(2,1)}, u32[]{:S(2)}) copy-start(bf16[8192,128]{1,0:T(8,128)(2,1)} %data_ref.1) | copy-start | bytes 6291460
  2.2 0.8 %copy-start.2 = (s32[8192]{0:T(1024)S(1)}, s32[8192]{0:T(1024)}, u32[]{:S(2)}) copy-start(s32[8192]{0:T(1024)} %param.5) | copy-start | bytes 98308
  3.0 5.6 %copy-start.3 = (s32[1,1,8,512]{3,2,1,0:T(8,128)S(1)}, s32[1,1,8,512]{3,2,1,0:T(8,128)}, u32[]{:S(2)}) copy-start(s32[1,1,8,512]{3,2,1,0:T(8,128)} %param.8) | copy-start | bytes 49156
  3.0 10.1 %copy-start.4 = (s32[1,1,8]{2,1,0:T(1,128)S(1)}, s32[1,1,8]{2,1,0:T(1,128)}, u32[]{:S(2)}) copy-start(s32[1,1,8]{2,1,0:T(1,128)} %param.9) | copy-start | bytes 100
  8.0 2.1 %collective-permute-start = (f32[1024,128]{1,0:T(8,128)S(1)}, f32[1024,128]{1,0:T(8,128)S(1)}, u32[]{:S(2)}, u32[]{:S(2)}) collective-permute-start(f32[1024,128]{1,0:T(8,128)S(1)} %get-tuple-element.14), channel_id=1, source_target_pairs={{0,8},{8,0},{1,9},{9,1},{2,10},{10,2},{3,11},{11,3},{4,12},{12,4},... | collective-permute-start | bytes 1572872 | tf_op jit(solution)/shard_map/ppermute | solution.py:340
  10.2 7.1 %collective-permute-start.1 = (s16[8,72,128]{2,1,0:T(8,128)(2,1)S(1)}, s16[8,72,128]{2,1,0:T(8,128)(2,1)S(1)}, u32[]{:S(2)}, u32[]{:S(2)}) collective-permute-start(s16[8,72,128]{2,1,0:T(8,128)(2,1)S(1)} %get-tuple-element.16), channel_id=1, source_target_pairs={{0,16},{16,0},{1,17},{17,1},{2,18},{18,2},{3,19},{19,3},{4,20},{20... | collective-permute-start | bytes 442376 | tf_op jit(solution)/shard_map/ppermute | solution.py:347
  18.0 18.9 %all-to-all-start = ((s16[8,72,128]{2,1,0:T(8,128)(2,1)}), s16[8,72,128]{2,1,0:T(8,128)(2,1)S(1)}, u32[]{:S(2)}, u32[]{:S(2)}) async-start(s16[8,72,128]{2,1,0:T(8,128)(2,1)} %join.1), calls=%async_computation | async-start | bytes 294912 | tf_op jit(solution)/shard_map/all_to_all | solution.py:351
  25.1 23.3 %collective-permute-start.3 = (bf16[512,128]{1,0:T(8,128)(2,1)S(1)}, bf16[512,128]{1,0:T(8,128)(2,1)S(1)}, u32[]{:S(2)}, u32[]{:S(2)}) collective-permute-start(bf16[512,128]{1,0:T(8,128)(2,1)S(1)} %get-tuple-element.17), channel_id=1, source_target_pairs={{0,4},{1,5},{2,6},{3,7},{4,0},{5,1},{6,2},{7,3},{8,12},{9,13},{10,... | collective-permute-start | bytes 393224 | tf_op jit(solution)/shard_map/ppermute | solution.py:334
  28.1 22.4 %collective-permute-start.4 = (bf16[512,128]{1,0:T(8,128)(2,1)S(1)}, bf16[512,128]{1,0:T(8,128)(2,1)S(1)}, u32[]{:S(2)}, u32[]{:S(2)}) collective-permute-start(bf16[512,128]{1,0:T(8,128)(2,1)S(1)} %get-tuple-element.18), channel_id=1, source_target_pairs={{0,5},{1,4},{2,7},{3,6},{4,1},{5,0},{6,3},{7,2},{8,13},{9,12},{10,... | collective-permute-start | bytes 393224 | tf_op jit(solution)/shard_map/ppermute | solution.py:334
  37.7 16.9 %all-to-all-start.1 = ((s16[16,72,128]{2,1,0:T(8,128)(2,1)}), s16[16,72,128]{2,1,0:T(8,128)(2,1)S(1)}, u32[]{:S(2)}, u32[]{:S(2)}) async-start(s16[16,72,128]{2,1,0:T(8,128)(2,1)} %add.5), calls=%async_computation.1 | async-start | bytes 589824 | tf_op jit(solution)/shard_map/all_to_all | solution.py:354
  41.9 16.4 %copy-start.1 = (bf16[1,1,8,512,128]{4,3,2,1,0:T(8,128)(2,1)S(1)}, bf16[1,1,8,512,128]{4,3,2,1,0:T(8,128)(2,1)}, u32[]{:S(2)}) copy-start(bf16[1,1,8,512,128]{4,3,2,1,0:T(8,128)(2,1)} %param.7) | copy-start | bytes 3145732
  43.2 9.3 %collective-permute-start.5 = (bf16[512,128]{1,0:T(8,128)(2,1)S(1)}, bf16[512,128]{1,0:T(8,128)(2,1)S(1)}, u32[]{:S(2)}, u32[]{:S(2)}) collective-permute-start(bf16[512,128]{1,0:T(8,128)(2,1)S(1)} %get-tuple-element.19), channel_id=1, source_target_pairs={{0,6},{1,7},{2,4},{3,5},{4,2},{5,3},{6,0},{7,1},{8,14},{9,15},{10,... | collective-permute-start | bytes 393224 | tf_op jit(solution)/shard_map/ppermute | solution.py:334
  47.0 7.6 %collective-permute-start.6 = (bf16[512,128]{1,0:T(8,128)(2,1)S(1)}, bf16[512,128]{1,0:T(8,128)(2,1)S(1)}, u32[]{:S(2)}, u32[]{:S(2)}) collective-permute-start(bf16[512,128]{1,0:T(8,128)(2,1)S(1)} %get-tuple-element.20), channel_id=1, source_target_pairs={{0,1},{1,0},{2,3},{3,2},{4,5},{5,4},{6,7},{7,6},{8,9},{9,8},{10,11... | collective-permute-start | bytes 393224 | tf_op jit(solution)/shard_map/ppermute | solution.py:334
  48.4 6.2 %collective-permute-start.7 = (bf16[512,128]{1,0:T(8,128)(2,1)S(1)}, bf16[512,128]{1,0:T(8,128)(2,1)S(1)}, u32[]{:S(2)}, u32[]{:S(2)}) collective-permute-start(bf16[512,128]{1,0:T(8,128)(2,1)S(1)} %get-tuple-element.21), channel_id=1, source_target_pairs={{0,2},{1,3},{2,0},{3,1},{4,6},{5,7},{6,4},{7,5},{8,10},{9,11},{10,... | collective-permute-start | bytes 393224 | tf_op jit(solution)/shard_map/ppermute | solution.py:334
  48.4 9.8 %collective-permute-start.8 = (bf16[512,128]{1,0:T(8,128)(2,1)S(1)}, bf16[512,128]{1,0:T(8,128)(2,1)S(1)}, u32[]{:S(2)}, u32[]{:S(2)}) collective-permute-start(bf16[512,128]{1,0:T(8,128)(2,1)S(1)} %get-tuple-element.22), channel_id=1, source_target_pairs={{0,3},{1,2},{2,1},{3,0},{4,7},{5,6},{6,5},{7,4},{8,11},{9,10},{10,... | collective-permute-start | bytes 393224 | tf_op jit(solution)/shard_map/ppermute | solution.py:334
  50.5 7.8 %collective-permute-start.9 = (bf16[512,128]{1,0:T(8,128)(2,1)S(1)}, bf16[512,128]{1,0:T(8,128)(2,1)S(1)}, u32[]{:S(2)}, u32[]{:S(2)}) collective-permute-start(bf16[512,128]{1,0:T(8,128)(2,1)S(1)} %get-tuple-element.23), channel_id=1, source_target_pairs={{0,7},{1,6},{2,5},{3,4},{4,3},{5,2},{6,1},{7,0},{8,15},{9,14},{10,... | collective-permute-start | bytes 393224 | tf_op jit(solution)/shard_map/ppermute | solution.py:334
  54.6 7.7 %collective-permute-start.2 = (s16[16,72,128]{2,1,0:T(8,128)(2,1)S(1)}, s16[16,72,128]{2,1,0:T(8,128)(2,1)S(1)}, u32[]{:S(2)}, u32[]{:S(2)}) collective-permute-start(s16[16,72,128]{2,1,0:T(8,128)(2,1)S(1)} %all-to-all-done.1.mine_ref), channel_id=1, source_target_pairs={{0,8},{8,0},{1,9},{9,1},{2,10},{10,2},{3,11},{11,3},{4,12},{12,4},... | collective-permute-start | bytes 884744 | tf_op jit(solution)/shard_map/ppermute | solution.py:356

commit v6 on v5

--- a/solution.py
+++ b/solution.py
@@ -233,29 +233,42 @@
     )(got)
 
 
-def unpack_kernel(mine_ref, other_ref, out_ref):
-    peers, rows, _ = mine_ref.shape
+def unpack_kernel(codes_ref, *refs, flip):
+    out_hbm, half_ref, sems = refs[-3:]
+    peers, rows, _ = codes_ref.shape
     rows -= SUB
     core = lax.axis_index("core")
-    for ref, side in ((mine_ref, core), (other_ref, 1 - core)):
-        for p in range(peers):
-            ends = widen(ref[p, rows:, :])
-            start = pl.multiple_of(side * (peers * rows) + p * rows, SUB)
-            out_ref[pl.ds(start, rows), :] = decode(widen(ref[p, :rows, :]), ends[:SCALES])
-
-
-def unpack(mine, other, table):
-    width = mine.shape[2]
-    whole = pl.BlockSpec(memory_space=pltpu.VMEM)
-    return pl.pallas_call(
-        unpack_kernel,
-        in_specs=[whole, whole],
-        out_specs=whole,
+    base = (1 - core if flip else core) * (peers * rows)
+    parts = sems.shape[0]
+    span = peers // parts
+    copies = []
+    for part in range(parts):
+        for p in range(part * span, (part + 1) * span):
+            ends = widen(codes_ref[p, rows:, :])
+            half_ref[pl.ds(p * rows, rows), :] = decode(widen(codes_ref[p, :rows, :]), ends[:SCALES])
+        start = pl.multiple_of(base + part * span * rows, SUB)
+        here = half_ref.at[pl.ds(part * span * rows, span * rows)]
+        copies.append(pltpu.make_async_copy(here, out_hbm.at[pl.ds(start, span * rows)], sems.at[part]))
+        copies[-1].start()
+    for copy in copies:
+        copy.wait()
+
+
+def unpack(codes, table, before=None):
+    peers, _, width = codes.shape
+    hbm = pl.BlockSpec(memory_space=pltpu.HBM)
+    flip = before is not None
+    return pl.pallas_call(
+        functools.partial(unpack_kernel, flip=flip),
+        in_specs=[pl.BlockSpec(memory_space=pltpu.VMEM)] + [hbm] * flip,
+        out_specs=hbm,
         out_shape=jax.ShapeDtypeStruct((table, width), jnp.float32),
-        cost_estimate=pl.CostEstimate(flops=table * width * 4, bytes_accessed=table * width * 6, transcendentals=0),
+        input_output_aliases={1: 0} if flip else {},
+        scratch_shapes=[pltpu.VMEM((table // 2, width), jnp.float32), pltpu.SemaphoreType.DMA((math.gcd(peers, 4),))],
+        cost_estimate=pl.CostEstimate(flops=table * width * 2, bytes_accessed=table * width * 3, transcendentals=0),
         compiler_params=ROOM,
         name="unpack",
-    )(mine, other)
+    )(codes, *([before] if flip else []))
 
 
 def partner(me, step, count):
@@ -354,7 +367,8 @@
     all_rows = lax.all_to_all(summed, everyone, split_axis=0, concat_axis=0, tiled=True)
     cold_grad = cold_sums(parts, blocks, [block for _, block in moved], [n for n, _ in moved], OWN_ROWS)
     others = lax.ppermute(all_rows, "core", swap)
-    hot_grad = unpack(all_rows, others, HOT)
+    hot_half = unpack(all_rows, HOT)
+    hot_grad = unpack(others, HOT, hot_half)
     return hot_grad, cold_grad.reshape(1, OWN_ROWS, width)
 
 

time: 63.9 us -> 64.5 us (level)
    pallas_call x1 -> x2, Pallas kernels: 1.11 us -> 1.68 us  [unpack(): pl.pallas_call(functools.partial(unpack_kernel, flip=flip), in_specs=[pl....]
  transfers between devices with their start and end apart: 12 -> 12, of which waited for: 6 -> 6; matrix products, arithmetic and copies ran while one was open for 0% -> 0% of each run, Pallas kernels for 11% -> 12%
where the time goes in v6:
time: 64.5 us; the launch traced here: 64 us
  starting transfers between devices  26.9 us (42%)
  waiting for transfers between devices  19.3 us (30%)
  Pallas kernels  14.7 us (23%)
  local copies, waits for them, and re-layouts  2.37 us (4%)
  between operations  0.72 us (1%)
    ppermute x7, starting transfers between devices, move(): moved.append((n, lax.ppermute(picked[n], 'gy', pairs)))  13.2 us
    all_to_all x1, waiting for transfers between devices, per_device(): lax.all_to_all(joined, 'gy', split_axis=0, concat_axis=0, tiled=True)  7.37 us
    all_to_all x1, starting transfers between devices, per_device(): lax.all_to_all(joined, 'gy', split_axis=0, concat_axis=0, tiled=True)  6.08 us
    pallas_call x1, Pallas kernels, hot_sums(): pl.pallas_call(functools.partial(hot_kernel, block=math.gcd(half, 256), s...  4.98 us
    ppermute x7, waiting for transfers between devices, move(): moved.append((n, lax.ppermute(picked[n], 'gy', pairs)))  4.29 us
    all_to_all x1, starting transfers between devices, per_device(): lax.all_to_all(summed, everyone, split_axis=0, concat_axis=0, tiled=True)  4.13 us
    ppermute x1, waiting for transfers between devices, per_device(): lax.ppermute(block, 'chip', [(i, partner(i, n, groups)[1]) for i in range...  4.07 us
    pallas_call x1, Pallas kernels, cold_sums(): pl.pallas_call(functools.partial(cold_kernel, block=math.gcd(table // 2,...  4.03 us
  transfers between devices with their start and end apart: 12, of which 6 were waited for; matrix products, arithmetic and copies ran while one was open for 0% of the time, Pallas kernels for 12%

profile of v6, /device:TPU:0, one launch (start us, length us, event | category | flops | bytes accessed | tf_op | source)
XLA Modules:
  0.0 64.0 jit_solution(15024748640730673262)
XLA Ops:
  0.6 0.0 copy-start
  0.6 1.6 %copy-done = bf16[8192,128]{1,0:T(8,128)(2,1)S(1)} copy-done((bf16[8192,128]{1,0:T(8,128)(2,1)S(1)}, bf16[8192,128]{1,0:T(8,128)(2,1)}, u32[]{:S(2)}) %copy-start) | copy-done | bytes 2097176
  2.2 0.0 copy-start.2
  2.2 0.8 %copy-done.2 = s32[8192]{0:T(1024)S(1)} copy-done((s32[8192]{0:T(1024)S(1)}, s32[8192]{0:T(1024)}, u32[]{:S(2)}) %copy-start.2) | copy-done | bytes 32792
  3.0 0.0 copy-start.3
  3.0 0.0 copy-start.4
  3.0 5.0 %hot_sums.1 = (f32[1024,128]{1,0:T(8,128)S(1)}, f32[1024,128]{1,0:T(8,128)S(1)}) custom-call(s32[64,128]{1,0:T(8,128)S(1)} %bitcast.9, bf16[8192,128]{1,0:T(8,128)(2,1)S(1)} %copy-done), custom_call_target="tpu_custom_call" | custom-call | flops 4294967296 | bytes 2097152 | tf_op jit(solution)/shard_map/hot_sums/pallas_call | solution.py:72
  8.0 0.6 collective-permute-start
  8.5 0.0 copy-done.3
  8.6 1.5 %collective-permute-done.got_ref = f32[1024,128]{1,0:T(8,128)S(1)} collective-permute-done((f32[1024,128]{1,0:T(8,128)S(1)}, f32[1024,128]{1,0:T(8,128)S(1)}, u32[]{:S(2)}, u32[]{:S(2)}) %collective-permute-start) | collective-permute-done | bytes 524320 | tf_op jit(solution)/shard_map/ppermute | solution.py:353
  10.1 0.1 pack.1
  10.2 2.9 %collective-permute-start.1 = (s16[8,72,128]{2,1,0:T(8,128)(2,1)S(1)}, s16[8,72,128]{2,1,0:T(8,128)(2,1)S(1)}, u32[]{:S(2)}, u32[]{:S(2)}) collective-permute-start(s16[8,72,128]{2,1,0:T(8,128)(2,1)S(1)} %get-tuple-element.16), channel_id=1, source_target_pairs={{0,16},{16,0},{1,17},{17,1},{2,18},{18,2},{3,19},{19,3},{4,20},{20... | collective-permute-start | bytes 442376 | tf_op jit(solution)/shard_map/ppermute | solution.py:360
  13.1 0.0 copy-done.4
  13.1 0.1 compare_select_fusion.slots_ref
  13.2 4.1 %collective-permute-done.1.refs_0_ = s16[8,72,128]{2,1,0:T(8,128)(2,1)S(1)} collective-permute-done((s16[8,72,128]{2,1,0:T(8,128)(2,1)S(1)}, s16[8,72,128]{2,1,0:T(8,128)(2,1)S(1)}, u32[]{:S(2)}, u32[]{:S(2)}) %collective-permute-start.1) | collective-permute-done | bytes 147488 | tf_op jit(solution)/shard_map/ppermute | solution.py:360
  17.2 0.8 %join.1 = s16[8,72,128]{2,1,0:T(8,128)(2,1)} custom-call(f32[512,128]{1,0:T(8,128)S(1)} %get-tuple-element.15.own_ref, s32[8,4,128]{2,1,0:T(4,128)S(1)} %compare_select_fusion.slots_ref, s16[8,72,128]{2,1,0:T(8,128)(2,1)S(1)} %collective-permute-done.1.refs_0_), custom_call_target="tpu_custom_call" | custom-call | flops 524288 | bytes 655360 | tf_op jit(solution)/shard_map/join/pallas_call | solution.py:197
  18.0 6.1 %all-to-all-start = ((s16[8,72,128]{2,1,0:T(8,128)(2,1)}), s16[8,72,128]{2,1,0:T(8,128)(2,1)S(1)}, u32[]{:S(2)}, u32[]{:S(2)}) async-start(s16[8,72,128]{2,1,0:T(8,128)(2,1)} %join.1), calls=%async_computation | async-start | bytes 294912 | tf_op jit(solution)/shard_map/all_to_all | solution.py:364
  24.1 1.0 %pick.2 = (bf16[512,128]{1,0:T(8,128)(2,1)S(1)}, bf16[512,128]{1,0:T(8,128)(2,1)S(1)}) custom-call(bf16[8,512,128]{2,1,0:T(8,128)(2,1)} %bitcast.6), custom_call_target="tpu_custom_call" | custom-call | flops 5000000000 | bytes 262144 | tf_op jit(solution)/shard_map/pick/pallas_call | solution.py:99
  25.1 3.0 %collective-permute-start.3 = (bf16[512,128]{1,0:T(8,128)(2,1)S(1)}, bf16[512,128]{1,0:T(8,128)(2,1)S(1)}, u32[]{:S(2)}, u32[]{:S(2)}) collective-permute-start(bf16[512,128]{1,0:T(8,128)(2,1)S(1)} %get-tuple-element.17), channel_id=1, source_target_pairs={{0,4},{1,5},{2,6},{3,7},{4,0},{5,1},{6,2},{7,3},{8,12},{9,13},{10,... | collective-permute-start | bytes 393224 | tf_op jit(solution)/shard_map/ppermute | solution.py:347
  28.1 1.5 %collective-permute-start.4 = (bf16[512,128]{1,0:T(8,128)(2,1)S(1)}, bf16[512,128]{1,0:T(8,128)(2,1)S(1)}, u32[]{:S(2)}, u32[]{:S(2)}) collective-permute-start(bf16[512,128]{1,0:T(8,128)(2,1)S(1)} %get-tuple-element.18), channel_id=1, source_target_pairs={{0,5},{1,4},{2,7},{3,6},{4,1},{5,0},{6,3},{7,2},{8,13},{9,12},{10,... | collective-permute-start | bytes 393224 | tf_op jit(solution)/shard_map/ppermute | solution.py:347
  29.5 7.4 %all-to-all-done.got_ref = s16[8,72,128]{2,1,0:T(8,128)(2,1)S(1)} async-done(((s16[8,72,128]{2,1,0:T(8,128)(2,1)}), s16[8,72,128]{2,1,0:T(8,128)(2,1)S(1)}, u32[]{:S(2)}, u32[]{:S(2)}) %all-to-all-start) | async-done | bytes 147488 | tf_op jit(solution)/shard_map/all_to_all | solution.py:364
  36.9 0.8 %add.5 = s16[16,72,128]{2,1,0:T(8,128)(2,1)} custom-call(s16[8,72,128]{2,1,0:T(8,128)(2,1)S(1)} %all-to-all-done.got_ref), custom_call_target="tpu_custom_call" | custom-call | flops 589824 | bytes 294912 | tf_op jit(solution)/shard_map/add/pallas_call | solution.py:225
  37.7 4.1 %all-to-all-start.1 = ((s16[16,72,128]{2,1,0:T(8,128)(2,1)}), s16[16,72,128]{2,1,0:T(8,128)(2,1)S(1)}, u32[]{:S(2)}, u32[]{:S(2)}) async-start(s16[16,72,128]{2,1,0:T(8,128)(2,1)} %add.5), calls=%async_computation.1 | async-start | bytes 589824 | tf_op jit(solution)/shard_map/all_to_all | solution.py:367
  41.9 0.0 copy-start.1
  41.9 1.3 %pick.3 = (bf16[512,128]{1,0:T(8,128)(2,1)S(1)}, bf16[512,128]{1,0:T(8,128)(2,1)S(1)}, bf16[512,128]{1,0:T(8,128)(2,1)S(1)}, bf16[512,128]{1,0:T(8,128)(2,1)S(1)}, bf16[512,128]{1,0:T(8,128)(2,1)S(1)}) custom-call(bf16[8,512,128]{2,1,0:T(8,128)(2,1)} %bitcast.7), custom_call_target="tpu_custom_call" | custom-call | flops 5000000000 | bytes 655360 | tf_op jit(solution)/shard_map/pick/pallas_call | solution.py:99
  43.2 3.8 %collective-permute-start.5 = (bf16[512,128]{1,0:T(8,128)(2,1)S(1)}, bf16[512,128]{1,0:T(8,128)(2,1)S(1)}, u32[]{:S(2)}, u32[]{:S(2)}) collective-permute-start(bf16[512,128]{1,0:T(8,128)(2,1)S(1)} %get-tuple-element.19), channel_id=1, source_target_pairs={{0,6},{1,7},{2,4},{3,5},{4,2},{5,3},{6,0},{7,1},{8,14},{9,15},{10,... | collective-permute-start | bytes 393224 | tf_op jit(solution)/shard_map/ppermute | solution.py:347
  47.0 1.5 %collective-permute-start.6 = (bf16[512,128]{1,0:T(8,128)(2,1)S(1)}, bf16[512,128]{1,0:T(8,128)(2,1)S(1)}, u32[]{:S(2)}, u32[]{:S(2)}) collective-permute-start(bf16[512,128]{1,0:T(8,128)(2,1)S(1)} %get-tuple-element.20), channel_id=1, source_target_pairs={{0,1},{1,0},{2,3},{3,2},{4,5},{5,4},{6,7},{7,6},{8,9},{9,8},{10,11... | collective-permute-start | bytes 393224 | tf_op jit(solution)/shard_map/ppermute | solution.py:347
  48.4 0.0 collective-permute-start.7
  48.4 0.0 collective-permute-done.3.refs_0_
  48.4 2.0 %collective-permute-start.8 = (bf16[512,128]{1,0:T(8,128)(2,1)S(1)}, bf16[512,128]{1,0:T(8,128)(2,1)S(1)}, u32[]{:S(2)}, u32[]{:S(2)}) collective-permute-start(bf16[512,128]{1,0:T(8,128)(2,1)S(1)} %get-tuple-element.22), channel_id=1, source_target_pairs={{0,3},{1,2},{2,1},{3,0},{4,7},{5,6},{6,5},{7,4},{8,11},{9,10},{10,... | collective-permute-start | bytes 393224 | tf_op jit(solution)/shard_map/ppermute | solution.py:347
  50.5 0.0 collective-permute-done.4.refs_1_
  50.5 1.5 %collective-permute-start.9 = (bf16[512,128]{1,0:T(8,128)(2,1)S(1)}, bf16[512,128]{1,0:T(8,128)(2,1)S(1)}, u32[]{:S(2)}, u32[]{:S(2)}) collective-permute-start(bf16[512,128]{1,0:T(8,128)(2,1)S(1)} %get-tuple-element.23), channel_id=1, source_target_pairs={{0,7},{1,6},{2,5},{3,4},{4,3},{5,2},{6,1},{7,0},{8,15},{9,14},{10,... | collective-permute-start | bytes 393224 | tf_op jit(solution)/shard_map/ppermute | solution.py:347
  51.9 0.6 collective-permute-done.5.refs_2_
  52.5 2.1 %all-to-all-done.1.codes_ref = s16[16,72,128]{2,1,0:T(8,128)(2,1)S(1)} async-done(((s16[16,72,128]{2,1,0:T(8,128)(2,1)}), s16[16,72,128]{2,1,0:T(8,128)(2,1)S(1)}, u32[]{:S(2)}, u32[]{:S(2)}) %all-to-all-start.1) | async-done | bytes 294944 | tf_op jit(solution)/shard_map/all_to_all | solution.py:367
  54.6 0.0 collective-permute-start.2
  54.6 0.0 collective-permute-done.6.refs_3_
  54.6 0.0 collective-permute-done.7.refs_4_
  54.6 3.7 %collective-permute-done.8.refs_5_ = bf16[512,128]{1,0:T(8,128)(2,1)S(1)} collective-permute-done((bf16[512,128]{1,0:T(8,128)(2,1)S(1)}, bf16[512,128]{1,0:T(8,128)(2,1)S(1)}, u32[]{:S(2)}, u32[]{:S(2)}) %collective-permute-start.8) | collective-permute-done | bytes 131104 | tf_op jit(solution)/shard_map/ppermute | solution.py:347
  58.3 0.0 collective-permute-done.9.refs_6_
  58.3 0.0 copy-done.1
  58.3 4.0 %cold_sums.1 = f32[2048,128]{1,0:T(8,128)} custom-call(s16[8,72,128]{2,1,0:T(8,128)(2,1)S(1)} %all-to-all-done.got_ref, bf16[8,512,128]{2,1,0:T(8,128)(2,1)S(1)} %bitcast.8, bf16[512,128]{1,0:T(8,128)(2,1)S(1)} %collective-permute-done.3.refs_0_, bf16[512,128]{1,0:T(8,128)(2,1)S(1)} %collective-permute-done.4.refs_1_, ...), custom_call_target="tpu_custom_call" | custom-call | flops 2147483648 | bytes 1048576 | tf_op jit(solution)/shard_map/cold_sums/pallas_call | solution.py:310
  62.3 0.8 %unpack.2.refs_0_ = f32[2048,128]{1,0:T(8,128)} custom-call(s16[16,72,128]{2,1,0:T(8,128)(2,1)S(1)} %all-to-all-done.1.codes_ref), custom_call_target="tpu_custom_call" | custom-call | flops 524288 | bytes 786432 | tf_op jit(solution)/shard_map/unpack/pallas_call | solution.py:261
  63.2 0.0 collective-permute-done.2.codes_ref
  63.2 0.8 %unpack.3 = f32[2048,128]{1,0:T(8,128)} custom-call(s16[16,72,128]{2,1,0:T(8,128)(2,1)S(1)} %collective-permute-done.2.codes_ref, f32[2048,128]{1,0:T(8,128)} %unpack.2.refs_0_), custom_call_target="tpu_custom_call", output_to_operand_aliasing={{}: (1, {})} | custom-call | flops 524288 | bytes 786432 | tf_op jit(solution)/shard_map/unpack/pallas_call | solution.py:261
  (2 shorter events, 0.0 us)
Async XLA Ops:
  0.6 1.6 %copy-start = (bf16[8192,128]{1,0:T(8,128)(2,1)S(1)}, bf16[8192,128]{1,0:T(8,128)(2,1)}, u32[]{:S(2)}) copy-start(bf16[8192,128]{1,0:T(8,128)(2,1)} %data_ref.1) | copy-start | bytes 6291460
  2.2 0.8 %copy-start.2 = (s32[8192]{0:T(1024)S(1)}, s32[8192]{0:T(1024)}, u32[]{:S(2)}) copy-start(s32[8192]{0:T(1024)} %param.5) | copy-start | bytes 98308
  3.0 5.6 %copy-start.3 = (s32[1,1,8,512]{3,2,1,0:T(8,128)S(1)}, s32[1,1,8,512]{3,2,1,0:T(8,128)}, u32[]{:S(2)}) copy-start(s32[1,1,8,512]{3,2,1,0:T(8,128)} %param.8) | copy-start | bytes 49156
  3.0 10.1 %copy-start.4 = (s32[1,1,8]{2,1,0:T(1,128)S(1)}, s32[1,1,8]{2,1,0:T(1,128)}, u32[]{:S(2)}) copy-start(s32[1,1,8]{2,1,0:T(1,128)} %param.9) | copy-start | bytes 100
  8.0 2.1 %collective-permute-start = (f32[1024,128]{1,0:T(8,128)S(1)}, f32[1024,128]{1,0:T(8,128)S(1)}, u32[]{:S(2)}, u32[]{:S(2)}) collective-permute-start(f32[1024,128]{1,0:T(8,128)S(1)} %get-tuple-element.14), channel_id=1, source_target_pairs={{0,8},{8,0},{1,9},{9,1},{2,10},{10,2},{3,11},{11,3},{4,12},{12,4},... | collective-permute-start | bytes 1572872 | tf_op jit(solution)/shard_map/ppermute | solution.py:353
  10.2 7.1 %collective-permute-start.1 = (s16[8,72,128]{2,1,0:T(8,128)(2,1)S(1)}, s16[8,72,128]{2,1,0:T(8,128)(2,1)S(1)}, u32[]{:S(2)}, u32[]{:S(2)}) collective-permute-start(s16[8,72,128]{2,1,0:T(8,128)(2,1)S(1)} %get-tuple-element.16), channel_id=1, source_target_pairs={{0,16},{16,0},{1,17},{17,1},{2,18},{18,2},{3,19},{19,3},{4,20},{20... | collective-permute-start | bytes 442376 | tf_op jit(solution)/shard_map/ppermute | solution.py:360
  18.0 18.9 %all-to-all-start = ((s16[8,72,128]{2,1,0:T(8,128)(2,1)}), s16[8,72,128]{2,1,0:T(8,128)(2,1)S(1)}, u32[]{:S(2)}, u32[]{:S(2)}) async-start(s16[8,72,128]{2,1,0:T(8,128)(2,1)} %join.1), calls=%async_computation | async-start | bytes 294912 | tf_op jit(solution)/shard_map/all_to_all | solution.py:364
  25.1 23.3 %collective-permute-start.3 = (bf16[512,128]{1,0:T(8,128)(2,1)S(1)}, bf16[512,128]{1,0:T(8,128)(2,1)S(1)}, u32[]{:S(2)}, u32[]{:S(2)}) collective-permute-start(bf16[512,128]{1,0:T(8,128)(2,1)S(1)} %get-tuple-element.17), channel_id=1, source_target_pairs={{0,4},{1,5},{2,6},{3,7},{4,0},{5,1},{6,2},{7,3},{8,12},{9,13},{10,... | collective-permute-start | bytes 393224 | tf_op jit(solution)/shard_map/ppermute | solution.py:347
  28.1 22.4 %collective-permute-start.4 = (bf16[512,128]{1,0:T(8,128)(2,1)S(1)}, bf16[512,128]{1,0:T(8,128)(2,1)S(1)}, u32[]{:S(2)}, u32[]{:S(2)}) collective-permute-start(bf16[512,128]{1,0:T(8,128)(2,1)S(1)} %get-tuple-element.18), channel_id=1, source_target_pairs={{0,5},{1,4},{2,7},{3,6},{4,1},{5,0},{6,3},{7,2},{8,13},{9,12},{10,... | collective-permute-start | bytes 393224 | tf_op jit(solution)/shard_map/ppermute | solution.py:347
  37.7 16.9 %all-to-all-start.1 = ((s16[16,72,128]{2,1,0:T(8,128)(2,1)}), s16[16,72,128]{2,1,0:T(8,128)(2,1)S(1)}, u32[]{:S(2)}, u32[]{:S(2)}) async-start(s16[16,72,128]{2,1,0:T(8,128)(2,1)} %add.5), calls=%async_computation.1 | async-start | bytes 589824 | tf_op jit(solution)/shard_map/all_to_all | solution.py:367
  41.9 16.4 %copy-start.1 = (bf16[1,1,8,512,128]{4,3,2,1,0:T(8,128)(2,1)S(1)}, bf16[1,1,8,512,128]{4,3,2,1,0:T(8,128)(2,1)}, u32[]{:S(2)}) copy-start(bf16[1,1,8,512,128]{4,3,2,1,0:T(8,128)(2,1)} %param.7) | copy-start | bytes 3145732
  43.2 9.3 %collective-permute-start.5 = (bf16[512,128]{1,0:T(8,128)(2,1)S(1)}, bf16[512,128]{1,0:T(8,128)(2,1)S(1)}, u32[]{:S(2)}, u32[]{:S(2)}) collective-permute-start(bf16[512,128]{1,0:T(8,128)(2,1)S(1)} %get-tuple-element.19), channel_id=1, source_target_pairs={{0,6},{1,7},{2,4},{3,5},{4,2},{5,3},{6,0},{7,1},{8,14},{9,15},{10,... | collective-permute-start | bytes 393224 | tf_op jit(solution)/shard_map/ppermute | solution.py:347
  47.0 7.6 %collective-permute-start.6 = (bf16[512,128]{1,0:T(8,128)(2,1)S(1)}, bf16[512,128]{1,0:T(8,128)(2,1)S(1)}, u32[]{:S(2)}, u32[]{:S(2)}) collective-permute-start(bf16[512,128]{1,0:T(8,128)(2,1)S(1)} %get-tuple-element.20), channel_id=1, source_target_pairs={{0,1},{1,0},{2,3},{3,2},{4,5},{5,4},{6,7},{7,6},{8,9},{9,8},{10,11... | collective-permute-start | bytes 393224 | tf_op jit(solution)/shard_map/ppermute | solution.py:347
  48.4 6.2 %collective-permute-start.7 = (bf16[512,128]{1,0:T(8,128)(2,1)S(1)}, bf16[512,128]{1,0:T(8,128)(2,1)S(1)}, u32[]{:S(2)}, u32[]{:S(2)}) collective-permute-start(bf16[512,128]{1,0:T(8,128)(2,1)S(1)} %get-tuple-element.21), channel_id=1, source_target_pairs={{0,2},{1,3},{2,0},{3,1},{4,6},{5,7},{6,4},{7,5},{8,10},{9,11},{10,... | collective-permute-start | bytes 393224 | tf_op jit(solution)/shard_map/ppermute | solution.py:347
  48.4 9.8 %collective-permute-start.8 = (bf16[512,128]{1,0:T(8,128)(2,1)S(1)}, bf16[512,128]{1,0:T(8,128)(2,1)S(1)}, u32[]{:S(2)}, u32[]{:S(2)}) collective-permute-start(bf16[512,128]{1,0:T(8,128)(2,1)S(1)} %get-tuple-element.22), channel_id=1, source_target_pairs={{0,3},{1,2},{2,1},{3,0},{4,7},{5,6},{6,5},{7,4},{8,11},{9,10},{10,... | collective-permute-start | bytes 393224 | tf_op jit(solution)/shard_map/ppermute | solution.py:347
  50.5 7.8 %collective-permute-start.9 = (bf16[512,128]{1,0:T(8,128)(2,1)S(1)}, bf16[512,128]{1,0:T(8,128)(2,1)S(1)}, u32[]{:S(2)}, u32[]{:S(2)}) collective-permute-start(bf16[512,128]{1,0:T(8,128)(2,1)S(1)} %get-tuple-element.23), channel_id=1, source_target_pairs={{0,7},{1,6},{2,5},{3,4},{4,3},{5,2},{6,1},{7,0},{8,15},{9,14},{10,... | collective-permute-start | bytes 393224 | tf_op jit(solution)/shard_map/ppermute | solution.py:347
  54.6 8.6 %collective-permute-start.2 = (s16[16,72,128]{2,1,0:T(8,128)(2,1)S(1)}, s16[16,72,128]{2,1,0:T(8,128)(2,1)S(1)}, u32[]{:S(2)}, u32[]{:S(2)}) collective-permute-start(s16[16,72,128]{2,1,0:T(8,128)(2,1)S(1)} %all-to-all-done.1.codes_ref), channel_id=1, source_target_pairs={{0,8},{8,0},{1,9},{9,1},{2,10},{10,2},{3,11},{11,3},{4,12},{12,4},... | collective-permute-start | bytes 884744 | tf_op jit(solution)/shard_map/ppermute | solution.py:369

commit v7 on v6

--- a/solution.py
+++ b/solution.py
@@ -67,7 +67,7 @@
 def hot_sums(ids, data, table):
     lookups, width = data.shape
     half = table // 2
-    step = math.gcd(lookups, 4096)
+    step = math.gcd(lookups, 8192)
     whole = pl.BlockSpec(memory_space=pltpu.VMEM)
     return pl.pallas_call(
         functools.partial(hot_kernel, block=math.gcd(half, 256), step=step),
@@ -280,7 +280,8 @@
 def cold_lots(owners):
     far, near = list(range(owners // 2, owners)), list(range(1, owners // 2))
     a, b, c = len(far) // 4, len(far) // 2, len(far) * 3 // 4
-    return far[:a], far[a:b], far[b:c], near + far[c:]
+    k = len(near) // 3
+    return far[:a], far[a:b], far[b:c] + near[:k], near[k:] + far[c:]
 
 
 def cold_kernel(got_ref, own_ref, *refs, block, at, lines, steps):

time: 64.5 us -> 64.4 us (level)
  no operation moved by 1% of the time
where the time goes in v7:
time: 64.4 us; the launch traced here: 64 us
  starting transfers between devices  26.9 us (42%)
  waiting for transfers between devices  19.3 us (30%)
  Pallas kernels  14.6 us (23%)
  local copies, waits for them, and re-layouts  2.37 us (4%)
  between operations  0.72 us (1%)
    ppermute x7, starting transfers between devices, move(): moved.append((n, lax.ppermute(picked[n], 'gy', pairs)))  13.2 us
    all_to_all x1, waiting for transfers between devices, per_device(): lax.all_to_all(joined, 'gy', split_axis=0, concat_axis=0, tiled=True)  7.36 us
    all_to_all x1, starting transfers between devices, per_device(): lax.all_to_all(joined, 'gy', split_axis=0, concat_axis=0, tiled=True)  6.08 us
    pallas_call x1, Pallas kernels, hot_sums(): pl.pallas_call(functools.partial(hot_kernel, block=math.gcd(half, 256), s...  4.95 us
    ppermute x7, waiting for transfers between devices, move(): moved.append((n, lax.ppermute(picked[n], 'gy', pairs)))  4.27 us
    all_to_all x1, starting transfers between devices, per_device(): lax.all_to_all(summed, everyone, split_axis=0, concat_axis=0, tiled=True)  4.15 us
    ppermute x1, waiting for transfers between devices, per_device(): lax.ppermute(block, 'chip', [(i, partner(i, n, groups)[1]) for i in range...  4.07 us
    pallas_call x1, Pallas kernels, cold_sums(): pl.pallas_call(functools.partial(cold_kernel, block=math.gcd(table // 2,...  4.03 us
  transfers between devices with their start and end apart: 12, of which 6 were waited for; matrix products, arithmetic and copies ran while one was open for 0% of the time, Pallas kernels for 12%

profile of v7, /device:TPU:0, one launch (start us, length us, event | category | flops | bytes accessed | tf_op | source)
XLA Modules:
  0.0 64.0 jit_solution(16277174804795853589)
XLA Ops:
  0.6 0.0 copy-start
  0.6 1.6 %copy-done = bf16[8192,128]{1,0:T(8,128)(2,1)S(1)} copy-done((bf16[8192,128]{1,0:T(8,128)(2,1)S(1)}, bf16[8192,128]{1,0:T(8,128)(2,1)}, u32[]{:S(2)}) %copy-start) | copy-done | bytes 2097176
  2.2 0.0 copy-start.2
  2.2 0.8 %copy-done.2 = s32[8192]{0:T(1024)S(1)} copy-done((s32[8192]{0:T(1024)S(1)}, s32[8192]{0:T(1024)}, u32[]{:S(2)}) %copy-start.2) | copy-done | bytes 32792
  3.0 0.0 copy-start.3
  3.0 0.0 copy-start.4
  3.0 5.0 %hot_sums.1 = (f32[1024,128]{1,0:T(8,128)S(1)}, f32[1024,128]{1,0:T(8,128)S(1)}) custom-call(s32[64,128]{1,0:T(8,128)S(1)} %bitcast.9, bf16[8192,128]{1,0:T(8,128)(2,1)S(1)} %copy-done), custom_call_target="tpu_custom_call" | custom-call | flops 4294967296 | bytes 2097152 | tf_op jit(solution)/shard_map/hot_sums/pallas_call | solution.py:72
  7.9 0.6 collective-permute-start
  8.5 0.0 copy-done.3
  8.5 1.5 %collective-permute-done.got_ref = f32[1024,128]{1,0:T(8,128)S(1)} collective-permute-done((f32[1024,128]{1,0:T(8,128)S(1)}, f32[1024,128]{1,0:T(8,128)S(1)}, u32[]{:S(2)}, u32[]{:S(2)}) %collective-permute-start) | collective-permute-done | bytes 524320 | tf_op jit(solution)/shard_map/ppermute | solution.py:354
  10.0 0.1 pack.1
  10.1 2.9 %collective-permute-start.1 = (s16[8,72,128]{2,1,0:T(8,128)(2,1)S(1)}, s16[8,72,128]{2,1,0:T(8,128)(2,1)S(1)}, u32[]{:S(2)}, u32[]{:S(2)}) collective-permute-start(s16[8,72,128]{2,1,0:T(8,128)(2,1)S(1)} %get-tuple-element.16), channel_id=1, source_target_pairs={{0,16},{16,0},{1,17},{17,1},{2,18},{18,2},{3,19},{19,3},{4,20},{20... | collective-permute-start | bytes 442376 | tf_op jit(solution)/shard_map/ppermute | solution.py:361
  13.1 0.0 copy-done.4
  13.1 0.1 compare_select_fusion.slots_ref
  13.1 4.1 %collective-permute-done.1.refs_0_ = s16[8,72,128]{2,1,0:T(8,128)(2,1)S(1)} collective-permute-done((s16[8,72,128]{2,1,0:T(8,128)(2,1)S(1)}, s16[8,72,128]{2,1,0:T(8,128)(2,1)S(1)}, u32[]{:S(2)}, u32[]{:S(2)}) %collective-permute-start.1) | collective-permute-done | bytes 147488 | tf_op jit(solution)/shard_map/ppermute | solution.py:361
  17.2 0.8 %join.1 = s16[8,72,128]{2,1,0:T(8,128)(2,1)} custom-call(f32[512,128]{1,0:T(8,128)S(1)} %get-tuple-element.15.own_ref, s32[8,4,128]{2,1,0:T(4,128)S(1)} %compare_select_fusion.slots_ref, s16[8,72,128]{2,1,0:T(8,128)(2,1)S(1)} %collective-permute-done.1.refs_0_), custom_call_target="tpu_custom_call" | custom-call | flops 524288 | bytes 655360 | tf_op jit(solution)/shard_map/join/pallas_call | solution.py:197
  18.0 6.1 %all-to-all-start = ((s16[8,72,128]{2,1,0:T(8,128)(2,1)}), s16[8,72,128]{2,1,0:T(8,128)(2,1)S(1)}, u32[]{:S(2)}, u32[]{:S(2)}) async-start(s16[8,72,128]{2,1,0:T(8,128)(2,1)} %join.1), calls=%async_computation | async-start | bytes 294912 | tf_op jit(solution)/shard_map/all_to_all | solution.py:365
  24.1 1.0 %pick.2 = (bf16[512,128]{1,0:T(8,128)(2,1)S(1)}, bf16[512,128]{1,0:T(8,128)(2,1)S(1)}) custom-call(bf16[8,512,128]{2,1,0:T(8,128)(2,1)} %bitcast.6), custom_call_target="tpu_custom_call" | custom-call | flops 5000000000 | bytes 262144 | tf_op jit(solution)/shard_map/pick/pallas_call | solution.py:99
  25.1 3.0 %collective-permute-start.3 = (bf16[512,128]{1,0:T(8,128)(2,1)S(1)}, bf16[512,128]{1,0:T(8,128)(2,1)S(1)}, u32[]{:S(2)}, u32[]{:S(2)}) collective-permute-start(bf16[512,128]{1,0:T(8,128)(2,1)S(1)} %get-tuple-element.17), channel_id=1, source_target_pairs={{0,4},{1,5},{2,6},{3,7},{4,0},{5,1},{6,2},{7,3},{8,12},{9,13},{10,... | collective-permute-start | bytes 393224 | tf_op jit(solution)/shard_map/ppermute | solution.py:348
  28.0 1.5 %collective-permute-start.4 = (bf16[512,128]{1,0:T(8,128)(2,1)S(1)}, bf16[512,128]{1,0:T(8,128)(2,1)S(1)}, u32[]{:S(2)}, u32[]{:S(2)}) collective-permute-start(bf16[512,128]{1,0:T(8,128)(2,1)S(1)} %get-tuple-element.18), channel_id=1, source_target_pairs={{0,5},{1,4},{2,7},{3,6},{4,1},{5,0},{6,3},{7,2},{8,13},{9,12},{10,... | collective-permute-start | bytes 393224 | tf_op jit(solution)/shard_map/ppermute | solution.py:348
  29.5 7.4 %all-to-all-done.got_ref = s16[8,72,128]{2,1,0:T(8,128)(2,1)S(1)} async-done(((s16[8,72,128]{2,1,0:T(8,128)(2,1)}), s16[8,72,128]{2,1,0:T(8,128)(2,1)S(1)}, u32[]{:S(2)}, u32[]{:S(2)}) %all-to-all-start) | async-done | bytes 147488 | tf_op jit(solution)/shard_map/all_to_all | solution.py:365
  36.9 0.8 %add.5 = s16[16,72,128]{2,1,0:T(8,128)(2,1)} custom-call(s16[8,72,128]{2,1,0:T(8,128)(2,1)S(1)} %all-to-all-done.got_ref), custom_call_target="tpu_custom_call" | custom-call | flops 589824 | bytes 294912 | tf_op jit(solution)/shard_map/add/pallas_call | solution.py:225
  37.7 4.1 %all-to-all-start.1 = ((s16[16,72,128]{2,1,0:T(8,128)(2,1)}), s16[16,72,128]{2,1,0:T(8,128)(2,1)S(1)}, u32[]{:S(2)}, u32[]{:S(2)}) async-start(s16[16,72,128]{2,1,0:T(8,128)(2,1)} %add.5), calls=%async_computation.1 | async-start | bytes 589824 | tf_op jit(solution)/shard_map/all_to_all | solution.py:368
  41.8 0.0 copy-start.1
  41.9 1.3 %pick.3 = (bf16[512,128]{1,0:T(8,128)(2,1)S(1)}, bf16[512,128]{1,0:T(8,128)(2,1)S(1)}, bf16[512,128]{1,0:T(8,128)(2,1)S(1)}, bf16[512,128]{1,0:T(8,128)(2,1)S(1)}, bf16[512,128]{1,0:T(8,128)(2,1)S(1)}) custom-call(bf16[8,512,128]{2,1,0:T(8,128)(2,1)} %bitcast.7), custom_call_target="tpu_custom_call" | custom-call | flops 5000000000 | bytes 655360 | tf_op jit(solution)/shard_map/pick/pallas_call | solution.py:99
  43.2 3.8 %collective-permute-start.5 = (bf16[512,128]{1,0:T(8,128)(2,1)S(1)}, bf16[512,128]{1,0:T(8,128)(2,1)S(1)}, u32[]{:S(2)}, u32[]{:S(2)}) collective-permute-start(bf16[512,128]{1,0:T(8,128)(2,1)S(1)} %get-tuple-element.19), channel_id=1, source_target_pairs={{0,6},{1,7},{2,4},{3,5},{4,2},{5,3},{6,0},{7,1},{8,14},{9,15},{10,... | collective-permute-start | bytes 393224 | tf_op jit(solution)/shard_map/ppermute | solution.py:348
  46.9 1.5 %collective-permute-start.6 = (bf16[512,128]{1,0:T(8,128)(2,1)S(1)}, bf16[512,128]{1,0:T(8,128)(2,1)S(1)}, u32[]{:S(2)}, u32[]{:S(2)}) collective-permute-start(bf16[512,128]{1,0:T(8,128)(2,1)S(1)} %get-tuple-element.20), channel_id=1, source_target_pairs={{0,1},{1,0},{2,3},{3,2},{4,5},{5,4},{6,7},{7,6},{8,9},{9,8},{10,11... | collective-permute-start | bytes 393224 | tf_op jit(solution)/shard_map/ppermute | solution.py:348
  48.4 0.0 collective-permute-start.7
  48.4 0.0 collective-permute-done.3.refs_0_
  48.4 2.0 %collective-permute-start.8 = (bf16[512,128]{1,0:T(8,128)(2,1)S(1)}, bf16[512,128]{1,0:T(8,128)(2,1)S(1)}, u32[]{:S(2)}, u32[]{:S(2)}) collective-permute-start(bf16[512,128]{1,0:T(8,128)(2,1)S(1)} %get-tuple-element.22), channel_id=1, source_target_pairs={{0,3},{1,2},{2,1},{3,0},{4,7},{5,6},{6,5},{7,4},{8,11},{9,10},{10,... | collective-permute-start | bytes 393224 | tf_op jit(solution)/shard_map/ppermute | solution.py:348
  50.4 0.0 collective-permute-done.4.refs_1_
  50.4 1.5 %collective-permute-start.9 = (bf16[512,128]{1,0:T(8,128)(2,1)S(1)}, bf16[512,128]{1,0:T(8,128)(2,1)S(1)}, u32[]{:S(2)}, u32[]{:S(2)}) collective-permute-start(bf16[512,128]{1,0:T(8,128)(2,1)S(1)} %get-tuple-element.23), channel_id=1, source_target_pairs={{0,7},{1,6},{2,5},{3,4},{4,3},{5,2},{6,1},{7,0},{8,15},{9,14},{10,... | collective-permute-start | bytes 393224 | tf_op jit(solution)/shard_map/ppermute | solution.py:348
  51.9 0.6 collective-permute-done.5.refs_2_
  52.5 2.1 %all-to-all-done.1.codes_ref = s16[16,72,128]{2,1,0:T(8,128)(2,1)S(1)} async-done(((s16[16,72,128]{2,1,0:T(8,128)(2,1)}), s16[16,72,128]{2,1,0:T(8,128)(2,1)S(1)}, u32[]{:S(2)}, u32[]{:S(2)}) %all-to-all-start.1) | async-done | bytes 294944 | tf_op jit(solution)/shard_map/all_to_all | solution.py:368
  54.6 0.0 collective-permute-start.2
  54.6 0.0 collective-permute-done.6.refs_3_
  54.6 0.0 collective-permute-done.7.refs_4_
  54.6 3.7 %collective-permute-done.8.refs_5_ = bf16[512,128]{1,0:T(8,128)(2,1)S(1)} collective-permute-done((bf16[512,128]{1,0:T(8,128)(2,1)S(1)}, bf16[512,128]{1,0:T(8,128)(2,1)S(1)}, u32[]{:S(2)}, u32[]{:S(2)}) %collective-permute-start.8) | collective-permute-done | bytes 131104 | tf_op jit(solution)/shard_map/ppermute | solution.py:348
  58.3 0.0 collective-permute-done.9.refs_6_
  58.3 0.0 copy-done.1
  58.3 4.0 %cold_sums.1 = f32[2048,128]{1,0:T(8,128)} custom-call(s16[8,72,128]{2,1,0:T(8,128)(2,1)S(1)} %all-to-all-done.got_ref, bf16[8,512,128]{2,1,0:T(8,128)(2,1)S(1)} %bitcast.8, bf16[512,128]{1,0:T(8,128)(2,1)S(1)} %collective-permute-done.3.refs_0_, bf16[512,128]{1,0:T(8,128)(2,1)S(1)} %collective-permute-done.4.refs_1_, ...), custom_call_target="tpu_custom_call" | custom-call | flops 2147483648 | bytes 1048576 | tf_op jit(solution)/shard_map/cold_sums/pallas_call | solution.py:311
  62.3 0.8 %unpack.2.refs_0_ = f32[2048,128]{1,0:T(8,128)} custom-call(s16[16,72,128]{2,1,0:T(8,128)(2,1)S(1)} %all-to-all-done.1.codes_ref), custom_call_target="tpu_custom_call" | custom-call | flops 524288 | bytes 786432 | tf_op jit(solution)/shard_map/unpack/pallas_call | solution.py:261
  63.1 0.0 collective-permute-done.2.codes_ref
  63.1 0.8 %unpack.3 = f32[2048,128]{1,0:T(8,128)} custom-call(s16[16,72,128]{2,1,0:T(8,128)(2,1)S(1)} %collective-permute-done.2.codes_ref, f32[2048,128]{1,0:T(8,128)} %unpack.2.refs_0_), custom_call_target="tpu_custom_call", output_to_operand_aliasing={{}: (1, {})} | custom-call | flops 524288 | bytes 786432 | tf_op jit(solution)/shard_map/unpack/pallas_call | solution.py:261
  (2 shorter events, 0.0 us)
Async XLA Ops:
  0.6 1.6 %copy-start = (bf16[8192,128]{1,0:T(8,128)(2,1)S(1)}, bf16[8192,128]{1,0:T(8,128)(2,1)}, u32[]{:S(2)}) copy-start(bf16[8192,128]{1,0:T(8,128)(2,1)} %data_ref.1) | copy-start | bytes 6291460
  2.2 0.8 %copy-start.2 = (s32[8192]{0:T(1024)S(1)}, s32[8192]{0:T(1024)}, u32[]{:S(2)}) copy-start(s32[8192]{0:T(1024)} %param.5) | copy-start | bytes 98308
  3.0 5.5 %copy-start.3 = (s32[1,1,8,512]{3,2,1,0:T(8,128)S(1)}, s32[1,1,8,512]{3,2,1,0:T(8,128)}, u32[]{:S(2)}) copy-start(s32[1,1,8,512]{3,2,1,0:T(8,128)} %param.8) | copy-start | bytes 49156
  3.0 10.1 %copy-start.4 = (s32[1,1,8]{2,1,0:T(1,128)S(1)}, s32[1,1,8]{2,1,0:T(1,128)}, u32[]{:S(2)}) copy-start(s32[1,1,8]{2,1,0:T(1,128)} %param.9) | copy-start | bytes 100
  7.9 2.1 %collective-permute-start = (f32[1024,128]{1,0:T(8,128)S(1)}, f32[1024,128]{1,0:T(8,128)S(1)}, u32[]{:S(2)}, u32[]{:S(2)}) collective-permute-start(f32[1024,128]{1,0:T(8,128)S(1)} %get-tuple-element.14), channel_id=1, source_target_pairs={{0,8},{8,0},{1,9},{9,1},{2,10},{10,2},{3,11},{11,3},{4,12},{12,4},... | collective-permute-start | bytes 1572872 | tf_op jit(solution)/shard_map/ppermute | solution.py:354
  10.1 7.1 %collective-permute-start.1 = (s16[8,72,128]{2,1,0:T(8,128)(2,1)S(1)}, s16[8,72,128]{2,1,0:T(8,128)(2,1)S(1)}, u32[]{:S(2)}, u32[]{:S(2)}) collective-permute-start(s16[8,72,128]{2,1,0:T(8,128)(2,1)S(1)} %get-tuple-element.16), channel_id=1, source_target_pairs={{0,16},{16,0},{1,17},{17,1},{2,18},{18,2},{3,19},{19,3},{4,20},{20... | collective-permute-start | bytes 442376 | tf_op jit(solution)/shard_map/ppermute | solution.py:361
  18.0 18.9 %all-to-all-start = ((s16[8,72,128]{2,1,0:T(8,128)(2,1)}), s16[8,72,128]{2,1,0:T(8,128)(2,1)S(1)}, u32[]{:S(2)}, u32[]{:S(2)}) async-start(s16[8,72,128]{2,1,0:T(8,128)(2,1)} %join.1), calls=%async_computation | async-start | bytes 294912 | tf_op jit(solution)/shard_map/all_to_all | solution.py:365
  25.1 23.4 %collective-permute-start.3 = (bf16[512,128]{1,0:T(8,128)(2,1)S(1)}, bf16[512,128]{1,0:T(8,128)(2,1)S(1)}, u32[]{:S(2)}, u32[]{:S(2)}) collective-permute-start(bf16[512,128]{1,0:T(8,128)(2,1)S(1)} %get-tuple-element.17), channel_id=1, source_target_pairs={{0,4},{1,5},{2,6},{3,7},{4,0},{5,1},{6,2},{7,3},{8,12},{9,13},{10,... | collective-permute-start | bytes 393224 | tf_op jit(solution)/shard_map/ppermute | solution.py:348
  28.0 22.4 %collective-permute-start.4 = (bf16[512,128]{1,0:T(8,128)(2,1)S(1)}, bf16[512,128]{1,0:T(8,128)(2,1)S(1)}, u32[]{:S(2)}, u32[]{:S(2)}) collective-permute-start(bf16[512,128]{1,0:T(8,128)(2,1)S(1)} %get-tuple-element.18), channel_id=1, source_target_pairs={{0,5},{1,4},{2,7},{3,6},{4,1},{5,0},{6,3},{7,2},{8,13},{9,12},{10,... | collective-permute-start | bytes 393224 | tf_op jit(solution)/shard_map/ppermute | solution.py:348
  37.7 16.9 %all-to-all-start.1 = ((s16[16,72,128]{2,1,0:T(8,128)(2,1)}), s16[16,72,128]{2,1,0:T(8,128)(2,1)S(1)}, u32[]{:S(2)}, u32[]{:S(2)}) async-start(s16[16,72,128]{2,1,0:T(8,128)(2,1)} %add.5), calls=%async_computation.1 | async-start | bytes 589824 | tf_op jit(solution)/shard_map/all_to_all | solution.py:368
  41.8 16.4 %copy-start.1 = (bf16[1,1,8,512,128]{4,3,2,1,0:T(8,128)(2,1)S(1)}, bf16[1,1,8,512,128]{4,3,2,1,0:T(8,128)(2,1)}, u32[]{:S(2)}) copy-start(bf16[1,1,8,512,128]{4,3,2,1,0:T(8,128)(2,1)} %param.7) | copy-start | bytes 3145732
  43.2 9.3 %collective-permute-start.5 = (bf16[512,128]{1,0:T(8,128)(2,1)S(1)}, bf16[512,128]{1,0:T(8,128)(2,1)S(1)}, u32[]{:S(2)}, u32[]{:S(2)}) collective-permute-start(bf16[512,128]{1,0:T(8,128)(2,1)S(1)} %get-tuple-element.19), channel_id=1, source_target_pairs={{0,6},{1,7},{2,4},{3,5},{4,2},{5,3},{6,0},{7,1},{8,14},{9,15},{10,... | collective-permute-start | bytes 393224 | tf_op jit(solution)/shard_map/ppermute | solution.py:348
  46.9 7.6 %collective-permute-start.6 = (bf16[512,128]{1,0:T(8,128)(2,1)S(1)}, bf16[512,128]{1,0:T(8,128)(2,1)S(1)}, u32[]{:S(2)}, u32[]{:S(2)}) collective-permute-start(bf16[512,128]{1,0:T(8,128)(2,1)S(1)} %get-tuple-element.20), channel_id=1, source_target_pairs={{0,1},{1,0},{2,3},{3,2},{4,5},{5,4},{6,7},{7,6},{8,9},{9,8},{10,11... | collective-permute-start | bytes 393224 | tf_op jit(solution)/shard_map/ppermute | solution.py:348
  48.4 6.2 %collective-permute-start.7 = (bf16[512,128]{1,0:T(8,128)(2,1)S(1)}, bf16[512,128]{1,0:T(8,128)(2,1)S(1)}, u32[]{:S(2)}, u32[]{:S(2)}) collective-permute-start(bf16[512,128]{1,0:T(8,128)(2,1)S(1)} %get-tuple-element.21), channel_id=1, source_target_pairs={{0,2},{1,3},{2,0},{3,1},{4,6},{5,7},{6,4},{7,5},{8,10},{9,11},{10,... | collective-permute-start | bytes 393224 | tf_op jit(solution)/shard_map/ppermute | solution.py:348
  48.4 9.8 %collective-permute-start.8 = (bf16[512,128]{1,0:T(8,128)(2,1)S(1)}, bf16[512,128]{1,0:T(8,128)(2,1)S(1)}, u32[]{:S(2)}, u32[]{:S(2)}) collective-permute-start(bf16[512,128]{1,0:T(8,128)(2,1)S(1)} %get-tuple-element.22), channel_id=1, source_target_pairs={{0,3},{1,2},{2,1},{3,0},{4,7},{5,6},{6,5},{7,4},{8,11},{9,10},{10,... | collective-permute-start | bytes 393224 | tf_op jit(solution)/shard_map/ppermute | solution.py:348
  50.4 7.8 %collective-permute-start.9 = (bf16[512,128]{1,0:T(8,128)(2,1)S(1)}, bf16[512,128]{1,0:T(8,128)(2,1)S(1)}, u32[]{:S(2)}, u32[]{:S(2)}) collective-permute-start(bf16[512,128]{1,0:T(8,128)(2,1)S(1)} %get-tuple-element.23), channel_id=1, source_target_pairs={{0,7},{1,6},{2,5},{3,4},{4,3},{5,2},{6,1},{7,0},{8,15},{9,14},{10,... | collective-permute-start | bytes 393224 | tf_op jit(solution)/shard_map/ppermute | solution.py:348
  54.6 8.6 %collective-permute-start.2 = (s16[16,72,128]{2,1,0:T(8,128)(2,1)S(1)}, s16[16,72,128]{2,1,0:T(8,128)(2,1)S(1)}, u32[]{:S(2)}, u32[]{:S(2)}) collective-permute-start(s16[16,72,128]{2,1,0:T(8,128)(2,1)S(1)} %all-to-all-done.1.codes_ref), channel_id=1, source_target_pairs={{0,8},{8,0},{1,9},{9,1},{2,10},{10,2},{3,11},{11,3},{4,12},{12,4},... | collective-permute-start | bytes 884744 | tf_op jit(solution)/shard_map/ppermute | solution.py:370
